TPU v7x, 64 devices: a 2x2x8 block of a 4x4x8 slice. The times are simulated.
64 devices in a mesh: dp: 4 (over x, y), cp: 16 (over z, core).
Axes of the slice: x: 2, y: 2, z: 8, core: 2. Of those that a mesh axis runs over, the one named last changes fastest.
The devices are a block of a 4x4x8 slice.
Arguments:
- x_act: bfloat16 [4, 2048, 2048], P('dp', 'cp'), parts along dimension 0
- d_out: bfloat16 [4, 2048, 2048], P('dp', 'cp'), parts along dimension 0
- positions: int32 [4, 2048], P('dp', 'cp'), parts along dimension 0
- ln_gain: float32 [2048], replicated
- ln_bias: float32 [2048], replicated
- w_query: bfloat16 [2048, 32, 64], replicated
- w_key: bfloat16 [2048, 8, 64], replicated
- w_value: bfloat16 [2048, 8, 64], replicated
- w_out: bfloat16 [2048, 2048], replicated
Outputs:
- output 1: bfloat16 [4, 2048, 2048], P('dp', 'cp'), parts along dimension 0
- output 2: bfloat16 [4, 2048, 2048], P('dp', 'cp'), parts along dimension 0
- output 3: float32 [8192, 32, 64], P(('dp', 'cp')), parts along dimension 0
- output 4: float32 [8192, 8, 64], P(('dp', 'cp')), parts along dimension 0
- output 5: float32 [8192, 8, 64], P(('dp', 'cp')), parts along dimension 0
- output 6: float32 [8192, 2048], P(('dp', 'cp')), parts along dimension 0
- output 7: float32 [8192], P('dp'), parts along dimension 0
- output 8: float32 [8192], P('dp'), parts along dimension 0
There are 4 independent parts. A program takes and returns all parts, laid end to end along the dimension named above; an argument that names none is the same for every part.
All inputs are finite; a program needn't handle non-finite values.
Results may differ from a plain program's by a relative error of at most 0.00648291.
Values are sent between devices in bfloat16 or wider.
A program may use at most 768 MiB of HBM per device.

v0:
```python
import math
import jax
import jax.numpy as jnp
from jax import lax
from jax.sharding import PartitionSpec as P

EPS = 1e-5
ROPE_BASE = 10000.0
Q_TILE = 128


def norm_forward(x_act, ln_gain, ln_bias):
    x_f32 = x_act.astype(jnp.float32)
    centered = x_f32 - jnp.mean(x_f32, axis=-1, keepdims=True)
    inv_std = lax.rsqrt(jnp.mean(centered * centered, axis=-1, keepdims=True) + EPS)
    x_hat = centered * inv_std
    return (x_hat * (1.0 + ln_gain) + ln_bias).astype(jnp.bfloat16), x_hat, inv_std


def norm_backward(grad_h, x_hat, inv_std, ln_gain):
    grad_hat = grad_h * (1.0 + ln_gain)
    mean_one = jnp.mean(grad_hat, axis=-1, keepdims=True)
    mean_two = jnp.mean(grad_hat * x_hat, axis=-1, keepdims=True)
    return inv_std * (grad_hat - mean_one - x_hat * mean_two)


def rope_tables(positions, head_dim):
    quarter = head_dim // 4
    freq_tab = jnp.exp(jnp.arange(quarter, dtype=jnp.float32) * (-2.0 * math.log(ROPE_BASE) / (head_dim // 2)))
    angles = positions.astype(jnp.float32)[..., None] * freq_tab
    return jnp.cos(angles)[..., None, :], jnp.sin(angles)[..., None, :]


def rope_rotate(values, cos_tab, sin_tab):
    quarter = cos_tab.shape[-1]
    first_half = values[..., :quarter]
    second_half = values[..., quarter:2 * quarter]
    return jnp.concatenate([first_half * cos_tab - second_half * sin_tab, second_half * cos_tab + first_half * sin_tab, values[..., 2 * quarter:]], axis=-1)


def tile_probs(q_tile, key_all, q_first):
    head_dim = q_tile.shape[-1]
    scores = jnp.einsum('bqkgd,blkd->bkgql', q_tile, key_all, preferred_element_type=jnp.float32) * (head_dim ** -0.5)
    q_index = q_first + jnp.arange(q_tile.shape[1])
    k_index = jnp.arange(key_all.shape[1])
    scores = jnp.where(k_index[None, :] <= q_index[:, None], scores, -1e30)
    shifted = jnp.exp(scores - jnp.max(scores, axis=-1, keepdims=True))
    return shifted / jnp.sum(shifted, axis=-1, keepdims=True)


def attention_forward(q_grouped, key_all, value_all, q_base):
    n_batch, seq_len = q_grouped.shape[0], q_grouped.shape[1]

    def one_tile(tile_idx):
        q_first = tile_idx * Q_TILE
        q_tile = lax.dynamic_slice_in_dim(q_grouped, q_first, Q_TILE, axis=1)
        tile_prob = tile_probs(q_tile, key_all, q_base + q_first)
        tile_mix = jnp.einsum('bkgql,blkd->bqkgd', tile_prob.astype(jnp.bfloat16), value_all, preferred_element_type=jnp.float32)
        return tile_mix.astype(jnp.bfloat16)

    out_tiles = lax.map(one_tile, jnp.arange(seq_len // Q_TILE))
    return jnp.moveaxis(out_tiles, 0, 1).reshape(n_batch * seq_len, -1)


def attention_backward(q_grouped, key_all, value_all, grad_attn, q_base):
    n_batch, seq_len = q_grouped.shape[0], q_grouped.shape[1]
    head_dim = q_grouped.shape[-1]

    def one_tile(acc_pair, tile_idx):
        grad_k, grad_v = acc_pair
        q_first = tile_idx * Q_TILE
        q_tile = lax.dynamic_slice_in_dim(q_grouped, q_first, Q_TILE, axis=1)
        ga_tile = lax.dynamic_slice_in_dim(grad_attn, q_first, Q_TILE, axis=1)
        tile_prob = tile_probs(q_tile, key_all, q_base + q_first)
        grad_prob = jnp.einsum('bqkgd,blkd->bkgql', ga_tile, value_all, preferred_element_type=jnp.float32)
        row_dot = jnp.sum(tile_prob * grad_prob, axis=-1, keepdims=True)
        grad_score = (tile_prob * (grad_prob - row_dot) * (head_dim ** -0.5)).astype(jnp.bfloat16)
        grad_q = jnp.einsum('bkgql,blkd->bqkgd', grad_score, key_all, preferred_element_type=jnp.float32)
        grad_k = grad_k + jnp.einsum('bkgql,bqkgd->blkd', grad_score, q_tile, preferred_element_type=jnp.float32)
        grad_v = grad_v + jnp.einsum('bkgql,bqkgd->blkd', tile_prob.astype(jnp.bfloat16), ga_tile, preferred_element_type=jnp.float32)
        return (grad_k, grad_v), grad_q

    zero_acc = jnp.zeros(key_all.shape, jnp.float32)
    (grad_k, grad_v), q_tiles = lax.scan(one_tile, (zero_acc, zero_acc), jnp.arange(seq_len // Q_TILE))
    grad_q = jnp.moveaxis(q_tiles, 0, 1).reshape(n_batch, seq_len, -1, head_dim)
    return grad_q, grad_k, grad_v


def reduce_rows(values):
    return lax.psum_scatter(values, 'cp', scatter_dimension=0, tiled=True)


def solution(mesh):
    def device_step(x_act, d_out, positions, ln_gain, ln_bias, w_query, w_key, w_value, w_out):
        n_batch, seq_len, n_width = x_act.shape
        q_heads = w_query.shape[1]
        kv_heads, head_dim = w_key.shape[1], w_key.shape[2]
        n_tokens = n_batch * seq_len
        q_base = lax.axis_index('cp') * seq_len
        normed, x_hat, inv_std = norm_forward(x_act, ln_gain, ln_bias)
        flat_h = normed.reshape(n_tokens, n_width)
        cos_tab, sin_tab = rope_tables(positions, head_dim)
        q_act = rope_rotate(jnp.einsum('td,dnh->tnh', flat_h, w_query, preferred_element_type=jnp.float32).reshape(n_batch, seq_len, q_heads, head_dim), cos_tab, sin_tab).astype(jnp.bfloat16)
        k_act = rope_rotate(jnp.einsum('td,dnh->tnh', flat_h, w_key, preferred_element_type=jnp.float32).reshape(n_batch, seq_len, kv_heads, head_dim), cos_tab, sin_tab).astype(jnp.bfloat16)
        v_act = jnp.einsum('td,dnh->tnh', flat_h, w_value, preferred_element_type=jnp.float32).astype(jnp.bfloat16).reshape(n_batch, seq_len, kv_heads, head_dim)
        q_grouped = q_act.reshape(n_batch, seq_len, kv_heads, q_heads // kv_heads, head_dim)
        key_all = lax.all_gather(k_act, 'cp', axis=1, tiled=True)
        value_all = lax.all_gather(v_act, 'cp', axis=1, tiled=True)
        attn_act = attention_forward(q_grouped, key_all, value_all, q_base)
        block_out = (x_act.astype(jnp.float32) + jnp.dot(attn_act, w_out, preferred_element_type=jnp.float32).reshape(n_batch, seq_len, n_width)).astype(jnp.bfloat16)
        grad_flat = d_out.reshape(n_tokens, n_width)
        grad_wo = jnp.einsum('tn,td->nd', attn_act, grad_flat, preferred_element_type=jnp.float32)
        grad_attn = jnp.einsum('td,nd->tn', grad_flat, w_out, preferred_element_type=jnp.float32).astype(jnp.bfloat16).reshape(q_grouped.shape)
        kv_again = lax.all_gather(jnp.stack([k_act, v_act]), 'cp', axis=2, tiled=True)
        grad_q, grad_k_all, grad_v_all = attention_backward(q_grouped, kv_again[0], kv_again[1], grad_attn, q_base)
        grad_k_own = lax.psum_scatter(grad_k_all, 'cp', scatter_dimension=1, tiled=True)
        grad_v_own = lax.psum_scatter(grad_v_all, 'cp', scatter_dimension=1, tiled=True)
        grad_q_pre = rope_rotate(grad_q, cos_tab, -sin_tab).astype(jnp.bfloat16).reshape(n_tokens, q_heads, head_dim)
        grad_k_pre = rope_rotate(grad_k_own, cos_tab, -sin_tab).astype(jnp.bfloat16).reshape(n_tokens, kv_heads, head_dim)
        grad_v_pre = grad_v_own.astype(jnp.bfloat16).reshape(n_tokens, kv_heads, head_dim)
        grad_h = (jnp.einsum('tnh,dnh->td', grad_q_pre, w_query, preferred_element_type=jnp.float32) + jnp.einsum('tnh,dnh->td', grad_k_pre, w_key, preferred_element_type=jnp.float32) + jnp.einsum('tnh,dnh->td', grad_v_pre, w_value, preferred_element_type=jnp.float32)).reshape(n_batch, seq_len, n_width)
        grad_wq = jnp.einsum('td,tnh->dnh', flat_h, grad_q_pre, preferred_element_type=jnp.float32)
        grad_wk = jnp.einsum('td,tnh->dnh', flat_h, grad_k_pre, preferred_element_type=jnp.float32)
        grad_wv = jnp.einsum('td,tnh->dnh', flat_h, grad_v_pre, preferred_element_type=jnp.float32)
        grad_x = (d_out.astype(jnp.float32) + norm_backward(grad_h, x_hat, inv_std, ln_gain)).astype(jnp.bfloat16)
        grad_gain = lax.psum(jnp.sum(grad_h * x_hat, axis=(0, 1)), 'cp')
        grad_bias = lax.psum(jnp.sum(grad_h, axis=(0, 1)), 'cp')
        return (block_out, grad_x, reduce_rows(grad_wq), reduce_rows(grad_wk), reduce_rows(grad_wv), reduce_rows(grad_wo), grad_gain, grad_bias)

    return jax.shard_map(device_step, mesh=mesh, in_specs=(P('dp', 'cp', None), P('dp', 'cp', None), P('dp', 'cp'), P(None), P(None), P(None, None, None), P(None, None, None), P(None, None, None), P(None, None)), out_specs=(P('dp', 'cp', None), P('dp', 'cp', None), P(('dp', 'cp'), None, None), P(('dp', 'cp'), None, None), P(('dp', 'cp'), None, None), P(('dp', 'cp'), None), P('dp'), P('dp')), check_vma=False)
```

profile of v0, /device:TPU:21, one launch (start us, length us, event | category | flops | bytes accessed | tf_op | source)
XLA Modules:
  0.0 696.7 jit_solution(11692483180890109804)
XLA Ops:
  8.1 1.2 convert_reduce_fusion
  9.4 1.3 fusion.48
  11.4 2.6 fusion.75
  14.7 1.9 fusion.73
  19.0 6.2 fusion.71
  26.3 2.9 convolution_convert_fusion
  29.5 1.3 subtract_convert_fusion.1
  31.0 37.4 %all-gather.7.cloned.1.call-done = bf16[2,1,2048,8,64]{2,4,3,1,0:T(8,128)(2,1)} async-done(((bf16[2,1,128,8,64]{2,4,3,1,0:T(8,128)(2,1)}), bf16[2,1,2048,8,64]{2,4,3,1,0:T(8,128)(2,1)}) %all-gather.7.cloned.1.call-update) | async-done | bytes 4194320 | tf_op jit(solution)/shard_map/all_gather | solution.py:114
  68.4 15.2 %fusion.8 = (f32[8,4,128]{2,1,0:T(4,128)S(1)}, f32[8,2048,128,4]{2,1,3,0:T(8,128)}) fusion(pred[128,2048]{0,1:T(8,128)(4,1)S(1)} %iota_compare_fusion, bf16[128,8,4,32]{0,3,2,1:T(8,128)(2,1)S(1)} %bitcast.229, bf16[128,8,4,16]{0,3,2,1:T(8,128)(2,1)S(1)} %bitcast.237, bf16[128,8,4,16]{0,3,2,1:T(8,128)(2,1)S(1)} %bitcast.234, ...), kind=kOutput, calls=%fused_computation.15 | convolution fusion | flops 1100476416 | bytes 36454400 | tf_op jit(solution)/shard_map/while/body/eval_jaxpr/bqkgd,blkd->bkgql/dot_general | solution.py:43
  83.6 23.2 %all-gather.5.cloned.1.call-done = bf16[1,2048,8,64]{1,3,2,0:T(8,128)(2,1)} async-done(((bf16[1,128,8,64]{1,3,2,0:T(8,128)(2,1)}), bf16[1,2048,8,64]{1,3,2,0:T(8,128)(2,1)}) %all-gather.5.cloned.1.call-update) | async-done | bytes 2097168 | tf_op jit(solution)/shard_map/all_gather | solution.py:107
  106.7 27.2 %fusion.6 = (f32[8,4,128]{2,1,0:T(4,128)S(1)}, f32[8,4,128]{2,1,0:T(4,128)S(1)}, f32[8,2048,128,4]{2,1,3,0:T(8,128)}) fusion(f32[8,2048,128,4]{2,1,3,0:T(8,128)} %get-tuple-element.75, f32[8,4,128]{2,1,0:T(4,128)S(1)} %get-tuple-element.74, pred[128,2048]{0,1:T(8,128)(4,1)S(1)} %iota_compare_fusion, bf16[128,8,4,32]{0,3,2,1:T(8,128)(2,1)S(1)} %bitcast.230, ...), kind=kOutput, calls=%fused_computation.13 | convolution fusion | flops 1134026752 | bytes 70041600 | tf_op jit(solution)/shard_map/while/body/eval_jaxpr/bqkgd,blkd->bkgql/dot_general | solution.py:43
  133.9 36.8 %fusion = (f32[8,4,128]{2,1,0:T(4,128)S(1)}, f32[8,4,128]{2,1,0:T(4,128)}, f32[8,2048,128,4]{2,1,3,0:T(8,128)}) fusion(f32[8,4,128]{2,1,0:T(4,128)S(1)} %get-tuple-element.50, f32[8,4,128]{2,1,0:T(4,128)S(1)} %get-tuple-element.74, f32[8,2048,128,4]{2,1,3,0:T(8,128)} %get-tuple-element.75, pred[128,2048]{0,1:T(8,128)(4,1)S(1)} %iota_compare_fusion, ...), kind=kOutput, calls=%fused_computation.4 | convolution fusion | flops 1157619712 | bytes 103628800 | tf_op jit(solution)/shard_map/while/body/eval_jaxpr/bqkgd,blkd->bkgql/dot_general | solution.py:75
  170.8 28.1 %fusion.9 = bf16[8,4,128,2048]{2,3,1,0:T(8,128)(2,1)} fusion(f32[8,2048,128,4]{2,1,3,0:T(8,128)} %get-tuple-element.77, f32[8,4,128]{2,1,0:T(4,128)S(1)} %get-tuple-element.48, f32[8,4,128]{2,1,0:T(4,128)S(1)} %get-tuple-element.50, f32[8,4,128]{2,1,0:T(4,128)S(1)} %get-tuple-element.74, f32[8,2048,128,4]{2,1,3,0:T(8,128)} %get-tuple-element.75, ...), kind=kLoop, calls=%fused_computation.16 | loop fusion | flops 67108864 | bytes 84197376 | tf_op jit(solution)/shard_map/reshape.54
  198.9 12.9 %convolution_bitcast_fusion = f32[1,2048,8,64]{1,3,2,0:T(8,128)} fusion(bf16[8,4,128,2048]{2,3,1,0:T(8,128)(2,1)} %fusion.9, bf16[128,8,4,32]{0,3,2,1:T(8,128)(2,1)S(1)} %bitcast.231, bf16[128,8,4,16]{0,3,2,1:T(8,128)(2,1)S(1)} %bitcast.239, bf16[128,8,4,16]{0,3,2,1:T(8,128)(2,1)S(1)} %bitcast.236), kind=kOutput, calls=%fused_computation.23 | convolution fusion | flops 1075314688 | bytes 21495808 | tf_op jit(solution)/shard_map/while/body/eval_jaxpr/bkgql,bqkgd->blkd/dot_general | solution.py:79
  212.0 16.6 %fusion.16 = f32[1,2048,8,64]{1,3,2,0:T(8,128)} fusion(bf16[128,8,4,64]{0,3,2,1:T(8,128)(2,1)} %bitcast.242, f32[8,4,128]{2,1,0:T(4,128)S(1)} %get-tuple-element.50, f32[8,4,128]{2,1,0:T(4,128)S(1)} %get-tuple-element.74, f32[8,2048,128,4]{2,1,3,0:T(8,128)} %get-tuple-element.75, pred[128,2048]{0,1:T(8,128)(4,1)S(1)} %iota_compare_fusion), kind=kOutput, calls=%fused_computation.22 | convolution fusion | flops 1115684864 | bytes 38567936 | tf_op jit(solution)/shard_map/while/body/eval_jaxpr/bkgql,bqkgd->blkd/dot_general | solution.py:80
  229.6 37.9 %reduce-scatter.7.cloned.1.call-done = f32[1,128,8,64]{1,3,2,0:T(8,128)} async-done(((f32[1,2048,8,64]{1,3,2,0:T(8,128)}), f32[1,128,8,64]{1,3,2,0:T(8,128)}) %reduce-scatter.7.cloned.1.call-update) | async-done | bytes 262160 | tf_op jit(solution)/shard_map/reduce_scatter | solution.py:116
  270.1 2.9 fusion.67
  273.1 55.3 %reduce-scatter.9.cloned.1.call-done = f32[1,128,8,64]{1,3,2,0:T(8,128)} async-done(((f32[1,2048,8,64]{1,3,2,0:T(8,128)}), f32[1,128,8,64]{1,3,2,0:T(8,128)}) %reduce-scatter.9.cloned.1.call-update) | async-done | bytes 262160 | tf_op jit(solution)/shard_map/reduce_scatter | solution.py:117
  330.1 2.8 fusion.69
  333.0 9.4 %fusion.27 = f32[8,64,4,128]{3,1,2,0:T(8,128)S(1)} fusion(bf16[8,4,128,2048]{2,3,1,0:T(8,128)(2,1)} %fusion.9, bf16[2,1,2048,8,64]{2,4,3,1,0:T(8,128)(2,1)} %all-gather.7.cloned.1.call-done), kind=kOutput, calls=%fused_computation.39 | convolution fusion | flops 1073741824 | bytes 19922944 | tf_op jit(solution)/shard_map/while/body/eval_jaxpr/bkgql,blkd->bqkgd/dot_general | solution.py:78
  342.6 8.2 %fusion.65 = f32[2048,2048]{0,1} fusion(bf16[128,2048]{0,1:T(8,128)(2,1)S(1)} %bitcast.226, bf16[1,128,2048]{2,1,0:T(8,128)(2,1)S(1)} %copy-done.1, f32[2048]{0:T(1024)S(1)} %copy-done.20, f32[2048]{0:T(1024)S(1)} %copy-done.16, f32[128]{0:T(128)S(1)} %copy-done.34, f32[128]{0:T(128)S(1)} %copy-done.30), kind=kOutput, calls=%fused_computation.104 | convolution fusion | flops 1075314688 | bytes 17843200
  351.1 18.8 %all-gather.9.cloned.1.call-done = bf16[2048,8,64]{0,2,1:T(8,128)(2,1)} async-done(((bf16[128,8,64]{0,2,1:T(8,128)(2,1)}), bf16[2048,8,64]{0,2,1:T(8,128)(2,1)}) %all-gather.9.cloned.1.call-update) | async-done | bytes 2097168 | tf_op jit(solution)/shard_map/all_gather | solution.py:108
  369.9 15.4 %fusion.29 = bf16[8,64,4,128]{3,1,2,0:T(8,128)(2,1)S(1)} fusion(f32[8,4,128]{2,1,0:T(4,128)} %get-tuple-element.49, f32[8,4,128]{2,1,0:T(4,128)} %copy-done.36, f32[8,2048,128,4]{2,1,3,0:T(8,128)} %get-tuple-element.76, pred[128,2048]{0,1:T(8,128)(4,1)} %copy-done.12, bf16[2048,8,64]{0,2,1:T(8,128)(2,1)} %all-gather.9.cloned.1.call-done), kind=kOutput, calls=%fused_computation.43 | convolution fusion | flops 1115947008 | bytes 36470784 | tf_op jit(solution)/shard_map/while/body/eval_jaxpr/bkgql,blkd->bqkgd/dot_general | solution.py:58
  386.1 8.1 %fusion.50 = f32[2048,2048]{1,0:T(8,128)} fusion(bf16[128,2048]{0,1:T(8,128)(2,1)S(1)} %bitcast.220, bf16[1,128,2048]{2,1,0:T(8,128)(2,1)S(1)} %copy-done.4), kind=kOutput, calls=%fused_computation.66 | convolution fusion | flops 1073741824 | bytes 17825792 | tf_op jit(solution)/shard_map/tn,td->nd/dot_general | solution.py:112
  394.3 4.9 convolution_bitcast_fusion.1
  399.2 5.5 fusion.22
  406.0 1.0 copy-done.2
  407.2 45.0 %all-reduce = (f32[2048]{0:T(1024)}, f32[2048]{0:T(1024)}) all-reduce(f32[2048]{0:T(1024)S(1)} %get-tuple-element.44, f32[2048]{0:T(1024)S(1)} %get-tuple-element.46), channel_id=1, replica_groups=mesh['dp'=4,'cp'=16] {'cp'}, use_global_device_ids=true, to_apply=%region_16.17 | all-reduce | flops 4096 | bytes 32768 | tf_op jit(solution)/shard_map/psum | solution.py:126
  452.2 2.5 fusion.46
  454.7 35.0 %reduce-scatter.15.cloned.1.call-done = f32[128,8,64]{0,2,1:T(8,128)} async-done(((f32[2048,8,64]{0,2,1:T(8,128)}), f32[128,8,64]{0,2,1:T(8,128)}) %reduce-scatter.15.cloned.1.call-update) | async-done | bytes 262160 | tf_op jit(solution)/shard_map/reduce_scatter | solution.py:90
  489.7 101.4 %reduce-scatter.11.cloned.1.call-done = f32[128,32,64]{0,2,1:T(8,128)} async-done(((f32[2048,32,64]{0,2,1:T(8,128)}), f32[128,32,64]{0,2,1:T(8,128)}) %reduce-scatter.11.cloned.1.call-update) | async-done | bytes 1048592 | tf_op jit(solution)/shard_map/reduce_scatter | solution.py:90
  591.1 98.9 %reduce-scatter.17.cloned.1.call-done = f32[128,2048]{1,0:T(8,128)} async-done(((f32[2048,2048]{1,0:T(8,128)}), f32[128,2048]{1,0:T(8,128)}) %reduce-scatter.17.cloned.1.call-update) | async-done | bytes 1048592 | tf_op jit(solution)/shard_map/reduce_scatter | solution.py:90
  (125 shorter events, 14.5 us)
Async XLA Ops:
  7.2 19.1 %copy-start.3 = (bf16[1,128,2048]{2,1,0:T(8,128)(2,1)S(1)}, bf16[1,128,2048]{2,1,0:T(8,128)(2,1)}, u32[]{:S(2)}) copy-start(bf16[1,128,2048]{2,1,0:T(8,128)(2,1)} %param.10) | copy-start | bytes 1572868
  7.2 61.2 %all-gather.7.cloned.1.call-start = ((), (), s32[]{:S(2)}) async-start(), calls=%async_computation.7 | async-start | bytes 4456448 | tf_op jit(solution)/shard_map/all_gather | solution.py:114
  8.1 17.1 %copy-start.15 = (f32[2048]{0:T(1024)}, f32[2048]{0:T(1024)S(1)}, u32[]{:S(2)}) copy-start(f32[2048]{0:T(1024)S(1)} %broadcast_add_fusion) | copy-start | bytes 24580
  9.4 15.9 %copy-start.28 = (f32[128]{0:T(128)}, f32[128]{0:T(128)S(1)}, u32[]{:S(2)}) copy-start(f32[128]{0:T(128)S(1)} %broadcast_multiply_fusion.2) | copy-start | bytes 1540
  10.7 14.6 %copy-start.32 = (f32[128]{0:T(128)}, f32[128]{0:T(128)S(1)}, u32[]{:S(2)}) copy-start(f32[128]{0:T(128)S(1)} %add_rsqrt_fusion) | copy-start | bytes 1540
  17.3 66.3 %copy-start.25 = (f32[128,16]{0,1:T(8,128)}, f32[128,16]{0,1:T(8,128)S(1)}, u32[]{:S(2)}) copy-start(f32[128,16]{0,1:T(8,128)S(1)} %get-tuple-element.73) | copy-start | bytes 24580
  18.1 88.6 %all-gather.5.cloned.1.call-start = ((), (), s32[]{:S(2)}) async-start(), calls=%async_computation.6 | async-start | bytes 2228224 | tf_op jit(solution)/shard_map/all_gather | solution.py:107
  18.9 248.5 %reduce-scatter.7.cloned.1.call-start = ((), (), s32[]{:S(2)}) async-start(), calls=%async_computation.8 | async-start | bytes 4456448 | tf_op jit(solution)/shard_map/reduce_scatter | solution.py:116
  29.5 104.5 %copy-start.19 = (bf16[128,2048]{0,1:T(8,128)(2,1)}, bf16[128,2048]{0,1:T(8,128)(2,1)S(1)}, u32[]{:S(2)}) copy-start(bf16[128,2048]{0,1:T(8,128)(2,1)S(1)} %copy.24) | copy-start | bytes 1572868
  31.0 181.0 %copy-start.12 = (pred[128,2048]{0,1:T(8,128)(4,1)}, pred[128,2048]{0,1:T(8,128)(4,1)S(1)}, u32[]{:S(2)}) copy-start(pred[128,2048]{0,1:T(8,128)(4,1)S(1)} %iota_compare_fusion) | copy-start | bytes 786436
  133.9 36.8 %copy-start.36 = (f32[8,4,128]{2,1,0:T(4,128)}, f32[8,4,128]{2,1,0:T(4,128)S(1)}, u32[]{:S(2)}) copy-start(f32[8,4,128]{2,1,0:T(4,128)S(1)} %get-tuple-element.60) | copy-start | bytes 49156
  211.9 16.9 %copy-start.14 = (f32[128,512]{0,1:S(1)}, f32[128,512]{0,1}, u32[]{:S(2)}) copy-start(f32[128,512]{0,1} %copy-done.13) | copy-start | bytes 786436
  211.9 55.6 %copy-start.26 = (f32[128,16]{0,1:T(8,128)S(1)}, f32[128,16]{0,1:T(8,128)}, u32[]{:S(2)}) copy-start(f32[128,16]{0,1:T(8,128)} %copy-done.25) | copy-start | bytes 24580
  211.9 55.6 %copy-start.27 = (f32[128,16]{0,1:T(8,128)S(1)}, f32[128,16]{0,1:T(8,128)}, u32[]{:S(2)}) copy-start(f32[128,16]{0,1:T(8,128)} %get-tuple-element.71) | copy-start | bytes 24580
  211.9 58.1 %copy-start.1 = (bf16[1,128,2048]{2,1,0:T(8,128)(2,1)S(1)}, bf16[1,128,2048]{2,1,0:T(8,128)(2,1)}, u32[]{:S(2)}) copy-start(bf16[1,128,2048]{2,1,0:T(8,128)(2,1)} %param.9) | copy-start | bytes 1572868
  211.9 58.1 %copy-start.16 = (f32[2048]{0:T(1024)S(1)}, f32[2048]{0:T(1024)}, u32[]{:S(2)}) copy-start(f32[2048]{0:T(1024)} %copy-done.15) | copy-start | bytes 24580
  211.9 58.1 %copy-start.20 = (f32[2048]{0:T(1024)S(1)}, f32[2048]{0:T(1024)}, u32[]{:S(2)}) copy-start(f32[2048]{0:T(1024)} %param.13) | copy-start | bytes 24580
  211.9 58.1 %copy-start.29 = (f32[128]{0:T(128)S(1)}, f32[128]{0:T(128)}, u32[]{:S(2)}) copy-start(f32[128]{0:T(128)} %copy-done.28) | copy-start | bytes 1540
  211.9 58.1 %copy-start.33 = (f32[128]{0:T(128)S(1)}, f32[128]{0:T(128)}, u32[]{:S(2)}) copy-start(f32[128]{0:T(128)} %copy-done.32) | copy-start | bytes 1540
  212.0 116.5 %reduce-scatter.9.cloned.1.call-start = ((), (), s32[]{:S(2)}) async-start(), calls=%async_computation.9 | async-start | bytes 4456448 | tf_op jit(solution)/shard_map/reduce_scatter | solution.py:117
  228.7 141.3 %all-gather.9.cloned.1.call-start = ((), (), s32[]{:S(2)}) async-start(), calls=%async_computation.14 | async-start | bytes 2228224 | tf_op jit(solution)/shard_map/all_gather | solution.py:108
  229.5 225.2 %reduce-scatter.13.cloned.1.call-start = ((), (), s32[]{:S(2)}) async-start(), calls=%async_computation.11 | async-start | bytes 4456448 | tf_op jit(solution)/shard_map/reduce_scatter | solution.py:90
  273.0 216.7 %reduce-scatter.15.cloned.1.call-start = ((), (), s32[]{:S(2)}) async-start(), calls=%async_computation.12 | async-start | bytes 4456448 | tf_op jit(solution)/shard_map/reduce_scatter | solution.py:90
  330.1 12.5 %copy-start.30 = (f32[128]{0:T(128)S(1)}, f32[128]{0:T(128)}, u32[]{:S(2)}) copy-start(f32[128]{0:T(128)} %copy-done.28) | copy-start | bytes 1540
  330.1 12.5 %copy-start.34 = (f32[128]{0:T(128)S(1)}, f32[128]{0:T(128)}, u32[]{:S(2)}) copy-start(f32[128]{0:T(128)} %copy-done.32) | copy-start | bytes 1540
  333.0 258.1 %reduce-scatter.11.cloned.1.call-start = ((), (), s32[]{:S(2)}) async-start(), calls=%async_computation.10 | async-start | bytes 17825792 | tf_op jit(solution)/shard_map/reduce_scatter | solution.py:90
  350.9 339.1 %reduce-scatter.17.cloned.1.call-start = ((), (), s32[]{:S(2)}) async-start(), calls=%async_computation.13 | async-start | bytes 17825792 | tf_op jit(solution)/shard_map/reduce_scatter | solution.py:90
  369.9 16.2 %copy-start.4 = (bf16[1,128,2048]{2,1,0:T(8,128)(2,1)S(1)}, bf16[1,128,2048]{2,1,0:T(8,128)(2,1)}, u32[]{:S(2)}) copy-start(bf16[1,128,2048]{2,1,0:T(8,128)(2,1)} %param.10) | copy-start | bytes 1572868
  394.3 10.9 %copy-start.18 = (bf16[128,8,32]{0,2,1:T(8,128)(2,1)S(1)}, bf16[128,8,32]{0,2,1:T(8,128)(2,1)}, u32[]{:S(2)}) copy-start(bf16[128,8,32]{0,2,1:T(8,128)(2,1)} %copy-done.17) | copy-start | bytes 196612
  394.3 10.9 %copy-start.22 = (bf16[128,8,16]{0,2,1:T(8,128)(2,1)S(1)}, bf16[128,8,16]{0,2,1:T(8,128)(2,1)}, u32[]{:S(2)}) copy-start(bf16[128,8,16]{0,2,1:T(8,128)(2,1)} %copy-done.21) | copy-start | bytes 98308
  394.3 10.9 %copy-start.24 = (bf16[128,8,16]{0,2,1:T(8,128)(2,1)S(1)}, bf16[128,8,16]{0,2,1:T(8,128)(2,1)}, u32[]{:S(2)}) copy-start(bf16[128,8,16]{0,2,1:T(8,128)(2,1)} %copy-done.23) | copy-start | bytes 98308
  394.3 10.9 %copy-start.31 = (f32[128]{0:T(128)S(1)}, f32[128]{0:T(128)}, u32[]{:S(2)}) copy-start(f32[128]{0:T(128)} %copy-done.28) | copy-start | bytes 1540
  (16 other events, 75.1 us)
Sparse Core Ops, SparseCore 0:
  18.2 50.0 all-gather.6
  70.5 36.1 all-gather.4
  212.0 55.4 reduce-scatter.6
  269.7 58.7 reduce-scatter.8
  330.4 39.4 all-gather.8
  372.7 55.5 reduce-scatter.12
  431.2 58.5 reduce-scatter.14
  492.7 98.3 reduce-scatter.10
  594.0 95.9 reduce-scatter.16
where the time goes:
time: 703 us; the launch traced here: 697 us
  waiting for transfers between devices  408 us (58%)
  matrix products  180 us (26%)
  blocking collectives  45 us (6%)
  other arithmetic  41.2 us (6%)
  between operations  14.7 us (2%)
    reduce_scatter x4, waiting for transfers between devices, reduce_rows(): return lax.psum_scatter(values, 'cp', scatter_dimension=0, tiled=True)  235 us
    reduce_scatter x1, waiting for transfers between devices, device_step(): lax.psum_scatter(grad_v_all, 'cp', scatter_dimension=1, tiled=True)  55.3 us
    psum x1, blocking collectives, device_step(): grad_gain = lax.psum(jnp.sum(grad_h * x_hat, axis=(0, 1)), 'cp')  45 us
    dot_general x2, matrix products, tile_probs(): jnp.einsum('bqkgd,blkd->bkgql', q_tile, key_all, preferred_element_type=j...  42.4 us
    reduce_scatter x1, waiting for transfers between devices, device_step(): lax.psum_scatter(grad_k_all, 'cp', scatter_dimension=1, tiled=True)  37.9 us
    all_gather x1, waiting for transfers between devices, device_step(): lax.all_gather(jnp.stack([k_act, v_act]), 'cp', axis=2, tiled=True)  37.4 us
    dot_general x1, matrix products, one_tile(): jnp.einsum('bqkgd,blkd->bkgql', ga_tile, value_all, preferred_element_typ...  36.8 us
    another operation x3, other arithmetic  29.5 us
  transfers between devices with their start and end apart: 9, of which 8 were waited for; matrix products, arithmetic and copies ran while one was open for 15% of the time, Pallas kernels for 0%

commit v1 on v0

v1 whole, which is shorter than its diff:
```python
import functools
import math

import jax
import jax.numpy as jnp
from jax import lax
from jax.experimental import pallas as pl
from jax.experimental.pallas import tpu as pltpu
from jax.sharding import PartitionSpec as P

EPS = 1e-5
ROPE_BASE = 10000.0
MESH = pl.DeviceIdType.MESH
BF = jnp.bfloat16
F32 = jnp.float32


def dot(lhs, rhs):
    return jnp.dot(lhs, rhs, preferred_element_type=F32)


def block_kernel(
    n_dev, hd, kv_w,
    x_hbm, dy_hbm, pos_ref, gain_ref, bias_ref, wq_hbm, wk_hbm, wv_hbm, wo_hbm,
    out_hbm, gx_hbm, gw_hbm, gwo_hbm, gg_hbm,
    hb, dyb, wt, wi_raw, wi, woi_raw, woi, pos_all, trig,
    qt, kvt, kv, bmat, bmat_t, sbuf, dpbuf, pds, dkv, dkvt, kv_rv, kv_mine,
    dwo, dwt, at_st, dqt_st, at_rv, dt_rv, a_nat, d_nat, x_v, dy_own, xhat, stat, dh, out_v, gg_st, gg_rv, gg_out,
    in_sem, wo_sem, w_sem, out_sem, loc_sem,
    hzs, hzr, hds, hdr, yzs, yzr, yds, ydr,
    pos_s, pos_r, a_s, a_r, q_s, q_r, x_s, x_r, kv_s, kv_r, w_s, w_r, wk_s, wk_r, g_s, g_r,
):
    tok, width = x_v.shape
    n_chip = n_dev // 2
    half = tok // 2
    me = lax.axis_index('cp')
    chip = me // 2
    core = me % 2
    right = 2 * ((chip + 1) % n_chip) + core
    left = 2 * ((chip + n_chip - 1) % n_chip) + core
    mate = 2 * chip + 1 - core
    q_rows = wq_hbm.shape[0]
    hw = 2 * hd
    quarter = hd // 4

    def remote(src, dst, send, recv, target):
        return pltpu.make_async_remote_copy(src_ref=src, dst_ref=dst, send_sem=send, recv_sem=recv, device_id={'cp': target}, device_id_type=MESH)

    def local(src, dst, sem):
        return pltpu.make_async_copy(src, dst, sem)

    load_x = local(x_hbm, x_v, in_sem.at[0])
    load_x.start()
    own_rows = pl.multiple_of(me * hw, hw)
    kv_rows = pl.multiple_of(chip * hd, hd)
    loads = [
        local(wq_hbm.at[pl.ds(own_rows, hw)], wi_raw.at[pl.ds(0, hw)], in_sem.at[1]),
        local(wk_hbm.at[pl.ds(kv_rows, hd)], wi_raw.at[pl.ds(hw, hd)], in_sem.at[2]),
        local(wv_hbm.at[pl.ds(kv_rows, hd)], wi_raw.at[pl.ds(hw + hd, hd)], in_sem.at[3]),
        local(wo_hbm.at[pl.ds(own_rows, hw)], woi_raw, in_sem.at[4]),
        local(dy_hbm, dyb.at[me], in_sem.at[5]),
        local(dy_hbm, dy_own, in_sem.at[6]),
    ]
    for item in loads:
        item.start()
    barrier = pltpu.get_barrier_semaphore()
    for step in range(1, n_dev):
        pl.semaphore_signal(barrier, inc=1, device_id={'cp': (me + step) % n_dev}, device_id_type=MESH)
    weight_loads = [
        local(wq_hbm, wt.at[pl.ds(0, q_rows)], w_sem.at[0]),
        local(wk_hbm, wt.at[pl.ds(q_rows, kv_w)], w_sem.at[1]),
        local(wv_hbm, wt.at[pl.ds(q_rows + kv_w, kv_w)], w_sem.at[2]),
    ]
    for item in weight_loads:
        item.start()

    load_x.wait()
    gain_one = 1.0 + gain_ref[...]
    x_f = x_v[...].astype(F32)
    centered = x_f - jnp.mean(x_f, axis=-1, keepdims=True)
    inv_std = lax.rsqrt(jnp.mean(centered * centered, axis=-1, keepdims=True) + EPS)
    x_hat = centered * inv_std
    xhat[...] = x_hat
    stat[...] = jnp.broadcast_to(inv_std, stat.shape)
    hb[me] = (x_hat * gain_one + bias_ref[...]).astype(BF)
    pos_all[me] = pos_ref[...]
    dkv[...] = jnp.zeros_like(dkv)
    dwo[...] = jnp.zeros_like(dwo)
    dwt[...] = jnp.zeros_like(dwt)
    bmat[...] = jnp.zeros_like(bmat)

    pl.semaphore_wait(barrier, n_dev - 1)

    def chunk(buf, slot, part):
        return buf.at[slot, pl.ds(pl.multiple_of(part * half, half), half)]

    def own_sends(buf, zs, zr, ds, dr):
        copies = []
        for part in range(2):
            piece = chunk(buf, me, part)
            copies.append(remote(piece, piece, zs.at[2 * part], zr.at[2 * part], right))
            copies.append(remote(piece, piece, zs.at[2 * part + 1], zr.at[2 * part + 1], left))
            copies.append(remote(piece, piece, ds.at[14 + part], dr.at[14 + part], mate))
        return copies

    def event_place(event, parity):
        step = event // 4 + 1
        turn = event % 4
        direction = turn % 2
        part = jnp.where(step < 4, turn // 2, turn)
        origin = jnp.where(direction == 0, chip + n_chip - step, chip + step) % n_chip
        return step, turn, direction, part, 2 * origin + parity

    def ring_event(buf, zs, zr, ds, dr, event):
        step, turn, direction, part, slot = event_place(event, core)
        piece = chunk(buf, slot, part)
        remote(piece, piece, zs.at[0], zr.at[event], right).wait_recv()
        onward = jnp.where(step < 3, event + 4, jnp.where(turn == 0, 12, 13))

        @pl.when((step < 3) | ((step == 3) & ((turn == 0) | (turn == 3))))
        def _():
            remote(piece, piece, zs.at[event + 4], zr.at[onward], jnp.where(direction == 0, right, left)).start()

        remote(piece, piece, ds.at[event], dr.at[event], mate).start()

    def ring_service(buf, zs, zr, ds, dr, k):
        @pl.when(k < 2)
        def _():
            ring_event(buf, zs, zr, ds, dr, 2 * k)
            ring_event(buf, zs, zr, ds, dr, 2 * k + 1)

        @pl.when((k >= 2) & (k < 12))
        def _():
            ring_event(buf, zs, zr, ds, dr, k + 2)

    def ring_slot(buf, ds, dr, k):
        turn = jnp.maximum(k - 2, 0)
        step = turn // 4 + 1
        way = turn % 4
        direction = way // 2
        other = jnp.where(k < 2, k, way % 2)
        origin = jnp.where(direction == 0, chip + n_chip - step, chip + step) % n_chip
        slot = 2 * jnp.where(k < 2, chip, origin) + jnp.where(other == 1, 1 - core, core)

        @pl.when(other == 1)
        def _():
            first = jnp.where(k < 2, 14, jnp.where(step < 4, 4 * (step - 1) + direction, 12))
            second = jnp.where(k < 2, 15, jnp.where(step < 4, 4 * (step - 1) + 2 + direction, 13))
            for part, event in ((0, first), (1, second)):
                piece = chunk(buf, slot, part)
                remote(piece, piece, ds.at[0], dr.at[event], mate).wait_recv()

        return slot

    h_sends = own_sends(hb, hzs, hzr, hds, hdr)
    for item in h_sends:
        item.start()
    pos_sends = [remote(pos_all.at[me], pos_all.at[me], pos_s.at[step], pos_r.at[step], (me + step) % n_dev) for step in range(1, n_dev)]
    for item in pos_sends:
        item.start()

    for item in loads:
        item.wait()
    for t in range(width // 128):
        cols = slice(128 * t, 128 * t + 128)
        wi[cols, 0:hw] = wi_raw[0:hw, cols].T
        wi[cols, hw:2 * hw] = wi_raw[hw:2 * hw, cols].T
        woi[cols, :] = woi_raw[:, cols].T

    freq = jnp.exp(lax.broadcasted_iota(jnp.int32, (quarter, tok), 0).astype(F32) * (-2.0 * math.log(ROPE_BASE) / (hd // 2)))

    def make_trig(slot):
        angle = pos_all[slot].astype(F32) * freq
        trig[slot, 0:quarter, :] = jnp.cos(angle)
        trig[slot, quarter:2 * quarter, :] = jnp.sin(angle)

    make_trig(me)
    for step in range(1, n_dev):
        source = (me + n_dev - step) % n_dev
        remote(pos_all.at[source], pos_all.at[source], pos_s.at[step], pos_r.at[step], me).wait_recv()
        make_trig(source)

    y_sends = own_sends(dyb, yzs, yzr, yds, ydr)

    @pl.loop(0, n_dev)
    def _(k):
        ring_service(hb, hzs, hzr, hds, hdr, k)

        @pl.when(k == 10)
        def _():
            for item in y_sends:
                item.start()

        slot = ring_slot(hb, hds, hdr, k)
        flat = dot(hb[slot], wi[...])
        q_f = flat[:, 0:hw].T
        kv_f = flat[:, hw:2 * hw].T
        cos_t = trig[slot, 0:quarter, :]
        sin_t = trig[slot, quarter:2 * quarter, :]

        def turned(val, base):
            u = val[base:base + quarter]
            w = val[base + quarter:base + 2 * quarter]
            return [u * cos_t - w * sin_t, w * cos_t + u * sin_t, val[base + 2 * quarter:base + hd]]

        for head in range(2):
            qt[slot, :, tok * head:tok * head + tok] = jnp.concatenate(turned(q_f, hd * head), axis=0).astype(BF)
        kv_rot = jnp.concatenate(turned(kv_f, 0) + [kv_f[hd:2 * hd]], axis=0).astype(BF)
        place = pl.ds(pl.multiple_of(slot * tok, tok), tok)
        kvt[:, place] = kv_rot
        kv[place, :] = kv_rot.T

    chunk_k = 2 * tok
    scale = hd ** -0.5

    @pl.loop(0, n_dev)
    def _(k):
        ring_service(dyb, yzs, yzr, yds, ydr, k)
        slot = ring_slot(dyb, yds, ydr, k)
        da = dot(dyb[slot], woi[...]).astype(BF)
        da_t = da.T
        bmat[0:hd, 0:2 * tok] = qt[slot]
        bmat[hd:2 * hd, 2 * tok:3 * tok] = da_t[0:hd]
        bmat[hd:2 * hd, 3 * tok:4 * tok] = da_t[hd:2 * hd]
        for t in range(4):
            bmat_t[tok * t:tok * t + tok, :] = bmat[:, tok * t:tok * t + tok].T
        n_chunks = slot // 2 + 1
        q_index = slot * tok + lax.broadcasted_iota(jnp.int32, (chunk_k, 2 * tok), 1) % tok
        k_row = lax.broadcasted_iota(jnp.int32, (chunk_k, 2 * tok), 0)

        def scores(c, top):
            rows = pl.ds(pl.multiple_of(c * chunk_k, chunk_k), chunk_k)
            both = dot(kv[rows, :], bmat[...])
            s = jnp.where(k_row + c * chunk_k <= q_index, both[:, 0:2 * tok] * scale, -1e30)
            sbuf[rows, :] = s
            dpbuf[rows, :] = both[:, 2 * tok:4 * tok]
            return jnp.maximum(top, jnp.max(s, axis=0, keepdims=True))

        top = lax.fori_loop(0, n_chunks, scores, jnp.full((1, 2 * tok), -3e38, F32))

        def exps(c, sums):
            rows = pl.ds(pl.multiple_of(c * chunk_k, chunk_k), chunk_k)
            p = jnp.exp(sbuf[rows, :] - top)
            sbuf[rows, :] = p
            return sums[0] + jnp.sum(p, axis=0, keepdims=True), sums[1] + jnp.sum(p * dpbuf[rows, :], axis=0, keepdims=True)

        zero_row = jnp.zeros((1, 2 * tok), F32)
        total, weighted = lax.fori_loop(0, n_chunks, exps, (zero_row, zero_row))
        inv = 1.0 / total
        row_dot = weighted * inv

        def grads(c, acc):
            rows = pl.ds(pl.multiple_of(c * chunk_k, chunk_k), chunk_k)
            p = sbuf[rows, :] * inv
            p_b = p.astype(BF)
            ds_b = (p * (dpbuf[rows, :] - row_dot) * scale).astype(BF)
            pds[:, 0:2 * tok] = ds_b
            pds[:, 2 * tok:4 * tok] = p_b
            dkv[rows, :] += dot(pds[...], bmat_t[...])
            return acc[0] + dot(kvt[hd:2 * hd, rows], p_b), acc[1] + dot(kvt[0:hd, rows], ds_b)

        zero_acc = jnp.zeros((hd, 2 * tok), F32)
        a_acc, dq_acc = lax.fori_loop(0, n_chunks, grads, (zero_acc, zero_acc))
        a_t = jnp.concatenate([a_acc[:, 0:tok], a_acc[:, tok:2 * tok]], axis=0).astype(BF)
        cos_t = trig[slot, 0:quarter, :]
        sin_t = trig[slot, quarter:2 * quarter, :]
        parts = []
        for head in range(2):
            u = dq_acc[0:quarter, tok * head:tok * head + tok]
            w = dq_acc[quarter:2 * quarter, tok * head:tok * head + tok]
            parts += [u * cos_t + w * sin_t, w * cos_t - u * sin_t, dq_acc[2 * quarter:hd, tok * head:tok * head + tok]]
        dq_t = jnp.concatenate(parts, axis=0).astype(BF)
        at_st[slot] = a_t
        dqt_st[slot] = dq_t

        @pl.when(slot == me)
        def _():
            at_rv[pl.ds(own_rows, hw), :] = a_t
            dt_rv[pl.ds(own_rows, hw), :] = dq_t

        @pl.when(slot != me)
        def _():
            remote(dqt_st.at[slot], dt_rv.at[pl.ds(own_rows, hw)], q_s.at[slot], q_r.at[me], slot).start()
            remote(at_st.at[slot], at_rv.at[pl.ds(own_rows, hw)], a_s.at[slot], a_r.at[me], slot).start()

        for t in range(width // 256):
            cols = slice(256 * t, 256 * t + 256)
            dwo[:, cols] += dot(a_t, dyb[slot, :, cols])
            dwt[0:hw, cols] += dot(dq_t, hb[slot, :, cols])

    for t in range(n_dev):
        dkvt[:, tok * t:tok * t + tok] = dkv[tok * t:tok * t + tok, :].T
    mine = pl.multiple_of(core * hd, hd)
    theirs = pl.multiple_of((1 - core) * hd, hd)
    swap = remote(dkvt.at[pl.ds(theirs, hd)], kv_rv, x_s, x_r, mate)
    swap.start()
    store_wo = local(dwo, gwo_hbm, out_sem.at[0])
    store_wo.start()

    def send_order():
        order = []
        for step in range(1, n_chip // 2 + 1):
            order += [step, n_chip - step] if 2 * step < n_chip else [step]
        return [(chip + step) % n_chip for step in order]

    targets = [mate] + [2 * far + c for far in send_order() for c in range(2)]

    swap.wait_recv()
    for t in range(n_dev):
        cols = slice(tok * t, tok * t + tok)
        g = dkvt[pl.ds(mine, hd), cols] + kv_rv[:, cols]
        cos_t = jnp.where(core == 0, trig[t, 0:quarter, :], 1.0)
        sin_t = jnp.where(core == 0, trig[t, quarter:2 * quarter, :], 0.0)
        u = g[0:quarter]
        w = g[quarter:2 * quarter]
        kv_mine[t] = jnp.concatenate([u * cos_t + w * sin_t, w * cos_t - u * sin_t, g[2 * quarter:hd]], axis=0).astype(BF)
    g_rows = pl.multiple_of(q_rows + core * kv_w + chip * hd, hd)
    dt_rv[pl.ds(g_rows, hd), :] = kv_mine[me]
    kv_sends = [remote(kv_mine.at[t], dt_rv.at[pl.ds(g_rows, hd)], kv_s.at[t], kv_r.at[me], t) for t in targets]
    for item in kv_sends:
        item.start()

    def block_cols(t):
        return pl.ds(pl.multiple_of(t * tok, tok), tok)

    w_own = local(dwt.at[pl.ds(0, hw), block_cols(me)], gw_hbm.at[pl.ds(own_rows, hw)], loc_sem.at[0])
    w_own.start()
    w_sends = [remote(dwt.at[pl.ds(0, hw), block_cols(t)], gw_hbm.at[pl.ds(own_rows, hw)], w_s.at[t], w_r.at[me], t) for t in targets]
    for item in w_sends:
        item.start()

    for t in range(width // 256):
        cols = slice(256 * t, 256 * t + 256)
        acc = jnp.zeros((hd, 256), F32)
        for s in range(0, n_dev):
            acc += dot(kv_mine[s], hb[s, :, cols])
        dwt[hw:hw + hd, cols] = acc
    wk_own = local(dwt.at[pl.ds(hw, hd), block_cols(me)], gw_hbm.at[pl.ds(g_rows, hd)], loc_sem.at[1])
    wk_own.start()

    def event_forwarded(event):
        return event < 8 or event in (8, 11)

    def finish_ring(buf, zs, zr, ds, dr):
        for item in own_sends(buf, zs, zr, ds, dr):
            item.wait_send()
        for event in range(14):
            _, _, direction, part, slot = event_place(event, core)
            piece = chunk(buf, slot, part)
            if event_forwarded(event):
                remote(piece, piece, zs.at[event + 4], zr.at[event], right).wait_send()
            remote(piece, piece, ds.at[event], dr.at[event], mate).wait_send()

    finish_ring(dyb, yzs, yzr, yds, ydr)
    wo_loads = [local(wo_hbm.at[pl.ds(tok * t, tok)], dyb.at[t], wo_sem.at[t]) for t in range(n_dev)]
    for item in wo_loads:
        item.start()

    for t in targets:
        rows = pl.ds(pl.multiple_of(t * hw, hw), hw)
        remote(at_st.at[0], at_rv.at[rows], a_s.at[t], a_r.at[t], t).wait_recv()
    for t in range(n_dev):
        a_nat[:, 128 * t:128 * t + 128] = at_rv[128 * t:128 * t + 128, :].T
    for item in wo_loads:
        item.wait()
    for t in range(width // 256):
        cols = slice(256 * t, 256 * t + 256)
        acc = x_v[:, cols].astype(F32)
        prod = jnp.zeros((tok, 256), F32)
        for s in range(n_dev):
            prod += dot(a_nat[:, 128 * s:128 * s + 128], dyb[s, :, cols])
        out_v[:, cols] = (acc + prod).astype(BF)
    store_out = local(out_v, out_hbm, out_sem.at[1])
    store_out.start()

    for item in weight_loads:
        item.wait()
    for t in targets:
        rows = pl.ds(pl.multiple_of(t * hw, hw), hw)
        remote(dqt_st.at[0], dt_rv.at[rows], q_s.at[t], q_r.at[t], t).wait_recv()
        rows = pl.ds(pl.multiple_of(q_rows + (t % 2) * kv_w + (t // 2) * hd, hd), hd)
        remote(kv_mine.at[0], dt_rv.at[rows], kv_s.at[t], kv_r.at[t], t).wait_recv()
    n_rows = q_rows + 2 * kv_w
    for t in range(n_rows // 128):
        d_nat[:, 128 * t:128 * t + 128] = dt_rv[128 * t:128 * t + 128, :].T

    for t in range(width // 256):
        cols = slice(256 * t, 256 * t + 256)
        acc = jnp.zeros((tok, 256), F32)
        for s in range(n_rows // 256):
            acc += dot(d_nat[:, 256 * s:256 * s + 256], wt[256 * s:256 * s + 256, cols])
        dh[:, cols] = acc
        gg_st[0:1, cols] = jnp.sum(acc * xhat[:, cols], axis=0, keepdims=True)
        gg_st[1:2, cols] = jnp.sum(acc, axis=0, keepdims=True)
    gg_rv[me] = gg_st[...]
    g_sends = [remote(gg_st, gg_rv.at[me], g_s.at[t], g_r.at[me], t) for t in targets]
    for item in g_sends:
        item.start()
    wk_sends = [remote(dwt.at[pl.ds(hw, hd), block_cols(t)], gw_hbm.at[pl.ds(g_rows, hd)], wk_s.at[t], wk_r.at[me], t) for t in targets]
    for item in wk_sends:
        item.start()

    grad_hat = dh[...] * gain_one
    x_hat = xhat[...]
    mean_one = jnp.mean(grad_hat, axis=-1, keepdims=True)
    mean_two = jnp.mean(grad_hat * x_hat, axis=-1, keepdims=True)
    store_out.wait()
    out_v[...] = (dy_own[...].astype(F32) + stat[:, 0:1] * (grad_hat - mean_one - x_hat * mean_two)).astype(BF)
    store_gx = local(out_v, gx_hbm, out_sem.at[2])
    store_gx.start()

    for t in targets:
        remote(gg_st, gg_rv.at[t], g_s.at[t], g_r.at[t], t).wait_recv()
    sums = gg_rv[0]
    for t in range(1, n_dev):
        sums = sums + gg_rv[t]
    gg_out[...] = sums
    store_gg = local(gg_out, gg_hbm, out_sem.at[3])
    store_gg.start()

    finish_ring(hb, hzs, hzr, hds, hdr)
    for item in pos_sends:
        item.wait_send()
    for t in targets:
        remote(at_st.at[0], at_rv.at[pl.ds(0, hw)], a_s.at[t], a_r.at[t], t).wait_send()
        remote(dqt_st.at[0], dt_rv.at[pl.ds(0, hw)], q_s.at[t], q_r.at[t], t).wait_send()
    swap.wait_send()
    for item in kv_sends + w_sends + g_sends + wk_sends:
        item.wait_send()
    for t in targets:
        rows = pl.ds(pl.multiple_of(t * hw, hw), hw)
        remote(dwt.at[pl.ds(0, hw), block_cols(t)], gw_hbm.at[rows], w_s.at[t], w_r.at[t], t).wait_recv()
        rows = pl.ds(pl.multiple_of(q_rows + (t % 2) * kv_w + (t // 2) * hd, hd), hd)
        remote(dwt.at[pl.ds(hw, hd), block_cols(t)], gw_hbm.at[rows], wk_s.at[t], wk_r.at[t], t).wait_recv()
    for item in (w_own, wk_own, store_wo, store_gx, store_gg):
        item.wait()


def solution(mesh):
    n_dev = mesh.shape['cp']

    def device_step(x_act, d_out, positions, ln_gain, ln_bias, w_query, w_key, w_value, w_out):
        tok, width = x_act.shape[1], x_act.shape[2]
        q_heads, hd = w_query.shape[1], w_query.shape[2]
        kv_heads = w_key.shape[1]
        q_w, kv_w = q_heads * hd, kv_heads * hd
        n_rows = q_w + 2 * kv_w
        seq = n_dev * tok
        hw = 2 * hd

        def flat_weight(w):
            return jnp.transpose(w, (1, 2, 0)).reshape(-1, width)

        hbm = pl.BlockSpec(memory_space=pltpu.HBM)
        vmem = pl.BlockSpec(memory_space=pltpu.VMEM)
        dma = pltpu.SemaphoreType.DMA
        scratch = [
            pltpu.VMEM((n_dev, tok, width), BF),
            pltpu.VMEM((n_dev, tok, width), BF),
            pltpu.VMEM((n_rows, width), BF),
            pltpu.VMEM((2 * hw, width), BF),
            pltpu.VMEM((width, 2 * hw), BF),
            pltpu.VMEM((hw, width), BF),
            pltpu.VMEM((width, hw), BF),
            pltpu.VMEM((n_dev, 1, tok), jnp.int32),
            pltpu.VMEM((n_dev, hd // 2, tok), F32),
            pltpu.VMEM((n_dev, hd, 2 * tok), BF),
            pltpu.VMEM((hw, seq), BF),
            pltpu.VMEM((seq, hw), BF),
            pltpu.VMEM((hw, 4 * tok), BF),
            pltpu.VMEM((4 * tok, hw), BF),
            pltpu.VMEM((seq, 2 * tok), F32),
            pltpu.VMEM((seq, 2 * tok), F32),
            pltpu.VMEM((2 * tok, 4 * tok), BF),
            pltpu.VMEM((seq, hw), F32),
            pltpu.VMEM((hw, seq), F32),
            pltpu.VMEM((hd, seq), F32),
            pltpu.VMEM((n_dev, hd, tok), BF),
            pltpu.VMEM((hw, width), F32),
            pltpu.VMEM((hw + hd, width), F32),
            pltpu.VMEM((n_dev, hw, tok), BF),
            pltpu.VMEM((n_dev, hw, tok), BF),
            pltpu.VMEM((q_w, tok), BF),
            pltpu.VMEM((n_rows, tok), BF),
            pltpu.VMEM((tok, q_w), BF),
            pltpu.VMEM((tok, n_rows), BF),
            pltpu.VMEM((tok, width), BF),
            pltpu.VMEM((tok, width), BF),
            pltpu.VMEM((tok, width), F32),
            pltpu.VMEM((tok, 128), F32),
            pltpu.VMEM((tok, width), F32),
            pltpu.VMEM((tok, width), BF),
            pltpu.VMEM((2, width), F32),
            pltpu.VMEM((n_dev, 2, width), F32),
            pltpu.VMEM((2, width), F32),
            dma((7,)), dma((n_dev,)), dma((3,)), dma((4,)), dma((2,)),
            dma((16,)), dma((14,)), dma((16,)), dma((16,)),
            dma((16,)), dma((14,)), dma((16,)), dma((16,)),
            dma((n_dev,)), dma((n_dev,)),
            dma((n_dev,)), dma((n_dev,)),
            dma((n_dev,)), dma((n_dev,)),
            dma, dma,
            dma((n_dev,)), dma((n_dev,)),
            dma((n_dev,)), dma((n_dev,)),
            dma((n_dev,)), dma((n_dev,)),
            dma((n_dev,)), dma((n_dev,)),
        ]
        out, gx, gw, gwo, gg = pl.pallas_call(
            functools.partial(block_kernel, n_dev, hd, kv_w),
            out_shape=(
                jax.ShapeDtypeStruct((tok, width), BF),
                jax.ShapeDtypeStruct((tok, width), BF),
                jax.ShapeDtypeStruct((n_rows, tok), F32),
                jax.ShapeDtypeStruct((hw, width), F32),
                jax.ShapeDtypeStruct((2, width), F32),
            ),
            in_specs=[hbm, hbm, vmem, vmem, vmem, hbm, hbm, hbm, hbm],
            out_specs=(hbm,) * 5,
            scratch_shapes=scratch,
            compiler_params=pltpu.CompilerParams(collective_id=0, has_side_effects=True, vmem_limit_bytes=67043328),
            name='attn_block',
        )(
            x_act.reshape(tok, width), d_out.reshape(tok, width), positions.reshape(1, tok),
            ln_gain.reshape(1, width), ln_bias.reshape(1, width),
            flat_weight(w_query), flat_weight(w_key), flat_weight(w_value), w_out,
        )

        def rows_out(block, heads):
            return jnp.transpose(block.reshape(heads, hd, tok), (2, 0, 1))

        return (
            out.reshape(1, tok, width), gx.reshape(1, tok, width),
            rows_out(gw[0:q_w], q_heads), rows_out(gw[q_w:q_w + kv_w], kv_heads), rows_out(gw[q_w + kv_w:], kv_heads),
            gwo, gg[0], gg[1],
        )

    return jax.shard_map(device_step, mesh=mesh, in_specs=(P('dp', 'cp', None), P('dp', 'cp', None), P('dp', 'cp'), P(None), P(None), P(None, None, None), P(None, None, None), P(None, None, None), P(None, None)), out_specs=(P('dp', 'cp', None), P('dp', 'cp', None), P(('dp', 'cp'), None, None), P(('dp', 'cp'), None, None), P(('dp', 'cp'), None, None), P(('dp', 'cp'), None), P('dp'), P('dp')), check_vma=False)
```

time: 703 us -> 194 us (0.28)
  waiting for transfers between devices: 408 us -> 0 us
  Pallas kernels: 0 us -> 184 us
  matrix products: 180 us -> 0 us
  blocking collectives: 45 us -> 0 us
  other arithmetic: 41.2 us -> 0 us
  between operations: 14.7 us -> 0.66 us
    reduce_scatter x6 -> x0, waiting for transfers between devices: 329 us -> none  [the longest x4 235 us: reduce_rows(): return lax.psum_scatter(values, 'cp', scatter_dimension=0, tiled=True)]
    pallas_call x0 -> x1, Pallas kernels: none -> 184 us  [device_step(): pl.pallas_call(functools.partial(block_kernel, n_dev, hd, kv_w), out_shap...]
    dot_general x13 -> x0, matrix products: 156 us -> none  [the longest x2 42.4 us: tile_probs(): jnp.einsum('bqkgd,blkd->bkgql', q_tile, key_all, preferred_element_type=j...]
    all_gather x3 -> x0, waiting for transfers between devices: 79.4 us -> none  [the longest x1 37.4 us: device_step(): lax.all_gather(jnp.stack([k_act, v_act]), 'cp', axis=2, tiled=True)]
    psum x1 -> x0, blocking collectives: 45 us -> none  [device_step(): grad_gain = lax.psum(jnp.sum(grad_h * x_hat, axis=(0, 1)), 'cp')]
    another operation x5 -> x0, other arithmetic: 30.2 us -> none
    unnamed x6 -> x0, matrix products: 24.5 us -> none
  transfers between devices with their start and end apart: 9 -> 0, of which waited for: 8 -> 0; matrix products, arithmetic and copies ran while one was open for 15% -> 0% of each run, Pallas kernels for 0% -> 0%
where the time goes in v1:
time: 194 us; the launch traced here: 193 us
  Pallas kernels  184 us (95%)
  local copies, waits for them, and re-layouts  8.24 us (4%)
    pallas_call x1, Pallas kernels, device_step(): pl.pallas_call(functools.partial(block_kernel, n_dev, hd, kv_w), out_shap...  184 us

profile of v1, /device:TPU:21, one launch (start us, length us, event | category | flops | bytes accessed | tf_op | source)
XLA Modules:
  0.0 193.3 jit_solution(5677233093712141129)
XLA Ops:
  0.6 184.4 %attn_block.1 = (bf16[128,2048]{1,0:T(8,128)(2,1)}, bf16[128,2048]{1,0:T(8,128)(2,1)}, f32[3072,128]{1,0:T(8,128)}, f32[128,2048]{1,0:T(8,128)}, f32[2,2048]{1,0:T(2,128)}) custom-call(bf16[128,2048]{1,0:T(8,128)(2,1)} %bitcast.30, bf16[128,2048]{1,0:T(8,128)(2,1)} %bitcast.31, s32[1,128]{1,0:T(1,128)} %pos_ref.1, f32[1,2048]{1,0:T(1,128)} %bitcast.36, ...), custom_call_target="tpu_custom_call" | custom-call | tf_op jit(solution)/shard_map/attn_block/pallas_call | solution.py:508
  185.1 0.0 copy-start.2
  185.1 1.4 fusion.1
  186.5 0.0 copy-start.1
  186.5 1.9 fusion
  188.4 0.0 copy-start
  188.4 2.4 %slice.15 = f32[2048,128]{1,0:T(8,128)} slice(f32[3072,128]{1,0:T(8,128)} %get-tuple-element.15), slice={[0:2048], [0:128]} | slice | bytes 2097152 | tf_op jit(solution)/shard_map/slice | solution.py:533
  190.8 0.0 copy-done.2
  190.8 0.8 copy.20
  191.6 0.0 copy-done.1
  191.6 0.8 copy.21
  192.4 0.0 copy-done
  192.4 1.0 copy.22
Async XLA Ops:
  185.1 5.7 %copy-start.2 = (bf16[128,2048]{1,0:T(8,128)(2,1)S(1)}, bf16[128,2048]{1,0:T(8,128)(2,1)}, u32[]{:S(2)}) copy-start(bf16[128,2048]{1,0:T(8,128)(2,1)} %get-tuple-element.13) | copy-start | bytes 1572868
  186.5 5.1 %copy-start.1 = (bf16[128,2048]{1,0:T(8,128)(2,1)S(1)}, bf16[128,2048]{1,0:T(8,128)(2,1)}, u32[]{:S(2)}) copy-start(bf16[128,2048]{1,0:T(8,128)(2,1)} %get-tuple-element.14) | copy-start | bytes 1572868
  188.4 3.9 %copy-start = (f32[128,2048]{1,0:T(8,128)S(1)}, f32[128,2048]{1,0:T(8,128)}, u32[]{:S(2)}) copy-start(f32[128,2048]{1,0:T(8,128)} %get-tuple-element.35) | copy-start | bytes 3145732

commit v2 on v1

v2 whole, which is shorter than its diff:
```python
import functools
import math

import jax
import jax.numpy as jnp
from jax import lax
from jax.experimental import pallas as pl
from jax.experimental.pallas import tpu as pltpu
from jax.sharding import PartitionSpec as P

EPS = 1e-5
ROPE_BASE = 10000.0
MESH = pl.DeviceIdType.MESH
BF = jnp.bfloat16
F32 = jnp.float32
EARLY = 4


def dot(lhs, rhs):
    return jnp.dot(lhs, rhs, preferred_element_type=F32)


def block_kernel(
    n_dev, hd, kv_w, early,
    x_hbm, dy_hbm, pos_ref, gain_ref, bias_ref, wq_hbm, wk_hbm, wv_hbm, wo_hbm,
    out_hbm, gx_hbm, gw_hbm, gwo_hbm, gg_hbm,
    hb, dyb, wt, wi_raw, wi, woi_raw, woi, pos_all, trig,
    qt, kvt, kv, bmat, bmat_t, sbuf, dpbuf, mbuf, adq, dkv, dkvt, kv_rv, kv_mine, kv_row,
    dwo, dwt, at_st, dqt_st, at_rv, dt_rv, a_nat, d_nat, x_v, dy_own, xhat, stat, dh, out_v, gg_st, gg_mx, gg_my, gg_rv, gg_out,
    in_sem, wo_sem, w_sem, out_sem, loc_sem,
    hzs, hzr, hds, hdr, yzs, yzr, yds, ydr,
    pos_s, pos_r, a_s, a_r, q_s, q_r, x_s, x_r, kv_s, kv_r, w_s, w_r, wk_s, wk_r, g_s, g_r,
):
    tok, width = x_v.shape
    n_chip = n_dev // 2
    half = tok // 2
    pair = 2 * tok
    me = lax.axis_index('cp')
    chip = me // 2
    core = me % 2
    right = 2 * ((chip + 1) % n_chip) + core
    left = 2 * ((chip + n_chip - 1) % n_chip) + core
    mate = 2 * chip + 1 - core
    q_rows = wq_hbm.shape[0]
    n_rows = q_rows + 2 * kv_w
    hw = 2 * hd
    quarter = hd // 4
    tile = 256

    def remote(src, dst, send, recv, target):
        return pltpu.make_async_remote_copy(src_ref=src, dst_ref=dst, send_sem=send, recv_sem=recv, device_id={'cp': target}, device_id_type=MESH)

    def local(src, dst, sem):
        return pltpu.make_async_copy(src, dst, sem)

    def part_of(i, size):
        return pl.ds(pl.multiple_of(i * size, size), size)

    load_x = local(x_hbm, x_v, in_sem.at[0])
    load_x.start()
    own_rows = part_of(me, hw)
    kv_rows = part_of(chip, hd)
    loads = [
        local(wq_hbm.at[own_rows], wi_raw.at[pl.ds(0, hw)], in_sem.at[1]),
        local(wk_hbm.at[kv_rows], wi_raw.at[pl.ds(hw, hd)], in_sem.at[2]),
        local(wv_hbm.at[kv_rows], wi_raw.at[pl.ds(hw + hd, hd)], in_sem.at[3]),
        local(wo_hbm.at[own_rows], woi_raw, in_sem.at[4]),
        local(dy_hbm, dyb.at[chip, part_of(core, tok)], in_sem.at[5]),
        local(dy_hbm, dy_own, in_sem.at[6]),
    ]
    for item in loads:
        item.start()
    barrier = pltpu.get_barrier_semaphore()
    for step in range(1, n_dev):
        pl.semaphore_signal(barrier, inc=1, device_id={'cp': (me + step) % n_dev}, device_id_type=MESH)

    load_x.wait()
    gain_one = 1.0 + gain_ref[...]
    x_f = x_v[...].astype(F32)
    centered = x_f - jnp.mean(x_f, axis=-1, keepdims=True)
    inv_std = lax.rsqrt(jnp.mean(centered * centered, axis=-1, keepdims=True) + EPS)
    x_hat = centered * inv_std
    hb[chip, part_of(core, tok), :] = (x_hat * gain_one + bias_ref[...]).astype(BF)
    xhat[...] = x_hat
    stat[...] = jnp.broadcast_to(inv_std, stat.shape)
    pos_all[me] = pos_ref[...]

    pl.semaphore_wait(barrier, n_dev - 1)

    def chunk(buf, origin, parity, part):
        return buf.at[origin, part_of(2 * parity + part, half)]

    def own_sends(buf, zs, zr, ds, dr):
        copies = []
        for part in range(2):
            piece = chunk(buf, chip, core, part)
            copies.append(remote(piece, piece, zs.at[2 * part], zr.at[2 * part], right))
            copies.append(remote(piece, piece, zs.at[2 * part + 1], zr.at[2 * part + 1], left))
            copies.append(remote(piece, piece, ds.at[14 + part], dr.at[14 + part], mate))
        return copies

    def event_place(event):
        step = event // 4 + 1
        turn = event % 4
        direction = turn % 2
        part = jnp.where(step < 4, turn // 2, turn)
        origin = jnp.where(direction == 0, chip + n_chip - step, chip + step) % n_chip
        return step, turn, direction, part, origin

    def ring_event(ring, event):
        buf, zs, zr, ds, dr = ring
        step, turn, direction, part, origin = event_place(event)
        piece = chunk(buf, origin, core, part)
        remote(piece, piece, zs.at[0], zr.at[event], right).wait_recv()
        onward = jnp.where(step < 3, event + 4, jnp.where(turn == 0, 12, 13))

        @pl.when((step < 3) | ((step == 3) & ((turn == 0) | (turn == 3))))
        def _():
            remote(piece, piece, zs.at[event + 4], zr.at[onward], jnp.where(direction == 0, right, left)).start()

        remote(piece, piece, ds.at[event], dr.at[event], mate).start()

    def ring_service(ring, event):
        @pl.when(event < 14)
        def _():
            ring_event(ring, event)

    def ring_origin(k):
        step = (k + 1) // 2
        return jnp.where(k % 2 == 1, chip + n_chip - step, chip + step) % n_chip

    def ring_mate(ring, k, origin):
        buf, zs, zr, ds, dr = ring
        step = (k + 1) // 2
        direction = (k + 1) % 2
        first = jnp.where(k == 0, 14, jnp.where(step < 4, 4 * (step - 1) + direction, 12))
        second = jnp.where(k == 0, 15, jnp.where(step < 4, 4 * (step - 1) + 2 + direction, 13))
        for part, event in ((0, first), (1, second)):
            piece = chunk(buf, origin, 1 - core, part)
            remote(piece, piece, ds.at[0], dr.at[event], mate).wait_recv()

    def finish_ring(ring):
        buf, zs, zr, ds, dr = ring
        for item in own_sends(buf, zs, zr, ds, dr):
            item.wait_send()
        for event in range(14):
            _, _, _, part, origin = event_place(event)
            piece = chunk(buf, origin, core, part)
            if event < 8 or event in (8, 11):
                remote(piece, piece, zs.at[event + 4], zr.at[event], right).wait_send()
            remote(piece, piece, ds.at[event], dr.at[event], mate).wait_send()

    h_ring = (hb, hzs, hzr, hds, hdr)
    y_ring = (dyb, yzs, yzr, yds, ydr)
    for item in own_sends(*h_ring):
        item.start()
    pos_sends = [remote(pos_all.at[me], pos_all.at[me], pos_s.at[step], pos_r.at[step], (me + step) % n_dev) for step in range(1, n_dev)]
    for item in pos_sends:
        item.start()
    weight_loads = [
        local(wq_hbm, wt.at[pl.ds(0, q_rows)], w_sem.at[0]),
        local(wk_hbm, wt.at[pl.ds(q_rows, kv_w)], w_sem.at[1]),
        local(wv_hbm, wt.at[pl.ds(q_rows + kv_w, kv_w)], w_sem.at[2]),
    ]
    for item in weight_loads:
        item.start()
    dkv[...] = jnp.zeros_like(dkv)
    dwo[...] = jnp.zeros_like(dwo)
    dwt[...] = jnp.zeros_like(dwt)
    bmat[...] = jnp.zeros_like(bmat)

    for item in loads:
        item.wait()
    for t in range(width // tok):
        cols = slice(tok * t, tok * t + tok)
        wi[cols, 0:hw] = wi_raw[0:hw, cols].T
        wi[cols, hw:2 * hw] = wi_raw[hw:2 * hw, cols].T
        woi[cols, :] = woi_raw[:, cols].T

    freq = jnp.exp(lax.broadcasted_iota(jnp.int32, (quarter, tok), 0).astype(F32) * (-2.0 * math.log(ROPE_BASE) / (hd // 2)))

    def make_trig(slot):
        angle = pos_all[slot].astype(F32) * freq
        trig[slot, 0:quarter, :] = jnp.cos(angle)
        trig[slot, quarter:2 * quarter, :] = jnp.sin(angle)

    make_trig(me)

    @pl.loop(1, n_dev)
    def _(step):
        source = (me + n_dev - step) % n_dev
        remote(pos_all.at[source], pos_all.at[source], pos_s.at[step], pos_r.at[step], me).wait_recv()
        make_trig(source)

    def turned(val, base, slot, back):
        cos_t = trig[slot, 0:quarter, :]
        sin_t = trig[slot, quarter:2 * quarter, :]
        u = val[base:base + quarter]
        w = val[base + quarter:base + 2 * quarter]
        rest = val[base + 2 * quarter:base + hd]
        if back:
            return [u * cos_t + w * sin_t, w * cos_t - u * sin_t, rest]
        return [u * cos_t - w * sin_t, w * cos_t + u * sin_t, rest]

    @pl.loop(0, n_chip)
    def _(k):
        ring_service(h_ring, 2 * k)
        ring_service(h_ring, 2 * k + 1)

        @pl.when(k == 5)
        def _():
            for item in own_sends(*y_ring):
                item.start()

        b = ring_origin(k)
        ring_mate(h_ring, k, b)
        flat = dot(hb[b], wi[...])
        for t in range(2):
            slot = 2 * b + t
            q_f = flat[tok * t:tok * t + tok, 0:hw].T
            kv_f = flat[tok * t:tok * t + tok, hw:2 * hw].T
            for head in range(2):
                qt[b, :, pair * t + tok * head:pair * t + tok * head + tok] = jnp.concatenate(turned(q_f, hd * head, slot, False), axis=0).astype(BF)
            kv_rot = jnp.concatenate(turned(kv_f, 0, slot, False) + [kv_f[hd:2 * hd]], axis=0).astype(BF)
            kvt[:, part_of(slot, tok)] = kv_rot
            kv[part_of(slot, tok), :] = kv_rot.T

    scale = hd ** -0.5
    cols_q = 2 * pair

    def send_a(slot):
        return remote(at_st.at[slot], at_rv.at[own_rows], a_s.at[slot], a_r.at[me], slot)

    @pl.loop(0, n_chip)
    def _(k):
        ring_service(y_ring, 2 * k)
        b = ring_origin(k)
        ring_mate(y_ring, k, b)
        da = dot(dyb[b], woi[...]).astype(BF)
        bmat[0:hd, 0:cols_q] = qt[b]
        for t in range(2):
            da_t = da[tok * t:tok * t + tok].T
            for head in range(2):
                lane = cols_q + pair * t + tok * head
                bmat[hd:2 * hd, lane:lane + tok] = da_t[hd * head:hd * head + hd]
        for t in range(2 * cols_q // tok):
            bmat_t[tok * t:tok * t + tok, :] = bmat[:, tok * t:tok * t + tok].T

        def both_of(c):
            rows = part_of(c, pair)
            both = dot(kv[rows, :], bmat[...])
            return rows, both[:, 0:cols_q] * scale, both[:, cols_q:2 * cols_q]

        lane = lax.broadcasted_iota(jnp.int32, (pair, cols_q), 1)
        seen = lax.broadcasted_iota(jnp.int32, (pair, cols_q), 0) <= (lane // pair) * tok + lane % tok
        rows, s, d_p = both_of(b)
        s = jnp.where(seen, s, -1e30)
        top = jnp.max(s, axis=0, keepdims=True)
        p = jnp.exp(s - top)
        sbuf[rows, :] = p
        dpbuf[rows, :] = d_p
        mbuf[b] = top

        def first_pass(c, state):
            old, total, weighted = state
            rows, s, d_p = both_of(c)
            new = jnp.maximum(old, jnp.max(s, axis=0, keepdims=True))
            p = jnp.exp(s - new)
            sbuf[rows, :] = p
            dpbuf[rows, :] = d_p
            mbuf[c] = new
            keep = jnp.exp(old - new)
            return new, total * keep + jnp.sum(p, axis=0, keepdims=True), weighted * keep + jnp.sum(p * d_p, axis=0, keepdims=True)

        top, total, weighted = lax.fori_loop(0, b, first_pass, (top, jnp.sum(p, axis=0, keepdims=True), jnp.sum(p * d_p, axis=0, keepdims=True)))
        inv = 1.0 / total
        row_dot = weighted * inv
        ring_service(y_ring, 2 * k + 1)
        adq[...] = jnp.zeros_like(adq)

        def second_pass(c, carry):
            rows = part_of(c, pair)
            p = sbuf[rows, :] * (jnp.exp(mbuf[c] - top) * inv)
            p_b = p.astype(BF)
            ds_b = (p * (dpbuf[rows, :] - row_dot) * scale).astype(BF)
            dkv[rows, :] += dot(ds_b, bmat_t[0:cols_q, :]) + dot(p_b, bmat_t[cols_q:2 * cols_q, :])
            adq[0:hd, :] += dot(kvt[0:hd, rows], ds_b)
            adq[hd:2 * hd, :] += dot(kvt[hd:2 * hd, rows], p_b)
            return carry

        lax.fori_loop(0, b + 1, second_pass, 0)
        a_pair = []
        dq_pair = []
        for t in range(2):
            slot = 2 * b + t
            lanes = [slice(pair * t + tok * head, pair * t + tok * head + tok) for head in range(2)]
            a_t = jnp.concatenate([adq[hd:2 * hd, lane] for lane in lanes], axis=0).astype(BF)
            parts = []
            for lane in lanes:
                parts += turned(adq[0:hd, lane], 0, slot, True)
            dq_t = jnp.concatenate(parts, axis=0).astype(BF)
            at_st[slot] = a_t
            dqt_st[slot] = dq_t
            a_pair.append(a_t)
            dq_pair.append(dq_t)

            @pl.when(slot == me)
            def _():
                at_rv[own_rows, :] = a_t
                dt_rv[own_rows, :] = dq_t

            @pl.when(slot != me)
            def _():
                remote(dqt_st.at[slot], dt_rv.at[own_rows], q_s.at[slot], q_r.at[me], slot).start()

            @pl.when((slot != me) & (k < early))
            def _():
                send_a(slot).start()

        a_pair = jnp.concatenate(a_pair, axis=1)
        dq_pair = jnp.concatenate(dq_pair, axis=1)
        for t in range(width // tile):
            cols = slice(tile * t, tile * t + tile)
            dwo[:, cols] += dot(a_pair, dyb[b, :, cols])
            dwt[0:hw, cols] += dot(dq_pair, hb[b, :, cols])

    for t in range(n_dev):
        dkvt[:, tok * t:tok * t + tok] = dkv[tok * t:tok * t + tok, :].T
    swap = remote(dkvt.at[part_of(1 - core, hd)], kv_rv, x_s, x_r, mate)
    swap.start()

    @pl.loop(early, n_chip)
    def _(k):
        b = ring_origin(k)
        for t in range(2):
            @pl.when(2 * b + t != me)
            def _():
                send_a(2 * b + t).start()

    store_wo = local(dwo, gwo_hbm, out_sem.at[0])
    store_wo.start()

    def order():
        steps = []
        for step in range(1, n_chip // 2 + 1):
            steps += [step, n_chip - step] if 2 * step < n_chip else [step]
        return [(chip + step) % n_chip for step in steps]

    far = order()
    targets = [mate] + [2 * c + p for c in far for p in range(2)]

    swap.wait_recv()
    mine = part_of(core, hd)
    g_rows = pl.ds(pl.multiple_of(q_rows + core * kv_w + chip * hd, hd), hd)
    for t in range(n_dev):
        cols = slice(tok * t, tok * t + tok)
        g = dkvt[mine, cols] + kv_rv[:, cols]
        cos_t = jnp.where(core == 0, trig[t, 0:quarter, :], 1.0)
        sin_t = jnp.where(core == 0, trig[t, quarter:2 * quarter, :], 0.0)
        u = g[0:quarter]
        w = g[quarter:2 * quarter]
        g_b = jnp.concatenate([u * cos_t + w * sin_t, w * cos_t - u * sin_t, g[2 * quarter:hd]], axis=0).astype(BF)
        kv_mine[t] = g_b
        kv_row[:, cols] = g_b
    dt_rv[g_rows, :] = kv_mine[me]
    kv_sends = [remote(kv_mine.at[t], dt_rv.at[g_rows], kv_s.at[t], kv_r.at[me], t) for t in targets]
    w_sends = [remote(dwt.at[pl.ds(0, hw), part_of(t, tok)], gw_hbm.at[own_rows], w_s.at[t], w_r.at[me], t) for t in targets]
    wk_sends = [remote(dwt.at[pl.ds(hw, hd), part_of(t, tok)], gw_hbm.at[g_rows], wk_s.at[t], wk_r.at[me], t) for t in targets]
    for item in kv_sends + w_sends:
        item.start()
    w_own = local(dwt.at[pl.ds(0, hw), part_of(me, tok)], gw_hbm.at[own_rows], loc_sem.at[0])
    w_own.start()

    for t in range(width // tile):
        cols = slice(tile * t, tile * t + tile)
        acc = jnp.zeros((hd, tile), F32)
        for s in range(n_chip):
            acc += dot(kv_row[:, pair * s:pair * s + pair], hb[s, :, cols])
        dwt[hw:hw + hd, cols] = acc
    wk_own = local(dwt.at[pl.ds(hw, hd), part_of(me, tok)], gw_hbm.at[g_rows], loc_sem.at[1])
    wk_own.start()

    finish_ring(y_ring)
    wo_loads = [local(wo_hbm.at[pl.ds(pair * t, pair)], dyb.at[t], wo_sem.at[t]) for t in range(n_chip)]
    for item in wo_loads:
        item.start()

    for t in targets:
        remote(at_st.at[0], at_rv.at[part_of(t, hw)], a_s.at[t], a_r.at[t], t).wait_recv()
    for t in range(q_rows // tok):
        a_nat[:, tok * t:tok * t + tok] = at_rv[tok * t:tok * t + tok, :].T
    for item in wo_loads:
        item.wait()
    for t in range(width // tile):
        cols = slice(tile * t, tile * t + tile)
        prod = jnp.zeros((tok, tile), F32)
        for s in range(n_chip):
            prod += dot(a_nat[:, pair * s:pair * s + pair], dyb[s, :, cols])
        out_v[:, cols] = (x_v[:, cols].astype(F32) + prod).astype(BF)
    store_out = local(out_v, out_hbm, out_sem.at[1])
    store_out.start()

    for item in weight_loads:
        item.wait()

    def kv_place(t):
        return pl.ds(pl.multiple_of(q_rows + (t % 2) * kv_w + (t // 2) * hd, hd), hd)

    for t in targets:
        remote(dqt_st.at[0], dt_rv.at[part_of(t, hw)], q_s.at[t], q_r.at[t], t).wait_recv()
        remote(kv_mine.at[0], dt_rv.at[kv_place(t)], kv_s.at[t], kv_r.at[t], t).wait_recv()
    for t in range(n_rows // tok):
        d_nat[:, tok * t:tok * t + tok] = dt_rv[tok * t:tok * t + tok, :].T

    for t in range(width // tile):
        cols = slice(tile * t, tile * t + tile)
        acc = jnp.zeros((tok, tile), F32)
        for s in range(n_rows // tile):
            acc += dot(d_nat[:, tile * s:tile * s + tile], wt[tile * s:tile * s + tile, cols])
        dh[:, cols] = acc
        gg_st[0, :, cols] = jnp.sum(acc * xhat[:, cols], axis=0, keepdims=True)
        gg_st[1, :, cols] = jnp.sum(acc, axis=0, keepdims=True)
    g_swap = remote(gg_st.at[1 - core], gg_mx, g_s.at[n_chip], g_r.at[n_chip], mate)
    g_swap.start()
    g_swap.wait_recv()
    gg_my[...] = jnp.where(core == 0, gg_st[0], gg_st[1]) + gg_mx[...]
    gg_rv[chip] = gg_my[...]
    g_sends = [remote(gg_my, gg_rv.at[chip], g_s.at[c], g_r.at[chip], 2 * c + core) for c in far]
    for item in g_sends + wk_sends:
        item.start()

    grad_hat = dh[...] * gain_one
    x_hat = xhat[...]
    mean_one = jnp.mean(grad_hat, axis=-1, keepdims=True)
    mean_two = jnp.mean(grad_hat * x_hat, axis=-1, keepdims=True)
    store_out.wait()
    out_v[...] = (dy_own[...].astype(F32) + stat[:, 0:1] * (grad_hat - mean_one - x_hat * mean_two)).astype(BF)
    store_gx = local(out_v, gx_hbm, out_sem.at[2])
    store_gx.start()

    for c in far:
        remote(gg_my, gg_rv.at[c], g_s.at[c], g_r.at[c], 2 * c + core).wait_recv()
    sums = gg_rv[0]
    for c in range(1, n_chip):
        sums = sums + gg_rv[c]
    gg_out[core] = sums
    g_swap_out = remote(gg_out.at[core], gg_out.at[core], g_s.at[n_chip + 1], g_r.at[n_chip + 1], mate)
    g_swap_out.start()
    remote(gg_out.at[core], gg_out.at[1 - core], g_s.at[n_chip + 1], g_r.at[n_chip + 1], mate).wait_recv()
    store_gg = local(gg_out, gg_hbm, out_sem.at[3])
    store_gg.start()

    finish_ring(h_ring)
    for item in pos_sends + [swap, g_swap, g_swap_out]:
        item.wait_send()
    for t in targets:
        remote(at_st.at[0], at_rv.at[pl.ds(0, hw)], a_s.at[t], a_r.at[t], t).wait_send()
        remote(dqt_st.at[0], dt_rv.at[pl.ds(0, hw)], q_s.at[t], q_r.at[t], t).wait_send()
    for item in kv_sends + w_sends + g_sends + wk_sends:
        item.wait_send()
    for t in targets:
        remote(dwt.at[pl.ds(0, hw), part_of(t, tok)], gw_hbm.at[part_of(t, hw)], w_s.at[t], w_r.at[t], t).wait_recv()
        remote(dwt.at[pl.ds(hw, hd), part_of(t, tok)], gw_hbm.at[kv_place(t)], wk_s.at[t], wk_r.at[t], t).wait_recv()
    for item in (w_own, wk_own, store_wo, store_gx, store_gg):
        item.wait()


def settle_kernel(q_rows, kv_w, out_i, gx_i, gw_i, gwo_i, gg_i, out_o, gx_o, gq_o, gk_o, gv_o, gwo_o, gain_o, bias_o, b_act, b_q, b_kv, b_o, b_gg, sem_in, sem_out, sem_gg):
    half_q = q_rows // 2
    half_o = gwo_i.shape[0] // 2
    moves = [(out_i, b_act.at[0], out_o), (gx_i, b_act.at[1], gx_o)]
    for t in range(2):
        moves.append((gw_i.at[pl.ds(half_q * t, half_q)], b_q.at[t], gq_o.at[pl.ds(half_q * t, half_q)]))
        moves.append((gwo_i.at[pl.ds(half_o * t, half_o)], b_o.at[t], gwo_o.at[pl.ds(half_o * t, half_o)]))
    moves.append((gw_i.at[pl.ds(q_rows, kv_w)], b_kv.at[0], gk_o))
    moves.append((gw_i.at[pl.ds(q_rows + kv_w, kv_w)], b_kv.at[1], gv_o))
    loads = [pltpu.make_async_copy(src, mid, sem_in.at[i]) for i, (src, mid, _) in enumerate(moves)]
    stores = [pltpu.make_async_copy(mid, dst, sem_out.at[i]) for i, (_, mid, dst) in enumerate(moves)]
    load_gg = pltpu.make_async_copy(gg_i, b_gg, sem_gg)
    load_gg.start()
    for item in loads:
        item.start()
    for load, store in zip(loads, stores):
        load.wait()
        store.start()
    load_gg.wait()
    gain_o[...] = b_gg[0, 0]
    bias_o[...] = b_gg[1, 0]
    for item in stores:
        item.wait()


def solution(mesh):
    n_dev = mesh.shape['cp']

    def device_step(x_act, d_out, positions, ln_gain, ln_bias, w_query, w_key, w_value, w_out):
        tok, width = x_act.shape[1], x_act.shape[2]
        q_heads, hd = w_query.shape[1], w_query.shape[2]
        kv_heads = w_key.shape[1]
        q_w, kv_w = q_heads * hd, kv_heads * hd
        n_rows = q_w + 2 * kv_w
        seq = n_dev * tok
        hw = 2 * hd

        def flat_weight(w):
            return jnp.transpose(w, (1, 2, 0)).reshape(-1, width)

        hbm = pl.BlockSpec(memory_space=pltpu.HBM)
        vmem = pl.BlockSpec(memory_space=pltpu.VMEM)
        dma = pltpu.SemaphoreType.DMA
        scratch = [
            pltpu.VMEM((n_dev // 2, 2 * tok, width), BF),
            pltpu.VMEM((n_dev // 2, 2 * tok, width), BF),
            pltpu.VMEM((n_rows, width), BF),
            pltpu.VMEM((2 * hw, width), BF),
            pltpu.VMEM((width, 2 * hw), BF),
            pltpu.VMEM((hw, width), BF),
            pltpu.VMEM((width, hw), BF),
            pltpu.VMEM((n_dev, 1, tok), jnp.int32),
            pltpu.VMEM((n_dev, hd // 2, tok), F32),
            pltpu.VMEM((n_dev // 2, hd, 4 * tok), BF),
            pltpu.VMEM((hw, seq), BF),
            pltpu.VMEM((seq, hw), BF),
            pltpu.VMEM((hw, 8 * tok), BF),
            pltpu.VMEM((8 * tok, hw), BF),
            pltpu.VMEM((seq, 4 * tok), F32),
            pltpu.VMEM((seq, 4 * tok), F32),
            pltpu.VMEM((n_dev // 2, 1, 4 * tok), F32),
            pltpu.VMEM((hw, 4 * tok), F32),
            pltpu.VMEM((seq, hw), F32),
            pltpu.VMEM((hw, seq), F32),
            pltpu.VMEM((hd, seq), F32),
            pltpu.VMEM((n_dev, hd, tok), BF),
            pltpu.VMEM((hd, seq), BF),
            pltpu.VMEM((hw, width), F32),
            pltpu.VMEM((hw + hd, width), F32),
            pltpu.VMEM((n_dev, hw, tok), BF),
            pltpu.VMEM((n_dev, hw, tok), BF),
            pltpu.VMEM((q_w, tok), BF),
            pltpu.VMEM((n_rows, tok), BF),
            pltpu.VMEM((tok, q_w), BF),
            pltpu.VMEM((tok, n_rows), BF),
            pltpu.VMEM((tok, width), BF),
            pltpu.VMEM((tok, width), BF),
            pltpu.VMEM((tok, width), F32),
            pltpu.VMEM((tok, 128), F32),
            pltpu.VMEM((tok, width), F32),
            pltpu.VMEM((tok, width), BF),
            pltpu.VMEM((2, 1, width), F32),
            pltpu.VMEM((1, width), F32),
            pltpu.VMEM((1, width), F32),
            pltpu.VMEM((n_dev // 2, 1, width), F32),
            pltpu.VMEM((2, 1, width), F32),
            dma((7,)), dma((n_dev,)), dma((3,)), dma((4,)), dma((2,)),
            dma((16,)), dma((14,)), dma((16,)), dma((16,)),
            dma((16,)), dma((14,)), dma((16,)), dma((16,)),
            dma((n_dev,)), dma((n_dev,)),
            dma((n_dev,)), dma((n_dev,)),
            dma((n_dev,)), dma((n_dev,)),
            dma, dma,
            dma((n_dev,)), dma((n_dev,)),
            dma((n_dev,)), dma((n_dev,)),
            dma((n_dev,)), dma((n_dev,)),
            dma((n_dev,)), dma((n_dev,)),
        ]
        out, gx, gw, gwo, gg = pl.pallas_call(
            functools.partial(block_kernel, n_dev, hd, kv_w, EARLY),
            out_shape=(
                jax.ShapeDtypeStruct((tok, width), BF),
                jax.ShapeDtypeStruct((tok, width), BF),
                jax.ShapeDtypeStruct((n_rows, tok), F32),
                jax.ShapeDtypeStruct((hw, width), F32),
                jax.ShapeDtypeStruct((2, 1, width), F32),
            ),
            in_specs=[hbm, hbm, vmem, vmem, vmem, hbm, hbm, hbm, hbm],
            out_specs=(hbm,) * 5,
            scratch_shapes=scratch,
            compiler_params=pltpu.CompilerParams(collective_id=0, has_side_effects=True, vmem_limit_bytes=67043328),
            name='attn_block',
        )(
            x_act.reshape(tok, width), d_out.reshape(tok, width), positions.reshape(1, tok),
            ln_gain.reshape(1, width), ln_bias.reshape(1, width),
            flat_weight(w_query), flat_weight(w_key), flat_weight(w_value), w_out,
        )

        out, gx, gq, gk, gv, gwo, gain, bias = pl.pallas_call(
            functools.partial(settle_kernel, q_w, kv_w),
            out_shape=(
                jax.ShapeDtypeStruct((tok, width), BF),
                jax.ShapeDtypeStruct((tok, width), BF),
                jax.ShapeDtypeStruct((q_w, tok), F32),
                jax.ShapeDtypeStruct((kv_w, tok), F32),
                jax.ShapeDtypeStruct((kv_w, tok), F32),
                jax.ShapeDtypeStruct((hw, width), F32),
                jax.ShapeDtypeStruct((width,), F32),
                jax.ShapeDtypeStruct((width,), F32),
            ),
            in_specs=[hbm] * 5,
            out_specs=(hbm,) * 6 + (vmem,) * 2,
            scratch_shapes=[
                pltpu.VMEM((2, tok, width), BF),
                pltpu.VMEM((2, q_w // 2, tok), F32),
                pltpu.VMEM((2, kv_w, tok), F32),
                pltpu.VMEM((2, hw // 2, width), F32),
                pltpu.VMEM((2, 1, width), F32),
                dma((8,)), dma((8,)), dma,
            ],
            name='settle',
        )(out, gx, gw, gwo, gg)

        def rows_out(block, heads):
            return jnp.transpose(block.reshape(heads, hd, tok), (2, 0, 1))

        return (
            out.reshape(1, tok, width), gx.reshape(1, tok, width),
            rows_out(gq, q_heads), rows_out(gk, kv_heads), rows_out(gv, kv_heads),
            gwo, gain, bias,
        )

    return jax.shard_map(device_step, mesh=mesh, in_specs=(P('dp', 'cp', None), P('dp', 'cp', None), P('dp', 'cp'), P(None), P(None), P(None, None, None), P(None, None, None), P(None, None, None), P(None, None)), out_specs=(P('dp', 'cp', None), P('dp', 'cp', None), P(('dp', 'cp'), None, None), P(('dp', 'cp'), None, None), P(('dp', 'cp'), None, None), P(('dp', 'cp'), None), P('dp'), P('dp')), check_vma=False)
```

time: 194 us -> 178 us (0.918)
  Pallas kernels: 184 us -> 175 us
  local copies, waits for them, and re-layouts: 8.24 us -> 0 us
    pallas_call x1 -> x2, Pallas kernels: 184 us -> 175 us  [the longest x1 172 us: device_step(): pl.pallas_call(functools.partial(block_kernel, n_dev, hd, kv_w, EARLY), o...]
    slice x3 -> x0, local copies, waits for them, and re-layouts: 5.67 us -> none  [the longest x1 2.35 us: device_step(): gw[0:q_w]]
    unnamed x9 -> x0, local copies, waits for them, and re-layouts: 2.57 us -> none
where the time goes in v2:
time: 178 us; the launch traced here: 176 us
  Pallas kernels  175 us (98%)
    pallas_call x1, Pallas kernels, device_step(): pl.pallas_call(functools.partial(block_kernel, n_dev, hd, kv_w, EARLY), o...  172 us
    pallas_call x1, Pallas kernels, device_step(): pl.pallas_call(functools.partial(settle_kernel, q_w, kv_w), out_shape=(ja...  3.62 us

profile of v2, /device:TPU:21, one launch (start us, length us, event | category | flops | bytes accessed | tf_op | source)
XLA Modules:
  0.0 176.0 jit_solution(16861217833201770071)
XLA Ops:
  0.6 171.8 %attn_block.1 = (bf16[128,2048]{1,0:T(8,128)(2,1)}, bf16[128,2048]{1,0:T(8,128)(2,1)}, f32[3072,128]{1,0:T(8,128)}, f32[128,2048]{1,0:T(8,128)}, f32[2,1,2048]{2,1,0:T(1,128)}) custom-call(bf16[128,2048]{1,0:T(8,128)(2,1)} %bitcast.27, bf16[128,2048]{1,0:T(8,128)(2,1)} %bitcast.28, s32[1,128]{1,0:T(1,128)} %pos_ref.1, f32[1,2048]{1,0:T(1,128)} %bitcast.29, ...), custom_call_target="tpu_custom_call" | custom-call | tf_op jit(solution)/shard_map/attn_block/pallas_call | solution.py:566
  172.4 3.6 %settle.1 = (bf16[128,2048]{1,0:T(8,128)(2,1)}, bf16[128,2048]{1,0:T(8,128)(2,1)}, f32[2048,128]{1,0:T(8,128)}, f32[512,128]{1,0:T(8,128)}, f32[512,128]{1,0:T(8...) custom-call(bf16[128,2048]{1,0:T(8,128)(2,1)} %get-tuple-element.21.out_i, ...), custom_call_target="tpu_custom_call" | custom-call | tf_op jit(solution)/shard_map/settle/pallas_call | solution.py:586

commit v3 on v2

v3 whole, which is shorter than its diff:
```python
import functools
import math

import jax
import jax.numpy as jnp
from jax import lax
from jax.experimental import pallas as pl
from jax.experimental.pallas import tpu as pltpu
from jax.sharding import PartitionSpec as P

EPS = 1e-5
ROPE_BASE = 10000.0
MESH = pl.DeviceIdType.MESH
BF = jnp.bfloat16
F32 = jnp.float32
NEAR = 1


def dot(lhs, rhs):
    return jnp.dot(lhs, rhs, preferred_element_type=F32)


def dot_t(lhs, rhs):
    return lax.dot_general(lhs, rhs, (((1,), (1,)), ((), ())), preferred_element_type=F32)


def block_kernel(
    n_dev, hd, kv_w, near,
    x_hbm, dy_hbm, pos_hbm, gain_hbm, bias_hbm, wq_hbm, wk_hbm, wv_hbm, wo_hbm,
    out_hbm, gx_hbm, gw_hbm, gwo_hbm, gg_hbm,
    hb, dyb, wt, wi, woi, w_far, pos_all, trig,
    qt, kvt, kv, kvt_far, kv_far, bmat, bmat_t, sbuf, dpbuf, mbuf, adq, dkv, dkvt, kv_rv, kv_mine, kv_row,
    dwo, dwt, at_st, dqt_st, at_rv, dt_rv, a_nat, d_nat, x_v, dy_own, gb_v, stat, out_v, gg_st, gg_mx, gg_my, gg_rv, gg_out,
    in_sem, far_sem, wo_sem, w_sem, out_sem, loc_sem,
    hzs, hzr, hds, hdr, yzs, yzr, yds, ydr,
    pos_s, pos_r, a_s, a_r, q_s, q_r, x_s, x_r, kv_s, kv_r, w_s, w_r, wk_s, wk_r, g_s, g_r,
):
    tok, width = x_v.shape
    n_chip = n_dev // 2
    half = tok // 2
    pair = 2 * tok
    me = lax.axis_index('cp')
    chip = me // 2
    core = me % 2
    right = 2 * ((chip + 1) % n_chip) + core
    left = 2 * ((chip + n_chip - 1) % n_chip) + core
    mate = 2 * chip + 1 - core
    q_rows = wq_hbm.shape[0]
    n_rows = q_rows + 2 * kv_w
    hw = 2 * hd
    quarter = hd // 4
    tile = 256
    scale = hd ** -0.5
    cols_q = 2 * pair
    n_far = n_chip - 1 - 2 * near

    def remote(src, dst, send, recv, target):
        return pltpu.make_async_remote_copy(src_ref=src, dst_ref=dst, send_sem=send, recv_sem=recv, device_id={'cp': target}, device_id_type=MESH)

    def local(src, dst, sem):
        return pltpu.make_async_copy(src, dst, sem)

    def part_of(i, size):
        return pl.ds(pl.multiple_of(i * size, size), size)

    def ring_steps(k):
        step = (k + 1) // 2
        return step, k % 2

    def ring_origin(k):
        step, ahead = ring_steps(k)
        return jnp.where(ahead == 1, chip + n_chip - step, chip + step) % n_chip

    own = (chip, part_of(core, tok))
    first_loads = [
        local(x_hbm, x_v, in_sem.at[0]),
        local(gain_hbm, gb_v.at[0], in_sem.at[1]),
        local(bias_hbm, gb_v.at[1], in_sem.at[2]),
        local(pos_hbm, pos_all.at[me], in_sem.at[3]),
    ]
    for item in first_loads:
        item.start()
    barrier = pltpu.get_barrier_semaphore()
    for step in range(1, n_dev):
        pl.semaphore_signal(barrier, inc=1, device_id={'cp': (me + step) % n_dev}, device_id_type=MESH)
    own_rows = part_of(me, hw)
    kv_rows = part_of(chip, hd)
    loads = [
        local(wq_hbm.at[own_rows], wi.at[pl.ds(0, hw)], in_sem.at[4]),
        local(wk_hbm.at[kv_rows], wi.at[pl.ds(hw, hd)], in_sem.at[5]),
        local(wv_hbm.at[kv_rows], wi.at[pl.ds(hw + hd, hd)], in_sem.at[6]),
        local(wo_hbm.at[own_rows], woi, in_sem.at[7]),
        local(dy_hbm, dyb.at[own], in_sem.at[8]),
        local(dy_hbm, dy_own, in_sem.at[9]),
    ]
    for f in range(n_far):
        far_rows = part_of(ring_origin(2 * near + 1 + f), hd)
        loads.append(local(wk_hbm.at[far_rows], w_far.at[pl.ds(hw * f, hd)], far_sem.at[2 * f]))
        loads.append(local(wv_hbm.at[far_rows], w_far.at[pl.ds(hw * f + hd, hd)], far_sem.at[2 * f + 1]))
    for item in loads:
        item.start()

    for item in first_loads:
        item.wait()
    gain_one = 1.0 + gb_v[0]
    x_f = x_v[...].astype(F32)
    mean = jnp.mean(x_f, axis=-1, keepdims=True)
    centered = x_f - mean
    inv_std = lax.rsqrt(jnp.mean(centered * centered, axis=-1, keepdims=True) + EPS)
    hb[chip, part_of(core, tok), :] = (centered * inv_std * gain_one + gb_v[1]).astype(BF)
    stat[0] = jnp.broadcast_to(mean, (tok, 128))
    stat[1] = jnp.broadcast_to(inv_std, (tok, 128))

    pl.semaphore_wait(barrier, n_dev - 1)

    def chunk(buf, origin, parity, part):
        return buf.at[origin, part_of(2 * parity + part, half)]

    def own_sends(buf, zs, zr, ds, dr):
        copies = []
        for part in range(2):
            piece = chunk(buf, chip, core, part)
            copies.append(remote(piece, piece, zs.at[2 * part], zr.at[2 * part], right))
            copies.append(remote(piece, piece, zs.at[2 * part + 1], zr.at[2 * part + 1], left))
            copies.append(remote(piece, piece, ds.at[14 + part], dr.at[14 + part], mate))
        return copies

    def event_place(event):
        step = event // 4 + 1
        turn = event % 4
        direction = turn % 2
        part = jnp.where(step < 4, turn // 2, turn)
        origin = jnp.where(direction == 0, chip + n_chip - step, chip + step) % n_chip
        return step, turn, direction, part, origin

    def ring_event(ring, event):
        buf, zs, zr, ds, dr = ring
        step, turn, direction, part, origin = event_place(event)
        piece = chunk(buf, origin, core, part)
        remote(piece, piece, zs.at[0], zr.at[event], right).wait_recv()
        onward = jnp.where(step < 3, event + 4, jnp.where(turn == 0, 12, 13))

        @pl.when((step < 3) | ((step == 3) & ((turn == 0) | (turn == 3))))
        def _():
            remote(piece, piece, zs.at[event + 4], zr.at[onward], jnp.where(direction == 0, right, left)).start()

        remote(piece, piece, ds.at[event], dr.at[event], mate).start()

    def ring_service(ring, event):
        @pl.when(event < 14)
        def _():
            ring_event(ring, event)

    def ring_mate(ring, k, origin):
        buf, zs, zr, ds, dr = ring
        step, ahead = ring_steps(k)
        first = jnp.where(k == 0, 14, jnp.where(step < 4, 4 * (step - 1) + 1 - ahead, 12))
        second = jnp.where(k == 0, 15, jnp.where(step < 4, 4 * (step - 1) + 3 - ahead, 13))
        for part, event in ((0, first), (1, second)):
            piece = chunk(buf, origin, 1 - core, part)
            remote(piece, piece, ds.at[0], dr.at[event], mate).wait_recv()

    def finish_ring(ring):
        buf, zs, zr, ds, dr = ring
        for item in own_sends(*ring):
            item.wait_send()
        for event in range(14):
            _, _, _, part, origin = event_place(event)
            piece = chunk(buf, origin, core, part)
            if event < 8 or event in (8, 11):
                remote(piece, piece, zs.at[event + 4], zr.at[event], right).wait_send()
            remote(piece, piece, ds.at[event], dr.at[event], mate).wait_send()

    h_ring = (hb, hzs, hzr, hds, hdr)
    y_ring = (dyb, yzs, yzr, yds, ydr)
    for item in own_sends(*h_ring):
        item.start()
    pos_sends = [remote(pos_all.at[me], pos_all.at[me], pos_s.at[step], pos_r.at[step], (me + step) % n_dev) for step in range(1, n_dev)]
    for item in pos_sends:
        item.start()
    weight_loads = [
        local(wq_hbm, wt.at[pl.ds(0, q_rows)], w_sem.at[0]),
        local(wk_hbm, wt.at[pl.ds(q_rows, kv_w)], w_sem.at[1]),
        local(wv_hbm, wt.at[pl.ds(q_rows + kv_w, kv_w)], w_sem.at[2]),
    ]
    for item in weight_loads:
        item.start()
    dkv[...] = jnp.zeros_like(dkv)
    dwo[...] = jnp.zeros_like(dwo)
    dwt[...] = jnp.zeros_like(dwt)
    bmat[...] = jnp.zeros_like(bmat)

    freq = jnp.exp(lax.broadcasted_iota(jnp.int32, (quarter, tok), 0).astype(F32) * (-2.0 * math.log(ROPE_BASE) / (hd // 2)))

    def make_trig(slot):
        angle = pos_all[slot].astype(F32) * freq
        trig[slot // 2, 0:quarter, part_of(slot % 2, tok)] = jnp.cos(angle)
        trig[slot // 2, quarter:2 * quarter, part_of(slot % 2, tok)] = jnp.sin(angle)

    make_trig(me)

    @pl.loop(1, n_dev)
    def _(step):
        source = (me + n_dev - step) % n_dev
        remote(pos_all.at[source], pos_all.at[source], pos_s.at[step], pos_r.at[step], me).wait_recv()
        make_trig(source)

    for item in loads:
        item.wait()

    def turned(val, cos_t, sin_t):
        u = val[0:quarter]
        w = val[quarter:2 * quarter]
        return [u * cos_t - w * sin_t, w * cos_t + u * sin_t, val[2 * quarter:hd]]

    def keys_values(val, cos_t, sin_t):
        return jnp.concatenate(turned(val[0:hd], cos_t, sin_t) + [val[hd:hw]], axis=0).astype(BF)

    @pl.loop(0, n_chip)
    def _(k):
        ring_service(h_ring, 2 * k)
        ring_service(h_ring, 2 * k + 1)

        @pl.when(k == 5)
        def _():
            for item in own_sends(*y_ring):
                item.start()

        b = ring_origin(k)
        ring_mate(h_ring, k, b)
        place = part_of(b, pair)
        cos_t = trig[b, 0:quarter, :]
        sin_t = trig[b, quarter:2 * quarter, :]
        flat = dot_t(wi[...], hb[b])
        for head in range(2):
            q_rot = jnp.concatenate(turned(flat[hd * head:hd * head + hd], cos_t, sin_t), axis=0).astype(BF)
            for t in range(2):
                lane = pair * t + tok * head
                qt[b, :, lane:lane + tok] = q_rot[:, tok * t:tok * t + tok]
        kv_rot = keys_values(flat[hw:2 * hw], cos_t, sin_t)
        kvt[:, place] = kv_rot
        kv[place, :] = kv_rot.T

        @pl.when(b <= chip)
        def _():
            flat_far = dot_t(w_far[...], hb[b])
            for f in range(n_far):
                far_rot = keys_values(flat_far[hw * f:hw * f + hw], cos_t, sin_t)
                kvt_far[f, :, place] = far_rot
                kv_far[f, place, :] = far_rot.T

    def first_part(b, seen, kv_of):
        def both_of(c):
            rows = part_of(c, pair)
            both = dot(kv_of(rows), bmat[...])
            return rows, both[:, 0:cols_q] * scale, both[:, cols_q:2 * cols_q]

        rows, s, d_p = both_of(b)
        s = jnp.where(seen, s, -1e30)
        top = jnp.max(s, axis=0, keepdims=True)
        p = jnp.exp(s - top)
        sbuf[rows, :] = p
        dpbuf[rows, :] = d_p
        mbuf[b] = top

        def step(c, state):
            old, total, weighted = state
            rows, s, d_p = both_of(c)
            new = jnp.maximum(old, jnp.max(s, axis=0, keepdims=True))
            p = jnp.exp(s - new)
            sbuf[rows, :] = p
            dpbuf[rows, :] = d_p
            mbuf[c] = new
            keep = jnp.exp(old - new)
            return new, total * keep + jnp.sum(p, axis=0, keepdims=True), weighted * keep + jnp.sum(p * d_p, axis=0, keepdims=True)

        top, total, weighted = lax.fori_loop(0, b, step, (top, jnp.sum(p, axis=0, keepdims=True), jnp.sum(p * d_p, axis=0, keepdims=True)))
        inv = 1.0 / total
        return top, inv, weighted * inv

    def second_part(b, stats, kvt_of, with_keys):
        top, inv, row_dot = stats
        adq[...] = jnp.zeros_like(adq)

        def step(c, carry):
            rows = part_of(c, pair)
            p = sbuf[rows, :] * (jnp.exp(mbuf[c] - top) * inv)
            p_b = p.astype(BF)
            ds_b = (p * (dpbuf[rows, :] - row_dot) * scale).astype(BF)
            if with_keys:
                dkv[rows, :] += dot(ds_b, bmat_t[0:cols_q, :]) + dot(p_b, bmat_t[cols_q:2 * cols_q, :])
            adq[0:hd, :] += dot(kvt_of(slice(0, hd), rows), ds_b)
            adq[hd:hw, :] += dot(kvt_of(slice(hd, hw), rows), p_b)
            return carry

        lax.fori_loop(0, b + 1, step, 0)

    lane = lax.broadcasted_iota(jnp.int32, (pair, cols_q), 1)
    row = lax.broadcasted_iota(jnp.int32, (pair, cols_q), 0)

    @pl.loop(0, n_chip)
    def _(k):
        ring_service(y_ring, 2 * k)
        b = ring_origin(k)
        ring_mate(y_ring, k, b)
        da_t = dot_t(woi[...], dyb[b]).astype(BF)
        bmat[0:hd, 0:cols_q] = qt[b]
        for t in range(2):
            for head in range(2):
                at = cols_q + pair * t + tok * head
                bmat[hd:hw, at:at + tok] = da_t[hd * head:hd * head + hd, tok * t:tok * t + tok]
        for t in range(2 * cols_q // tok):
            bmat_t[tok * t:tok * t + tok, :] = bmat[:, tok * t:tok * t + tok].T
        stats = first_part(b, row <= (lane // pair) * tok + lane % tok, lambda rows: kv[rows, :])
        ring_service(y_ring, 2 * k + 1)
        second_part(b, stats, lambda part, rows: kvt[part, rows], True)
        a_pair = []
        dq_pair = []
        for t in range(2):
            slot = 2 * b + t
            lanes = [slice(pair * t + tok * head, pair * t + tok * head + tok) for head in range(2)]
            a_t = jnp.concatenate([adq[hd:hw, at] for at in lanes], axis=0).astype(BF)
            cos_t = trig[b, 0:quarter, tok * t:tok * t + tok]
            sin_t = trig[b, quarter:2 * quarter, tok * t:tok * t + tok]
            dq_t = jnp.concatenate([piece for at in lanes for piece in turned(adq[0:hd, at], cos_t, -sin_t)], axis=0).astype(BF)
            a_pair.append(a_t)
            dq_pair.append(dq_t)

            @pl.when(slot == me)
            def _():
                at_rv[own_rows, :] = a_t
                dt_rv[own_rows, :] = dq_t

            @pl.when((slot != me) & (k < 1 + 2 * near))
            def _():
                at_st[slot] = a_t
                dqt_st[slot] = dq_t
                remote(dqt_st.at[slot], dt_rv.at[own_rows], q_s.at[slot], q_r.at[me], slot).start()
                remote(at_st.at[slot], at_rv.at[own_rows], a_s.at[slot], a_r.at[me], slot).start()

        a_pair = jnp.concatenate(a_pair, axis=1)
        dq_pair = jnp.concatenate(dq_pair, axis=1)
        for t in range(width // tile):
            cols = slice(tile * t, tile * t + tile)
            dwo[:, cols] += dot(a_pair, dyb[b, :, cols])
            dwt[0:hw, cols] += dot(dq_pair, hb[b, :, cols])

    far = [ring_origin(k) for k in range(1, n_chip)]
    targets = [mate] + [2 * c + p for c in far for p in range(2)]
    near_targets = targets[0:1 + 4 * near]
    w_sends = [remote(dwt.at[pl.ds(0, hw), part_of(t, tok)], gw_hbm.at[own_rows], w_s.at[t], w_r.at[me], t) for t in targets]
    for item in w_sends:
        item.start()
    w_own = local(dwt.at[pl.ds(0, hw), part_of(me, tok)], gw_hbm.at[own_rows], loc_sem.at[0])
    w_own.start()

    for t in range(n_dev):
        dkvt[:, tok * t:tok * t + tok] = dkv[tok * t:tok * t + tok, :].T
    swap = remote(dkvt.at[part_of(1 - core, hd)], kv_rv, x_s, x_r, mate)
    swap.start()
    store_wo = local(dwo, gwo_hbm, out_sem.at[0])
    store_wo.start()

    finish_ring(y_ring)
    wo_loads = [local(wo_hbm.at[pl.ds(pair * t, pair)], dyb.at[t], wo_sem.at[t]) for t in range(n_chip)]
    for item in wo_loads:
        item.start()

    swap.wait_recv()
    mine = part_of(core, hd)
    g_rows = pl.ds(pl.multiple_of(q_rows + core * kv_w + chip * hd, hd), hd)
    for t in range(n_chip):
        cols = slice(pair * t, pair * t + pair)
        g = dkvt[mine, cols] + kv_rv[:, cols]
        cos_t = jnp.where(core == 0, trig[t, 0:quarter, :], 1.0)
        sin_t = jnp.where(core == 0, trig[t, quarter:2 * quarter, :], 0.0)
        g_b = jnp.concatenate(turned(g, cos_t, -sin_t), axis=0).astype(BF)
        kv_mine[2 * t] = g_b[:, 0:tok]
        kv_mine[2 * t + 1] = g_b[:, tok:pair]
        kv_row[:, cols] = g_b
    dt_rv[g_rows, :] = kv_mine[me]
    kv_sends = [remote(kv_mine.at[t], dt_rv.at[g_rows], kv_s.at[t], kv_r.at[me], t) for t in targets]
    for item in kv_sends:
        item.start()
    for t in range(width // tile):
        cols = slice(tile * t, tile * t + tile)
        acc = jnp.zeros((hd, tile), F32)
        for s in range(n_chip):
            acc += dot(kv_row[:, pair * s:pair * s + pair], hb[s, :, cols])
        dwt[hw:hw + hd, cols] = acc
    wk_own = local(dwt.at[pl.ds(hw, hd), part_of(me, tok)], gw_hbm.at[g_rows], loc_sem.at[1])
    wk_own.start()
    wk_sends = [remote(dwt.at[pl.ds(hw, hd), part_of(t, tok)], gw_hbm.at[g_rows], wk_s.at[t], wk_r.at[me], t) for t in targets]
    for item in wk_sends:
        item.start()

    for item in weight_loads + wo_loads:
        item.wait()

    @pl.loop(0, n_far)
    def _(f):
        c_far = ring_origin(2 * near + 1 + f)
        cos_t = trig[chip, 0:quarter, part_of(core, tok)]
        sin_t = trig[chip, quarter:2 * quarter, part_of(core, tok)]
        q_t = dot_t(wt[part_of(c_far, 2 * hw), :], hb[chip, part_of(core, tok), :])
        da_t = dot_t(dyb[c_far], dy_own[...]).astype(BF)
        for head in range(4):
            part = slice(hd * head, hd * head + hd)
            at = tok * head
            bmat[0:hd, at:at + tok] = jnp.concatenate(turned(q_t[part], cos_t, sin_t), axis=0).astype(BF)
            bmat[hd:hw, cols_q + at:cols_q + at + tok] = da_t[part]
        stats = first_part(chip, row <= core * tok + lane % tok, lambda rows: kv_far[f, rows, :])
        second_part(chip, stats, lambda part, rows: kvt_far[f, part, rows], False)
        for head in range(4):
            at = slice(tok * head, tok * head + tok)
            place = pl.ds(pl.multiple_of(c_far * 2 * hw + hd * head, hd), hd)
            at_rv[place, :] = adq[hd:hw, at].astype(BF)
            dt_rv[place, :] = jnp.concatenate(turned(adq[0:hd, at], cos_t, -sin_t), axis=0).astype(BF)

    for t in near_targets:
        remote(at_st.at[0], at_rv.at[part_of(t, hw)], a_s.at[t], a_r.at[t], t).wait_recv()
    for t in range(q_rows // tok):
        a_nat[:, tok * t:tok * t + tok] = at_rv[tok * t:tok * t + tok, :].T
    for t in range(width // tile):
        cols = slice(tile * t, tile * t + tile)
        prod = jnp.zeros((tok, tile), F32)
        for s in range(n_chip):
            prod += dot(a_nat[:, pair * s:pair * s + pair], dyb[s, :, cols])
        out_v[:, cols] = (x_v[:, cols].astype(F32) + prod).astype(BF)
    store_out = local(out_v, out_hbm, out_sem.at[1])
    store_out.start()

    def kv_place(t):
        return pl.ds(pl.multiple_of(q_rows + (t % 2) * kv_w + (t // 2) * hd, hd), hd)

    for t in near_targets:
        remote(dqt_st.at[0], dt_rv.at[part_of(t, hw)], q_s.at[t], q_r.at[t], t).wait_recv()
    for t in targets:
        remote(kv_mine.at[0], dt_rv.at[kv_place(t)], kv_s.at[t], kv_r.at[t], t).wait_recv()
    swap.wait_send()
    for t in range(n_rows // tok):
        d_nat[:, tok * t:tok * t + tok] = dt_rv[tok * t:tok * t + tok, :].T

    mean = stat[0, :, 0:1]
    inv_std = stat[1, :, 0:1]
    dh = dkvt
    for t in range(width // tile):
        cols = slice(tile * t, tile * t + tile)
        acc = jnp.zeros((tok, tile), F32)
        for s in range(n_rows // tile):
            acc += dot(d_nat[:, tile * s:tile * s + tile], wt[tile * s:tile * s + tile, cols])
        dh[:, cols] = acc
        gg_st[0, :, cols] = jnp.sum(acc * ((x_v[:, cols].astype(F32) - mean) * inv_std), axis=0, keepdims=True)
        gg_st[1, :, cols] = jnp.sum(acc, axis=0, keepdims=True)
    g_swap = remote(gg_st.at[1 - core], gg_mx, g_s.at[n_chip], g_r.at[n_chip], mate)
    g_swap.start()
    g_swap.wait_recv()
    gg_my[...] = jnp.where(core == 0, gg_st[0], gg_st[1]) + gg_mx[...]
    gg_rv[chip] = gg_my[...]
    g_sends = [remote(gg_my, gg_rv.at[chip], g_s.at[c], g_r.at[chip], 2 * c + core) for c in far]
    for item in g_sends:
        item.start()

    grad_hat = dh[...] * gain_one
    x_hat = (x_v[...].astype(F32) - mean) * inv_std
    mean_one = jnp.mean(grad_hat, axis=-1, keepdims=True)
    mean_two = jnp.mean(grad_hat * x_hat, axis=-1, keepdims=True)
    store_out.wait()
    out_v[...] = (dy_own[...].astype(F32) + inv_std * (grad_hat - mean_one - x_hat * mean_two)).astype(BF)
    store_gx = local(out_v, gx_hbm, out_sem.at[2])
    store_gx.start()

    for c in far:
        remote(gg_my, gg_rv.at[c], g_s.at[c], g_r.at[c], 2 * c + core).wait_recv()
    sums = gg_rv[0]
    for c in range(1, n_chip):
        sums = sums + gg_rv[c]
    gg_out[core] = sums
    g_swap_out = remote(gg_out.at[core], gg_out.at[core], g_s.at[n_chip + 1], g_r.at[n_chip + 1], mate)
    g_swap_out.start()
    remote(gg_out.at[core], gg_out.at[1 - core], g_s.at[n_chip + 1], g_r.at[n_chip + 1], mate).wait_recv()
    store_gg = local(gg_out, gg_hbm, out_sem.at[3])
    store_gg.start()

    finish_ring(h_ring)
    for item in pos_sends + [g_swap, g_swap_out]:
        item.wait_send()
    for t in near_targets:
        remote(at_st.at[0], at_rv.at[pl.ds(0, hw)], a_s.at[t], a_r.at[t], t).wait_send()
        remote(dqt_st.at[0], dt_rv.at[pl.ds(0, hw)], q_s.at[t], q_r.at[t], t).wait_send()
    for item in kv_sends + w_sends + g_sends + wk_sends:
        item.wait_send()
    for t in targets:
        remote(dwt.at[pl.ds(0, hw), part_of(t, tok)], gw_hbm.at[part_of(t, hw)], w_s.at[t], w_r.at[t], t).wait_recv()
        remote(dwt.at[pl.ds(hw, hd), part_of(t, tok)], gw_hbm.at[kv_place(t)], wk_s.at[t], wk_r.at[t], t).wait_recv()
    for item in (w_own, wk_own, store_wo, store_gx, store_gg):
        item.wait()


def settle_kernel(q_rows, kv_w, out_i, gx_i, gw_i, gwo_i, gg_i, out_o, gx_o, gq_o, gk_o, gv_o, gwo_o, gain_o, bias_o, b_act, b_q, b_kv, b_o, b_gg, sem_in, sem_out, sem_gg):
    half_q = q_rows // 2
    half_o = gwo_i.shape[0] // 2
    moves = [(out_i, b_act.at[0], out_o), (gx_i, b_act.at[1], gx_o)]
    for t in range(2):
        moves.append((gw_i.at[pl.ds(half_q * t, half_q)], b_q.at[t], gq_o.at[pl.ds(half_q * t, half_q)]))
        moves.append((gwo_i.at[pl.ds(half_o * t, half_o)], b_o.at[t], gwo_o.at[pl.ds(half_o * t, half_o)]))
    moves.append((gw_i.at[pl.ds(q_rows, kv_w)], b_kv.at[0], gk_o))
    moves.append((gw_i.at[pl.ds(q_rows + kv_w, kv_w)], b_kv.at[1], gv_o))
    loads = [pltpu.make_async_copy(src, mid, sem_in.at[i]) for i, (src, mid, _) in enumerate(moves)]
    stores = [pltpu.make_async_copy(mid, dst, sem_out.at[i]) for i, (_, mid, dst) in enumerate(moves)]
    load_gg = pltpu.make_async_copy(gg_i, b_gg, sem_gg)
    load_gg.start()
    for item in loads:
        item.start()
    for load, store in zip(loads, stores):
        load.wait()
        store.start()
    load_gg.wait()
    gain_o[...] = b_gg[0, 0]
    bias_o[...] = b_gg[1, 0]
    for item in stores:
        item.wait()


def solution(mesh):
    n_dev = mesh.shape['cp']

    def device_step(x_act, d_out, positions, ln_gain, ln_bias, w_query, w_key, w_value, w_out):
        tok, width = x_act.shape[1], x_act.shape[2]
        q_heads, hd = w_query.shape[1], w_query.shape[2]
        kv_heads = w_key.shape[1]
        q_w, kv_w = q_heads * hd, kv_heads * hd
        n_rows = q_w + 2 * kv_w
        seq = n_dev * tok
        hw = 2 * hd

        def flat_weight(w):
            return jnp.transpose(w, (1, 2, 0)).reshape(-1, width)

        hbm = pl.BlockSpec(memory_space=pltpu.HBM)
        vmem = pl.BlockSpec(memory_space=pltpu.VMEM)
        dma = pltpu.SemaphoreType.DMA
        n_chip = n_dev // 2
        n_far = n_chip - 1 - 2 * NEAR
        pair = 2 * tok
        scratch = [
            pltpu.VMEM((n_chip, pair, width), BF),
            pltpu.VMEM((n_chip, pair, width), BF),
            pltpu.VMEM((n_rows, width), BF),
            pltpu.VMEM((2 * hw, width), BF),
            pltpu.VMEM((hw, width), BF),
            pltpu.VMEM((n_far * hw, width), BF),
            pltpu.VMEM((n_dev, 1, tok), jnp.int32),
            pltpu.VMEM((n_chip, hd // 2, pair), F32),
            pltpu.VMEM((n_chip, hd, 2 * pair), BF),
            pltpu.VMEM((hw, seq), BF),
            pltpu.VMEM((seq, hw), BF),
            pltpu.VMEM((n_far, hw, seq), BF),
            pltpu.VMEM((n_far, seq, hw), BF),
            pltpu.VMEM((hw, 4 * pair), BF),
            pltpu.VMEM((4 * pair, hw), BF),
            pltpu.VMEM((seq, 2 * pair), F32),
            pltpu.VMEM((seq, 2 * pair), F32),
            pltpu.VMEM((n_chip, 1, 2 * pair), F32),
            pltpu.VMEM((hw, 2 * pair), F32),
            pltpu.VMEM((seq, hw), F32),
            pltpu.VMEM((hw, seq), F32),
            pltpu.VMEM((hd, seq), F32),
            pltpu.VMEM((n_dev, hd, tok), BF),
            pltpu.VMEM((hd, seq), BF),
            pltpu.VMEM((hw, width), F32),
            pltpu.VMEM((hw + hd, width), F32),
            pltpu.VMEM((n_dev, hw, tok), BF),
            pltpu.VMEM((n_dev, hw, tok), BF),
            pltpu.VMEM((q_w, tok), BF),
            pltpu.VMEM((n_rows, tok), BF),
            pltpu.VMEM((tok, q_w), BF),
            pltpu.VMEM((tok, n_rows), BF),
            pltpu.VMEM((tok, width), BF),
            pltpu.VMEM((tok, width), BF),
            pltpu.VMEM((2, 1, width), F32),
            pltpu.VMEM((2, tok, 128), F32),
            pltpu.VMEM((tok, width), BF),
            pltpu.VMEM((2, 1, width), F32),
            pltpu.VMEM((1, width), F32),
            pltpu.VMEM((1, width), F32),
            pltpu.VMEM((n_chip, 1, width), F32),
            pltpu.VMEM((2, 1, width), F32),
            dma((10,)), dma((2 * n_far,)), dma((n_chip,)), dma((3,)), dma((4,)), dma((2,)),
            dma((16,)), dma((14,)), dma((16,)), dma((16,)),
            dma((16,)), dma((14,)), dma((16,)), dma((16,)),
        ] + [dma((n_dev,))] * 6 + [dma] * 2 + [dma((n_dev,))] * 8
        out, gx, gw, gwo, gg = pl.pallas_call(
            functools.partial(block_kernel, n_dev, hd, kv_w, NEAR),
            out_shape=(
                jax.ShapeDtypeStruct((tok, width), BF),
                jax.ShapeDtypeStruct((tok, width), BF),
                jax.ShapeDtypeStruct((n_rows, tok), F32),
                jax.ShapeDtypeStruct((hw, width), F32),
                jax.ShapeDtypeStruct((2, 1, width), F32),
            ),
            in_specs=[hbm] * 9,
            out_specs=(hbm,) * 5,
            scratch_shapes=scratch,
            compiler_params=pltpu.CompilerParams(collective_id=0, has_side_effects=True, vmem_limit_bytes=67043328),
            name='attn_block',
        )(
            x_act.reshape(tok, width), d_out.reshape(tok, width), positions.reshape(1, tok),
            ln_gain.reshape(1, width), ln_bias.reshape(1, width),
            flat_weight(w_query), flat_weight(w_key), flat_weight(w_value), w_out,
        )

        out, gx, gq, gk, gv, gwo, gain, bias = pl.pallas_call(
            functools.partial(settle_kernel, q_w, kv_w),
            out_shape=(
                jax.ShapeDtypeStruct((tok, width), BF),
                jax.ShapeDtypeStruct((tok, width), BF),
                jax.ShapeDtypeStruct((q_w, tok), F32),
                jax.ShapeDtypeStruct((kv_w, tok), F32),
                jax.ShapeDtypeStruct((kv_w, tok), F32),
                jax.ShapeDtypeStruct((hw, width), F32),
                jax.ShapeDtypeStruct((width,), F32),
                jax.ShapeDtypeStruct((width,), F32),
            ),
            in_specs=[hbm] * 5,
            out_specs=(hbm,) * 6 + (vmem,) * 2,
            scratch_shapes=[
                pltpu.VMEM((2, tok, width), BF),
                pltpu.VMEM((2, q_w // 2, tok), F32),
                pltpu.VMEM((2, kv_w, tok), F32),
                pltpu.VMEM((2, hw // 2, width), F32),
                pltpu.VMEM((2, 1, width), F32),
                dma((8,)), dma((8,)), dma,
            ],
            name='settle',
        )(out, gx, gw, gwo, gg)

        def rows_out(block, heads):
            return jnp.transpose(block.reshape(heads, hd, tok), (2, 0, 1))

        return (
            out.reshape(1, tok, width), gx.reshape(1, tok, width),
            rows_out(gq, q_heads), rows_out(gk, kv_heads), rows_out(gv, kv_heads),
            gwo, gain, bias,
        )

    return jax.shard_map(device_step, mesh=mesh, in_specs=(P('dp', 'cp', None), P('dp', 'cp', None), P('dp', 'cp'), P(None), P(None), P(None, None, None), P(None, None, None), P(None, None, None), P(None, None)), out_specs=(P('dp', 'cp', None), P('dp', 'cp', None), P(('dp', 'cp'), None, None), P(('dp', 'cp'), None, None), P(('dp', 'cp'), None, None), P(('dp', 'cp'), None), P('dp'), P('dp')), check_vma=False)
```

time: 178 us -> 164 us (0.921); the launches traced: 176 us -> 164 us
  Pallas kernels: 175 us -> 163 us
    pallas_call x1, Pallas kernels: 172 us -> 160 us  [device_step(): pl.pallas_call(functools.partial(block_kernel, n_dev, hd, kv_w, NEAR), ou...]
where the time goes in v3:
time: 164 us
  Pallas kernels  163 us (99%)
    pallas_call x1, Pallas kernels, device_step(): pl.pallas_call(functools.partial(block_kernel, n_dev, hd, kv_w, NEAR), ou...  160 us
    pallas_call x1, Pallas kernels, device_step(): pl.pallas_call(functools.partial(settle_kernel, q_w, kv_w), out_shape=(ja...  3.62 us

profile of v3, /device:TPU:21, one launch (start us, length us, event | category | flops | bytes accessed | tf_op | source)
XLA Modules:
  0.0 164.1 jit_solution(15992035696546402899)
XLA Ops:
  0.6 159.8 %attn_block.1 = (bf16[128,2048]{1,0:T(8,128)(2,1)}, bf16[128,2048]{1,0:T(8,128)(2,1)}, f32[3072,128]{1,0:T(8,128)}, f32[128,2048]{1,0:T(8,128)}, f32[2,1,2048]{2,1,0:T(1,128)}) custom-call(bf16[128,2048]{1,0:T(8,128)(2,1)} %bitcast.27, bf16[128,2048]{1,0:T(8,128)(2,1)} %bitcast.28, s32[1,128]{1,0:T(1,128)} %pos_hbm.1, f32[1,2048]{1,0:T(1,128)} %bitcast.29, ...), custom_call_target="tpu_custom_call" | custom-call | tf_op jit(solution)/shard_map/attn_block/pallas_call | solution.py:593
  160.5 3.6 %settle.1 = (bf16[128,2048]{1,0:T(8,128)(2,1)}, bf16[128,2048]{1,0:T(8,128)(2,1)}, f32[2048,128]{1,0:T(8,128)}, f32[512,128]{1,0:T(8,128)}, f32[512,128]{1,0:T(8...) custom-call(bf16[128,2048]{1,0:T(8,128)(2,1)} %get-tuple-element.21.out_i, ...), custom_call_target="tpu_custom_call" | custom-call | tf_op jit(solution)/shard_map/settle/pallas_call | solution.py:613

commit v4 on v3

--- a/solution.py
+++ b/solution.py
@@ -14,6 +14,7 @@
 BF = jnp.bfloat16
 F32 = jnp.float32
 NEAR = 1
+PARTS = 4
 
 
 def dot(lhs, rhs):
@@ -25,11 +26,11 @@
 
 
 def block_kernel(
-    n_dev, hd, kv_w, near,
+    n_dev, hd, kv_w, near, parts,
     x_hbm, dy_hbm, pos_hbm, gain_hbm, bias_hbm, wq_hbm, wk_hbm, wv_hbm, wo_hbm,
     out_hbm, gx_hbm, gw_hbm, gwo_hbm, gg_hbm,
     hb, dyb, wt, wi, woi, w_far, pos_all, trig,
-    qt, kvt, kv, kvt_far, kv_far, bmat, bmat_t, sbuf, dpbuf, mbuf, adq, dkv, dkvt, kv_rv, kv_mine, kv_row,
+    qt, kvt, kv, kvt_far, kv_far, q_far, da_far, bmat, bmat_t, sbuf, dpbuf, mbuf, adq, dkv, dkvt, kv_rv, kv_mine, kv_row,
     dwo, dwt, at_st, dqt_st, at_rv, dt_rv, a_nat, d_nat, x_v, dy_own, gb_v, stat, out_v, gg_st, gg_mx, gg_my, gg_rv, gg_out,
     in_sem, far_sem, wo_sem, w_sem, out_sem, loc_sem,
     hzs, hzr, hds, hdr, yzs, yzr, yds, ydr,
@@ -37,7 +38,6 @@
 ):
     tok, width = x_v.shape
     n_chip = n_dev // 2
-    half = tok // 2
     pair = 2 * tok
     me = lax.axis_index('cp')
     chip = me // 2
@@ -97,6 +97,8 @@
         far_rows = part_of(ring_origin(2 * near + 1 + f), hd)
         loads.append(local(wk_hbm.at[far_rows], w_far.at[pl.ds(hw * f, hd)], far_sem.at[2 * f]))
         loads.append(local(wv_hbm.at[far_rows], w_far.at[pl.ds(hw * f + hd, hd)], far_sem.at[2 * f + 1]))
+        far_wo = part_of(ring_origin(2 * near + 1 + f), 2 * hw)
+        loads.append(local(wo_hbm.at[far_wo], wt.at[pl.ds(2 * hw * f, 2 * hw)], far_sem.at[2 * n_far + f]))
     for item in loads:
         item.start()
 
@@ -114,49 +116,53 @@
     pl.semaphore_wait(barrier, n_dev - 1)
 
     def chunk(buf, origin, parity, part):
-        return buf.at[origin, part_of(2 * parity + part, half)]
+        return buf.at[origin, part_of(parts * parity + part, tok // parts)]
+
+    turns = 2 * parts
 
     def own_sends(buf, zs, zr, ds, dr):
         copies = []
-        for part in range(2):
+        for part in range(parts):
             piece = chunk(buf, chip, core, part)
             copies.append(remote(piece, piece, zs.at[2 * part], zr.at[2 * part], right))
             copies.append(remote(piece, piece, zs.at[2 * part + 1], zr.at[2 * part + 1], left))
-            copies.append(remote(piece, piece, ds.at[14 + part], dr.at[14 + part], mate))
+            copies.append(remote(piece, piece, ds.at[7 * parts + part], dr.at[7 * parts + part], mate))
         return copies
 
     def event_place(event):
-        step = event // 4 + 1
-        turn = event % 4
+        step = event // turns + 1
+        turn = event % turns
         direction = turn % 2
-        part = jnp.where(step < 4, turn // 2, turn)
+        part = jnp.where(step < 4, turn // 2, turn // 2 + direction * (parts // 2))
         origin = jnp.where(direction == 0, chip + n_chip - step, chip + step) % n_chip
-        return step, turn, direction, part, origin
+        return step, direction, part, origin
+
+    def last_event(part, direction):
+        return 6 * parts + 2 * (part - direction * (parts // 2)) + direction
 
     def ring_event(ring, event):
         buf, zs, zr, ds, dr = ring
-        step, turn, direction, part, origin = event_place(event)
+        step, direction, part, origin = event_place(event)
         piece = chunk(buf, origin, core, part)
         remote(piece, piece, zs.at[0], zr.at[event], right).wait_recv()
-        onward = jnp.where(step < 3, event + 4, jnp.where(turn == 0, 12, 13))
-
-        @pl.when((step < 3) | ((step == 3) & ((turn == 0) | (turn == 3))))
+        onward = jnp.where(step < 3, event + turns, last_event(part, direction))
+
+        @pl.when((step < 3) | ((step == 3) & ((part >= parts // 2) == (direction == 1))))
         def _():
-            remote(piece, piece, zs.at[event + 4], zr.at[onward], jnp.where(direction == 0, right, left)).start()
+            remote(piece, piece, zs.at[event + turns], zr.at[onward], jnp.where(direction == 0, right, left)).start()
 
         remote(piece, piece, ds.at[event], dr.at[event], mate).start()
 
     def ring_service(ring, event):
-        @pl.when(event < 14)
+        @pl.when(event < 7 * parts)
         def _():
             ring_event(ring, event)
 
     def ring_mate(ring, k, origin):
         buf, zs, zr, ds, dr = ring
         step, ahead = ring_steps(k)
-        first = jnp.where(k == 0, 14, jnp.where(step < 4, 4 * (step - 1) + 1 - ahead, 12))
-        second = jnp.where(k == 0, 15, jnp.where(step < 4, 4 * (step - 1) + 3 - ahead, 13))
-        for part, event in ((0, first), (1, second)):
+        for part in range(parts):
+            event = jnp.where(k == 0, 7 * parts + part, jnp.where(step < 4, turns * (step - 1) + 2 * part + 1 - ahead, last_event(part, part // (parts // 2))))
             piece = chunk(buf, origin, 1 - core, part)
             remote(piece, piece, ds.at[0], dr.at[event], mate).wait_recv()
 
@@ -164,11 +170,16 @@
         buf, zs, zr, ds, dr = ring
         for item in own_sends(*ring):
             item.wait_send()
-        for event in range(14):
-            _, _, _, part, origin = event_place(event)
+
+        @pl.loop(0, 7 * parts)
+        def _(event):
+            step, direction, part, origin = event_place(event)
             piece = chunk(buf, origin, core, part)
-            if event < 8 or event in (8, 11):
-                remote(piece, piece, zs.at[event + 4], zr.at[event], right).wait_send()
+
+            @pl.when((step < 3) | ((step == 3) & ((part >= parts // 2) == (direction == 1))))
+            def _():
+                remote(piece, piece, zs.at[event + turns], zr.at[event], right).wait_send()
+
             remote(piece, piece, ds.at[event], dr.at[event], mate).wait_send()
 
     h_ring = (hb, hzs, hzr, hds, hdr)
@@ -183,8 +194,6 @@
         local(wk_hbm, wt.at[pl.ds(q_rows, kv_w)], w_sem.at[1]),
         local(wv_hbm, wt.at[pl.ds(q_rows + kv_w, kv_w)], w_sem.at[2]),
     ]
-    for item in weight_loads:
-        item.start()
     dkv[...] = jnp.zeros_like(dkv)
     dwo[...] = jnp.zeros_like(dwo)
     dwt[...] = jnp.zeros_like(dwt)
@@ -208,23 +217,48 @@
     for item in loads:
         item.wait()
 
+    @pl.loop(0, n_far)
+    def _(f):
+        da_t = dot_t(wt[part_of(f, 2 * hw), :], dy_own[...]).astype(BF)
+        for head in range(4):
+            da_far[f, :, tok * head:tok * head + tok] = da_t[hd * head:hd * head + hd]
+
+    for item in weight_loads:
+        item.start()
+
     def turned(val, cos_t, sin_t):
         u = val[0:quarter]
         w = val[quarter:2 * quarter]
         return [u * cos_t - w * sin_t, w * cos_t + u * sin_t, val[2 * quarter:hd]]
 
+    def eighth(val):
+        return val.astype(BF) * jnp.asarray(scale, BF)
+
     def keys_values(val, cos_t, sin_t):
         return jnp.concatenate(turned(val[0:hd], cos_t, sin_t) + [val[hd:hw]], axis=0).astype(BF)
 
     @pl.loop(0, n_chip)
     def _(k):
-        ring_service(h_ring, 2 * k)
-        ring_service(h_ring, 2 * k + 1)
+        for turn in range(parts):
+            ring_service(h_ring, parts * k + turn)
 
         @pl.when(k == 5)
         def _():
             for item in own_sends(*y_ring):
                 item.start()
+
+        @pl.when(k == 4)
+        def _():
+            for item in weight_loads:
+                item.wait()
+
+            @pl.loop(0, n_far)
+            def _(f):
+                cos_t = trig[chip, 0:quarter, part_of(core, tok)]
+                sin_t = trig[chip, quarter:2 * quarter, part_of(core, tok)]
+                q_t = dot_t(wt[part_of(ring_origin(2 * near + 1 + f), 2 * hw), :], hb[chip, part_of(core, tok), :])
+                for head in range(4):
+                    q_far[f, :, tok * head:tok * head + tok] = eighth(jnp.concatenate(turned(q_t[hd * head:hd * head + hd], cos_t, sin_t), axis=0))
 
         b = ring_origin(k)
         ring_mate(h_ring, k, b)
@@ -233,7 +267,7 @@
         sin_t = trig[b, quarter:2 * quarter, :]
         flat = dot_t(wi[...], hb[b])
         for head in range(2):
-            q_rot = jnp.concatenate(turned(flat[hd * head:hd * head + hd], cos_t, sin_t), axis=0).astype(BF)
+            q_rot = eighth(jnp.concatenate(turned(flat[hd * head:hd * head + hd], cos_t, sin_t), axis=0))
             for t in range(2):
                 lane = pair * t + tok * head
                 qt[b, :, lane:lane + tok] = q_rot[:, tok * t:tok * t + tok]
@@ -249,58 +283,76 @@
                 kvt_far[f, :, place] = far_rot
                 kv_far[f, place, :] = far_rot.T
 
+    groups = [slice(tile * g, tile * g + tile) for g in range(cols_q // tile)]
+
     def first_part(b, seen, kv_of):
-        def both_of(c):
+        def scores(c, at):
             rows = part_of(c, pair)
-            both = dot(kv_of(rows), bmat[...])
-            return rows, both[:, 0:cols_q] * scale, both[:, cols_q:2 * cols_q]
-
-        rows, s, d_p = both_of(b)
-        s = jnp.where(seen, s, -1e30)
-        top = jnp.max(s, axis=0, keepdims=True)
-        p = jnp.exp(s - top)
-        sbuf[rows, :] = p
-        dpbuf[rows, :] = d_p
-        mbuf[b] = top
+            keys = kv_of(rows)
+            s = dot(keys, bmat[:, at])
+            d_p = dot(keys, bmat[:, cols_q + at.start:cols_q + at.stop])
+            dpbuf[rows, at] = d_p
+            return rows, s, d_p
+
+        begin = []
+        for at in groups:
+            rows, s, d_p = scores(b, at)
+            s = jnp.where(seen(at), s, -1e30)
+            top = jnp.max(s, axis=0, keepdims=True)
+            p = jnp.exp(s - top)
+            sbuf[rows, at] = p
+            mbuf[b, :, at] = top
+            begin += [top, jnp.sum(p, axis=0, keepdims=True), jnp.sum(p * d_p, axis=0, keepdims=True)]
 
         def step(c, state):
-            old, total, weighted = state
-            rows, s, d_p = both_of(c)
-            new = jnp.maximum(old, jnp.max(s, axis=0, keepdims=True))
-            p = jnp.exp(s - new)
-            sbuf[rows, :] = p
-            dpbuf[rows, :] = d_p
-            mbuf[c] = new
-            keep = jnp.exp(old - new)
-            return new, total * keep + jnp.sum(p, axis=0, keepdims=True), weighted * keep + jnp.sum(p * d_p, axis=0, keepdims=True)
-
-        top, total, weighted = lax.fori_loop(0, b, step, (top, jnp.sum(p, axis=0, keepdims=True), jnp.sum(p * d_p, axis=0, keepdims=True)))
-        inv = 1.0 / total
-        return top, inv, weighted * inv
+            after = []
+            for g, at in enumerate(groups):
+                old, total, weighted = state[3 * g:3 * g + 3]
+                rows, s, d_p = scores(c, at)
+                new = jnp.maximum(old, jnp.max(s, axis=0, keepdims=True))
+                p = jnp.exp(s - new)
+                sbuf[rows, at] = p
+                mbuf[c, :, at] = new
+                keep = jnp.exp(old - new)
+                after += [new, total * keep + jnp.sum(p, axis=0, keepdims=True), weighted * keep + jnp.sum(p * d_p, axis=0, keepdims=True)]
+            return after
+
+        state = lax.fori_loop(0, b, step, begin)
+        stats = []
+        for g in range(len(groups)):
+            top, total, weighted = state[3 * g:3 * g + 3]
+            inv = 1.0 / total
+            stats.append((top, inv, weighted * inv))
+        return stats
 
     def second_part(b, stats, kvt_of, with_keys):
-        top, inv, row_dot = stats
         adq[...] = jnp.zeros_like(adq)
 
         def step(c, carry):
             rows = part_of(c, pair)
-            p = sbuf[rows, :] * (jnp.exp(mbuf[c] - top) * inv)
-            p_b = p.astype(BF)
-            ds_b = (p * (dpbuf[rows, :] - row_dot) * scale).astype(BF)
+            grad = None
+            for at, (top, inv, row_dot) in zip(groups, stats):
+                p = sbuf[rows, at] * (jnp.exp(mbuf[c, :, at] - top) * inv)
+                p_b = p.astype(BF)
+                ds_b = (p * (dpbuf[rows, at] - row_dot)).astype(BF)
+                adq[0:hd, at] += dot(kvt_of(slice(0, hd), rows), ds_b)
+                adq[hd:hw, at] += dot(kvt_of(slice(hd, hw), rows), p_b)
+                if with_keys:
+                    more = dot(ds_b, bmat_t[at, :]) + dot(p_b, bmat_t[cols_q + at.start:cols_q + at.stop, :])
+                    grad = more if grad is None else grad + more
             if with_keys:
-                dkv[rows, :] += dot(ds_b, bmat_t[0:cols_q, :]) + dot(p_b, bmat_t[cols_q:2 * cols_q, :])
-            adq[0:hd, :] += dot(kvt_of(slice(0, hd), rows), ds_b)
-            adq[hd:hw, :] += dot(kvt_of(slice(hd, hw), rows), p_b)
+                dkv[rows, :] += grad
             return carry
 
         lax.fori_loop(0, b + 1, step, 0)
 
-    lane = lax.broadcasted_iota(jnp.int32, (pair, cols_q), 1)
-    row = lax.broadcasted_iota(jnp.int32, (pair, cols_q), 0)
+    lane = lax.broadcasted_iota(jnp.int32, (pair, tile), 1)
+    row = lax.broadcasted_iota(jnp.int32, (pair, tile), 0)
 
     @pl.loop(0, n_chip)
     def _(k):
-        ring_service(y_ring, 2 * k)
+        for turn in range(parts - 1):
+            ring_service(y_ring, parts * k + turn)
         b = ring_origin(k)
         ring_mate(y_ring, k, b)
         da_t = dot_t(woi[...], dyb[b]).astype(BF)
@@ -311,8 +363,8 @@
                 bmat[hd:hw, at:at + tok] = da_t[hd * head:hd * head + hd, tok * t:tok * t + tok]
         for t in range(2 * cols_q // tok):
             bmat_t[tok * t:tok * t + tok, :] = bmat[:, tok * t:tok * t + tok].T
-        stats = first_part(b, row <= (lane // pair) * tok + lane % tok, lambda rows: kv[rows, :])
-        ring_service(y_ring, 2 * k + 1)
+        stats = first_part(b, lambda at: row <= (at.start // pair) * tok + lane % tok, lambda rows: kv[rows, :])
+        ring_service(y_ring, parts * k + parts - 1)
         second_part(b, stats, lambda part, rows: kvt[part, rows], True)
         a_pair = []
         dq_pair = []
@@ -322,7 +374,7 @@
             a_t = jnp.concatenate([adq[hd:hw, at] for at in lanes], axis=0).astype(BF)
             cos_t = trig[b, 0:quarter, tok * t:tok * t + tok]
             sin_t = trig[b, quarter:2 * quarter, tok * t:tok * t + tok]
-            dq_t = jnp.concatenate([piece for at in lanes for piece in turned(adq[0:hd, at], cos_t, -sin_t)], axis=0).astype(BF)
+            dq_t = jnp.concatenate([piece for at in lanes for piece in turned(adq[0:hd, at] * scale, cos_t, -sin_t)], axis=0).astype(BF)
             a_pair.append(a_t)
             dq_pair.append(dq_t)
 
@@ -394,31 +446,25 @@
     for item in wk_sends:
         item.start()
 
-    for item in weight_loads + wo_loads:
-        item.wait()
-
     @pl.loop(0, n_far)
     def _(f):
         c_far = ring_origin(2 * near + 1 + f)
         cos_t = trig[chip, 0:quarter, part_of(core, tok)]
         sin_t = trig[chip, quarter:2 * quarter, part_of(core, tok)]
-        q_t = dot_t(wt[part_of(c_far, 2 * hw), :], hb[chip, part_of(core, tok), :])
-        da_t = dot_t(dyb[c_far], dy_own[...]).astype(BF)
-        for head in range(4):
-            part = slice(hd * head, hd * head + hd)
-            at = tok * head
-            bmat[0:hd, at:at + tok] = jnp.concatenate(turned(q_t[part], cos_t, sin_t), axis=0).astype(BF)
-            bmat[hd:hw, cols_q + at:cols_q + at + tok] = da_t[part]
-        stats = first_part(chip, row <= core * tok + lane % tok, lambda rows: kv_far[f, rows, :])
+        bmat[0:hd, 0:cols_q] = q_far[f]
+        bmat[hd:hw, cols_q:2 * cols_q] = da_far[f]
+        stats = first_part(chip, lambda at: row <= core * tok + lane % tok, lambda rows: kv_far[f, rows, :])
         second_part(chip, stats, lambda part, rows: kvt_far[f, part, rows], False)
         for head in range(4):
             at = slice(tok * head, tok * head + tok)
             place = pl.ds(pl.multiple_of(c_far * 2 * hw + hd * head, hd), hd)
             at_rv[place, :] = adq[hd:hw, at].astype(BF)
-            dt_rv[place, :] = jnp.concatenate(turned(adq[0:hd, at], cos_t, -sin_t), axis=0).astype(BF)
+            dt_rv[place, :] = jnp.concatenate(turned(adq[0:hd, at] * scale, cos_t, -sin_t), axis=0).astype(BF)
 
     for t in near_targets:
         remote(at_st.at[0], at_rv.at[part_of(t, hw)], a_s.at[t], a_r.at[t], t).wait_recv()
+    for item in wo_loads:
+        item.wait()
     for t in range(q_rows // tok):
         a_nat[:, tok * t:tok * t + tok] = at_rv[tok * t:tok * t + tok, :].T
     for t in range(width // tile):
@@ -557,6 +603,8 @@
             pltpu.VMEM((seq, hw), BF),
             pltpu.VMEM((n_far, hw, seq), BF),
             pltpu.VMEM((n_far, seq, hw), BF),
+            pltpu.VMEM((n_far, hd, 2 * pair), BF),
+            pltpu.VMEM((n_far, hd, 2 * pair), BF),
             pltpu.VMEM((hw, 4 * pair), BF),
             pltpu.VMEM((4 * pair, hw), BF),
             pltpu.VMEM((seq, 2 * pair), F32),
@@ -586,12 +634,10 @@
             pltpu.VMEM((1, width), F32),
             pltpu.VMEM((n_chip, 1, width), F32),
             pltpu.VMEM((2, 1, width), F32),
-            dma((10,)), dma((2 * n_far,)), dma((n_chip,)), dma((3,)), dma((4,)), dma((2,)),
-            dma((16,)), dma((14,)), dma((16,)), dma((16,)),
-            dma((16,)), dma((14,)), dma((16,)), dma((16,)),
-        ] + [dma((n_dev,))] * 6 + [dma] * 2 + [dma((n_dev,))] * 8
+            dma((10,)), dma((3 * n_far,)), dma((n_chip,)), dma((3,)), dma((4,)), dma((2,)),
+        ] + [dma((9 * PARTS,)), dma((7 * PARTS,)), dma((8 * PARTS,)), dma((8 * PARTS,))] * 2 + [dma((n_dev,))] * 6 + [dma] * 2 + [dma((n_dev,))] * 8
         out, gx, gw, gwo, gg = pl.pallas_call(
-            functools.partial(block_kernel, n_dev, hd, kv_w, NEAR),
+            functools.partial(block_kernel, n_dev, hd, kv_w, NEAR, PARTS),
             out_shape=(
                 jax.ShapeDtypeStruct((tok, width), BF),
                 jax.ShapeDtypeStruct((tok, width), BF),

time: 164 us -> 167 us (1.018)
  Pallas kernels: 163 us -> 167 us
    pallas_call x1, Pallas kernels: 160 us -> 163 us  [device_step(): pl.pallas_call(functools.partial(block_kernel, n_dev, hd, kv_w, NEAR, PAR...]
where the time goes in v4:
time: 167 us
  Pallas kernels  167 us (100%)
    pallas_call x1, Pallas kernels, device_step(): pl.pallas_call(functools.partial(block_kernel, n_dev, hd, kv_w, NEAR, PAR...  163 us
    pallas_call x1, Pallas kernels, device_step(): pl.pallas_call(functools.partial(settle_kernel, q_w, kv_w), out_shape=(ja...  3.62 us

profile of v4, /device:TPU:21, one launch (start us, length us, event | category | flops | bytes accessed | tf_op | source)
XLA Modules:
  0.0 167.2 jit_solution(13244019734323611978)
XLA Ops:
  0.6 163.0 %attn_block.1 = (bf16[128,2048]{1,0:T(8,128)(2,1)}, bf16[128,2048]{1,0:T(8,128)(2,1)}, f32[3072,128]{1,0:T(8,128)}, f32[128,2048]{1,0:T(8,128)}, f32[2,1,2048]{2,1,0:T(1,128)}) custom-call(bf16[128,2048]{1,0:T(8,128)(2,1)} %bitcast.27, bf16[128,2048]{1,0:T(8,128)(2,1)} %bitcast.28, s32[1,128]{1,0:T(1,128)} %pos_hbm.1, f32[1,2048]{1,0:T(1,128)} %bitcast.29, ...), custom_call_target="tpu_custom_call" | custom-call | tf_op jit(solution)/shard_map/attn_block/pallas_call | solution.py:639
  163.6 3.6 %settle.1 = (bf16[128,2048]{1,0:T(8,128)(2,1)}, bf16[128,2048]{1,0:T(8,128)(2,1)}, f32[2048,128]{1,0:T(8,128)}, f32[512,128]{1,0:T(8,128)}, f32[512,128]{1,0:T(8...) custom-call(bf16[128,2048]{1,0:T(8,128)(2,1)} %get-tuple-element.21.out_i, ...), custom_call_target="tpu_custom_call" | custom-call | tf_op jit(solution)/shard_map/settle/pallas_call | solution.py:659

commit v5 on v4

--- a/solution.py
+++ b/solution.py
@@ -30,7 +30,7 @@
     x_hbm, dy_hbm, pos_hbm, gain_hbm, bias_hbm, wq_hbm, wk_hbm, wv_hbm, wo_hbm,
     out_hbm, gx_hbm, gw_hbm, gwo_hbm, gg_hbm,
     hb, dyb, wt, wi, woi, w_far, pos_all, trig,
-    qt, kvt, kv, kvt_far, kv_far, q_far, da_far, bmat, bmat_t, sbuf, dpbuf, mbuf, adq, dkv, dkvt, kv_rv, kv_mine, kv_row,
+    qt, kvt, kv, kvt_far, kv_far, q_far, da_far, bmat, sbuf, dpbuf, mbuf, adq, dkvt, kv_rv, kv_mine, kv_row,
     dwo, dwt, at_st, dqt_st, at_rv, dt_rv, a_nat, d_nat, x_v, dy_own, gb_v, stat, out_v, gg_st, gg_mx, gg_my, gg_rv, gg_out,
     in_sem, far_sem, wo_sem, w_sem, out_sem, loc_sem,
     hzs, hzr, hds, hdr, yzs, yzr, yds, ydr,
@@ -194,7 +194,7 @@
         local(wk_hbm, wt.at[pl.ds(q_rows, kv_w)], w_sem.at[1]),
         local(wv_hbm, wt.at[pl.ds(q_rows + kv_w, kv_w)], w_sem.at[2]),
     ]
-    dkv[...] = jnp.zeros_like(dkv)
+    dkvt[...] = jnp.zeros_like(dkvt)
     dwo[...] = jnp.zeros_like(dwo)
     dwt[...] = jnp.zeros_like(dwt)
     bmat[...] = jnp.zeros_like(bmat)
@@ -286,68 +286,62 @@
     groups = [slice(tile * g, tile * g + tile) for g in range(cols_q // tile)]
 
     def first_part(b, seen, kv_of):
-        def scores(c, at):
+        def both_of(c):
             rows = part_of(c, pair)
-            keys = kv_of(rows)
-            s = dot(keys, bmat[:, at])
-            d_p = dot(keys, bmat[:, cols_q + at.start:cols_q + at.stop])
-            dpbuf[rows, at] = d_p
-            return rows, s, d_p
-
-        begin = []
-        for at in groups:
-            rows, s, d_p = scores(b, at)
-            s = jnp.where(seen(at), s, -1e30)
-            top = jnp.max(s, axis=0, keepdims=True)
-            p = jnp.exp(s - top)
-            sbuf[rows, at] = p
-            mbuf[b, :, at] = top
-            begin += [top, jnp.sum(p, axis=0, keepdims=True), jnp.sum(p * d_p, axis=0, keepdims=True)]
+            both = dot(kv_of(rows), bmat[...])
+            return rows, both[:, 0:cols_q], both[:, cols_q:2 * cols_q]
+
+        rows, s, d_p = both_of(b)
+        s = jnp.where(seen, s, -1e30)
+        top = jnp.max(s, axis=0, keepdims=True)
+        p = jnp.exp(s - top)
+        sbuf[rows, :] = p
+        dpbuf[rows, :] = d_p
+        mbuf[b] = top
 
         def step(c, state):
-            after = []
-            for g, at in enumerate(groups):
-                old, total, weighted = state[3 * g:3 * g + 3]
-                rows, s, d_p = scores(c, at)
-                new = jnp.maximum(old, jnp.max(s, axis=0, keepdims=True))
-                p = jnp.exp(s - new)
-                sbuf[rows, at] = p
-                mbuf[c, :, at] = new
-                keep = jnp.exp(old - new)
-                after += [new, total * keep + jnp.sum(p, axis=0, keepdims=True), weighted * keep + jnp.sum(p * d_p, axis=0, keepdims=True)]
-            return after
-
-        state = lax.fori_loop(0, b, step, begin)
-        stats = []
-        for g in range(len(groups)):
-            top, total, weighted = state[3 * g:3 * g + 3]
-            inv = 1.0 / total
-            stats.append((top, inv, weighted * inv))
-        return stats
+            old, total, weighted = state
+            rows, s, d_p = both_of(c)
+            new = jnp.maximum(old, jnp.max(s, axis=0, keepdims=True))
+            p = jnp.exp(s - new)
+            sbuf[rows, :] = p
+            dpbuf[rows, :] = d_p
+            mbuf[c] = new
+            keep = jnp.exp(old - new)
+            return new, total * keep + jnp.sum(p, axis=0, keepdims=True), weighted * keep + jnp.sum(p * d_p, axis=0, keepdims=True)
+
+        top, total, weighted = lax.fori_loop(0, b, step, (top, jnp.sum(p, axis=0, keepdims=True), jnp.sum(p * d_p, axis=0, keepdims=True)))
+        inv = 1.0 / total
+        return top, inv, weighted * inv
 
     def second_part(b, stats, kvt_of, with_keys):
+        top, inv, row_dot = stats
         adq[...] = jnp.zeros_like(adq)
 
         def step(c, carry):
             rows = part_of(c, pair)
-            grad = None
-            for at, (top, inv, row_dot) in zip(groups, stats):
-                p = sbuf[rows, at] * (jnp.exp(mbuf[c, :, at] - top) * inv)
+            factor = jnp.exp(mbuf[c] - top) * inv
+            d_k = d_v = None
+            for at in groups:
+                p = sbuf[rows, at] * factor[:, at]
                 p_b = p.astype(BF)
-                ds_b = (p * (dpbuf[rows, at] - row_dot)).astype(BF)
+                ds_b = (p * (dpbuf[rows, at] - row_dot[:, at])).astype(BF)
                 adq[0:hd, at] += dot(kvt_of(slice(0, hd), rows), ds_b)
                 adq[hd:hw, at] += dot(kvt_of(slice(hd, hw), rows), p_b)
                 if with_keys:
-                    more = dot(ds_b, bmat_t[at, :]) + dot(p_b, bmat_t[cols_q + at.start:cols_q + at.stop, :])
-                    grad = more if grad is None else grad + more
+                    more_k = dot_t(bmat[0:hd, at], ds_b)
+                    more_v = dot_t(bmat[hd:hw, cols_q + at.start:cols_q + at.stop], p_b)
+                    d_k = more_k if d_k is None else d_k + more_k
+                    d_v = more_v if d_v is None else d_v + more_v
             if with_keys:
-                dkv[rows, :] += grad
+                dkvt[0:hd, rows] += d_k
+                dkvt[hd:hw, rows] += d_v
             return carry
 
         lax.fori_loop(0, b + 1, step, 0)
 
-    lane = lax.broadcasted_iota(jnp.int32, (pair, tile), 1)
-    row = lax.broadcasted_iota(jnp.int32, (pair, tile), 0)
+    lane = lax.broadcasted_iota(jnp.int32, (pair, cols_q), 1)
+    row = lax.broadcasted_iota(jnp.int32, (pair, cols_q), 0)
 
     @pl.loop(0, n_chip)
     def _(k):
@@ -361,9 +355,7 @@
             for head in range(2):
                 at = cols_q + pair * t + tok * head
                 bmat[hd:hw, at:at + tok] = da_t[hd * head:hd * head + hd, tok * t:tok * t + tok]
-        for t in range(2 * cols_q // tok):
-            bmat_t[tok * t:tok * t + tok, :] = bmat[:, tok * t:tok * t + tok].T
-        stats = first_part(b, lambda at: row <= (at.start // pair) * tok + lane % tok, lambda rows: kv[rows, :])
+        stats = first_part(b, row <= (lane // pair) * tok + lane % tok, lambda rows: kv[rows, :])
         ring_service(y_ring, parts * k + parts - 1)
         second_part(b, stats, lambda part, rows: kvt[part, rows], True)
         a_pair = []
@@ -406,8 +398,6 @@
     w_own = local(dwt.at[pl.ds(0, hw), part_of(me, tok)], gw_hbm.at[own_rows], loc_sem.at[0])
     w_own.start()
 
-    for t in range(n_dev):
-        dkvt[:, tok * t:tok * t + tok] = dkv[tok * t:tok * t + tok, :].T
     swap = remote(dkvt.at[part_of(1 - core, hd)], kv_rv, x_s, x_r, mate)
     swap.start()
     store_wo = local(dwo, gwo_hbm, out_sem.at[0])
@@ -453,7 +443,7 @@
         sin_t = trig[chip, quarter:2 * quarter, part_of(core, tok)]
         bmat[0:hd, 0:cols_q] = q_far[f]
         bmat[hd:hw, cols_q:2 * cols_q] = da_far[f]
-        stats = first_part(chip, lambda at: row <= core * tok + lane % tok, lambda rows: kv_far[f, rows, :])
+        stats = first_part(chip, row <= core * tok + lane % tok, lambda rows: kv_far[f, rows, :])
         second_part(chip, stats, lambda part, rows: kvt_far[f, part, rows], False)
         for head in range(4):
             at = slice(tok * head, tok * head + tok)
@@ -606,12 +596,10 @@
             pltpu.VMEM((n_far, hd, 2 * pair), BF),
             pltpu.VMEM((n_far, hd, 2 * pair), BF),
             pltpu.VMEM((hw, 4 * pair), BF),
-            pltpu.VMEM((4 * pair, hw), BF),
             pltpu.VMEM((seq, 2 * pair), F32),
             pltpu.VMEM((seq, 2 * pair), F32),
             pltpu.VMEM((n_chip, 1, 2 * pair), F32),
             pltpu.VMEM((hw, 2 * pair), F32),
-            pltpu.VMEM((seq, hw), F32),
             pltpu.VMEM((hw, seq), F32),
             pltpu.VMEM((hd, seq), F32),
             pltpu.VMEM((n_dev, hd, tok), BF),

time: 167 us -> 167 us (level)
  no operation moved by 1% of the time
where the time goes in v5:
time: 167 us
  Pallas kernels  166 us (99%)
    pallas_call x1, Pallas kernels, device_step(): pl.pallas_call(functools.partial(block_kernel, n_dev, hd, kv_w, NEAR, PAR...  162 us
    pallas_call x1, Pallas kernels, device_step(): pl.pallas_call(functools.partial(settle_kernel, q_w, kv_w), out_shape=(ja...  3.62 us

profile of v5, /device:TPU:21, one launch (start us, length us, event | category | flops | bytes accessed | tf_op | source)
XLA Modules:
  0.0 166.7 jit_solution(5317511298214071002)
XLA Ops:
  0.6 162.4 %attn_block.1 = (bf16[128,2048]{1,0:T(8,128)(2,1)}, bf16[128,2048]{1,0:T(8,128)(2,1)}, f32[3072,128]{1,0:T(8,128)}, f32[128,2048]{1,0:T(8,128)}, f32[2,1,2048]{2,1,0:T(1,128)}) custom-call(bf16[128,2048]{1,0:T(8,128)(2,1)} %bitcast.27, bf16[128,2048]{1,0:T(8,128)(2,1)} %bitcast.28, s32[1,128]{1,0:T(1,128)} %pos_hbm.1, f32[1,2048]{1,0:T(1,128)} %bitcast.29, ...), custom_call_target="tpu_custom_call" | custom-call | tf_op jit(solution)/shard_map/attn_block/pallas_call | solution.py:627
  163.0 3.6 %settle.1 = (bf16[128,2048]{1,0:T(8,128)(2,1)}, bf16[128,2048]{1,0:T(8,128)(2,1)}, f32[2048,128]{1,0:T(8,128)}, f32[512,128]{1,0:T(8,128)}, f32[512,128]{1,0:T(8...) custom-call(bf16[128,2048]{1,0:T(8,128)(2,1)} %get-tuple-element.21.out_i, ...), custom_call_target="tpu_custom_call" | custom-call | tf_op jit(solution)/shard_map/settle/pallas_call | solution.py:647

commit v6 on v5

--- a/solution.py
+++ b/solution.py
@@ -15,6 +15,8 @@
 F32 = jnp.float32
 NEAR = 1
 PARTS = 4
+FIRST = 2
+HELD = 4
 
 
 def dot(lhs, rhs):
@@ -93,25 +95,31 @@
         local(dy_hbm, dyb.at[own], in_sem.at[8]),
         local(dy_hbm, dy_own, in_sem.at[9]),
     ]
+    far_loads = []
     for f in range(n_far):
         far_rows = part_of(ring_origin(2 * near + 1 + f), hd)
         loads.append(local(wk_hbm.at[far_rows], w_far.at[pl.ds(hw * f, hd)], far_sem.at[2 * f]))
         loads.append(local(wv_hbm.at[far_rows], w_far.at[pl.ds(hw * f + hd, hd)], far_sem.at[2 * f + 1]))
         far_wo = part_of(ring_origin(2 * near + 1 + f), 2 * hw)
-        loads.append(local(wo_hbm.at[far_wo], wt.at[pl.ds(2 * hw * f, 2 * hw)], far_sem.at[2 * n_far + f]))
-    for item in loads:
+        far_loads.append(local(wo_hbm.at[far_wo], wt.at[pl.ds(2 * hw * f, 2 * hw)], far_sem.at[2 * n_far + f]))
+    for item in loads + far_loads:
         item.start()
 
     for item in first_loads:
         item.wait()
     gain_one = 1.0 + gb_v[0]
-    x_f = x_v[...].astype(F32)
-    mean = jnp.mean(x_f, axis=-1, keepdims=True)
-    centered = x_f - mean
-    inv_std = lax.rsqrt(jnp.mean(centered * centered, axis=-1, keepdims=True) + EPS)
-    hb[chip, part_of(core, tok), :] = (centered * inv_std * gain_one + gb_v[1]).astype(BF)
-    stat[0] = jnp.broadcast_to(mean, (tok, 128))
-    stat[1] = jnp.broadcast_to(inv_std, (tok, 128))
+    block = 16
+
+    @pl.loop(0, tok // block)
+    def _(i):
+        rows = part_of(i, block)
+        x_f = x_v[rows, :].astype(F32)
+        mean = jnp.mean(x_f, axis=-1, keepdims=True)
+        centered = x_f - mean
+        inv_std = lax.rsqrt(jnp.mean(centered * centered, axis=-1, keepdims=True) + EPS)
+        hb[chip, part_of(core * (tok // block) + i, block), :] = (centered * inv_std * gain_one + gb_v[1]).astype(BF)
+        stat[0, rows, :] = jnp.broadcast_to(mean, (block, 128))
+        stat[1, rows, :] = jnp.broadcast_to(inv_std, (block, 128))
 
     pl.semaphore_wait(barrier, n_dev - 1)
 
@@ -186,7 +194,7 @@
     y_ring = (dyb, yzs, yzr, yds, ydr)
     for item in own_sends(*h_ring):
         item.start()
-    pos_sends = [remote(pos_all.at[me], pos_all.at[me], pos_s.at[step], pos_r.at[step], (me + step) % n_dev) for step in range(1, n_dev)]
+    pos_sends = [remote(pos_all.at[me], pos_all.at[me], pos_s.at[step], pos_r.at[me], (me + step) % n_dev) for step in range(1, n_dev)]
     for item in pos_sends:
         item.start()
     weight_loads = [
@@ -201,30 +209,17 @@
 
     freq = jnp.exp(lax.broadcasted_iota(jnp.int32, (quarter, tok), 0).astype(F32) * (-2.0 * math.log(ROPE_BASE) / (hd // 2)))
 
-    def make_trig(slot):
-        angle = pos_all[slot].astype(F32) * freq
-        trig[slot // 2, 0:quarter, part_of(slot % 2, tok)] = jnp.cos(angle)
-        trig[slot // 2, quarter:2 * quarter, part_of(slot % 2, tok)] = jnp.sin(angle)
-
-    make_trig(me)
-
-    @pl.loop(1, n_dev)
-    def _(step):
-        source = (me + n_dev - step) % n_dev
-        remote(pos_all.at[source], pos_all.at[source], pos_s.at[step], pos_r.at[step], me).wait_recv()
-        make_trig(source)
-
-    for item in loads:
-        item.wait()
-
-    @pl.loop(0, n_far)
-    def _(f):
-        da_t = dot_t(wt[part_of(f, 2 * hw), :], dy_own[...]).astype(BF)
-        for head in range(4):
-            da_far[f, :, tok * head:tok * head + tok] = da_t[hd * head:hd * head + hd]
-
-    for item in weight_loads:
-        item.start()
+    def make_trig(b):
+        for t in range(2):
+            slot = 2 * b + t
+
+            @pl.when(slot != me)
+            def _():
+                remote(pos_all.at[slot], pos_all.at[slot], pos_s.at[0], pos_r.at[slot], me).wait_recv()
+
+            angle = pos_all[slot].astype(F32) * freq
+            trig[b, 0:quarter, tok * t:tok * t + tok] = jnp.cos(angle)
+            trig[b, quarter:2 * quarter, tok * t:tok * t + tok] = jnp.sin(angle)
 
     def turned(val, cos_t, sin_t):
         u = val[0:quarter]
@@ -247,21 +242,31 @@
             for item in own_sends(*y_ring):
                 item.start()
 
-        @pl.when(k == 4)
+        @pl.when(k == 0)
+        def _():
+            for item in loads:
+                item.wait()
+
+        @pl.when(k == 2)
+        def _():
+            for item in far_loads:
+                item.wait()
+
+        @pl.when((k >= 2) & (k < 2 + n_far))
+        def _():
+            f = k - 2
+            da_t = dot_t(wt[part_of(f, 2 * hw), :], dy_own[...]).astype(BF)
+            for head in range(4):
+                da_far[f, :, tok * head:tok * head + tok] = da_t[hd * head:hd * head + hd]
+
+        @pl.when(k == 1 + n_far)
         def _():
             for item in weight_loads:
-                item.wait()
-
-            @pl.loop(0, n_far)
-            def _(f):
-                cos_t = trig[chip, 0:quarter, part_of(core, tok)]
-                sin_t = trig[chip, quarter:2 * quarter, part_of(core, tok)]
-                q_t = dot_t(wt[part_of(ring_origin(2 * near + 1 + f), 2 * hw), :], hb[chip, part_of(core, tok), :])
-                for head in range(4):
-                    q_far[f, :, tok * head:tok * head + tok] = eighth(jnp.concatenate(turned(q_t[hd * head:hd * head + hd], cos_t, sin_t), axis=0))
+                item.start()
 
         b = ring_origin(k)
         ring_mate(h_ring, k, b)
+        make_trig(b)
         place = part_of(b, pair)
         cos_t = trig[b, 0:quarter, :]
         sin_t = trig[b, quarter:2 * quarter, :]
@@ -349,6 +354,21 @@
             ring_service(y_ring, parts * k + turn)
         b = ring_origin(k)
         ring_mate(y_ring, k, b)
+
+        @pl.when(k == 1)
+        def _():
+            for item in weight_loads:
+                item.wait()
+
+        @pl.when((k >= 1) & (k < 1 + n_far))
+        def _():
+            f = k - 1
+            cos_t = trig[chip, 0:quarter, part_of(core, tok)]
+            sin_t = trig[chip, quarter:2 * quarter, part_of(core, tok)]
+            q_t = dot_t(wt[part_of(ring_origin(2 * near + 1 + f), 2 * hw), :], hb[chip, part_of(core, tok), :])
+            for head in range(4):
+                q_far[f, :, tok * head:tok * head + tok] = eighth(jnp.concatenate(turned(q_t[hd * head:hd * head + hd], cos_t, sin_t), axis=0))
+
         da_t = dot_t(woi[...], dyb[b]).astype(BF)
         bmat[0:hd, 0:cols_q] = qt[b]
         for t in range(2):
@@ -389,11 +409,11 @@
             dwo[:, cols] += dot(a_pair, dyb[b, :, cols])
             dwt[0:hw, cols] += dot(dq_pair, hb[b, :, cols])
 
-    far = [ring_origin(k) for k in range(1, n_chip)]
-    targets = [mate] + [2 * c + p for c in far for p in range(2)]
-    near_targets = targets[0:1 + 4 * near]
+    far = [ring_origin(k) for k in range(n_chip - 1, 0, -1)]
+    targets = [2 * c + p for c in far for p in range(2)] + [mate]
+    near_targets = targets[-1 - 4 * near:]
     w_sends = [remote(dwt.at[pl.ds(0, hw), part_of(t, tok)], gw_hbm.at[own_rows], w_s.at[t], w_r.at[me], t) for t in targets]
-    for item in w_sends:
+    for item in w_sends[0:FIRST]:
         item.start()
     w_own = local(dwt.at[pl.ds(0, hw), part_of(me, tok)], gw_hbm.at[own_rows], loc_sem.at[0])
     w_own.start()
@@ -422,7 +442,7 @@
         kv_row[:, cols] = g_b
     dt_rv[g_rows, :] = kv_mine[me]
     kv_sends = [remote(kv_mine.at[t], dt_rv.at[g_rows], kv_s.at[t], kv_r.at[me], t) for t in targets]
-    for item in kv_sends:
+    for item in kv_sends + w_sends[FIRST:]:
         item.start()
     for t in range(width // tile):
         cols = slice(tile * t, tile * t + tile)
@@ -433,7 +453,7 @@
     wk_own = local(dwt.at[pl.ds(hw, hd), part_of(me, tok)], gw_hbm.at[g_rows], loc_sem.at[1])
     wk_own.start()
     wk_sends = [remote(dwt.at[pl.ds(hw, hd), part_of(t, tok)], gw_hbm.at[g_rows], wk_s.at[t], wk_r.at[me], t) for t in targets]
-    for item in wk_sends:
+    for item in wk_sends[0:HELD]:
         item.start()
 
     @pl.loop(0, n_far)
@@ -494,7 +514,7 @@
     gg_my[...] = jnp.where(core == 0, gg_st[0], gg_st[1]) + gg_mx[...]
     gg_rv[chip] = gg_my[...]
     g_sends = [remote(gg_my, gg_rv.at[chip], g_s.at[c], g_r.at[chip], 2 * c + core) for c in far]
-    for item in g_sends:
+    for item in g_sends + wk_sends[HELD:]:
         item.start()
 
     grad_hat = dh[...] * gain_one

time: 167 us -> 157 us (0.940)
  Pallas kernels: 166 us -> 156 us
    pallas_call x1, Pallas kernels: 162 us -> 153 us  [device_step(): pl.pallas_call(functools.partial(block_kernel, n_dev, hd, kv_w, NEAR, PAR...]
where the time goes in v6:
time: 157 us
  Pallas kernels  156 us (99%)
    pallas_call x1, Pallas kernels, device_step(): pl.pallas_call(functools.partial(block_kernel, n_dev, hd, kv_w, NEAR, PAR...  153 us
    pallas_call x1, Pallas kernels, device_step(): pl.pallas_call(functools.partial(settle_kernel, q_w, kv_w), out_shape=(ja...  3.62 us

profile of v6, /device:TPU:21, one launch (start us, length us, event | category | flops | bytes accessed | tf_op | source)
XLA Modules:
  0.0 156.8 jit_solution(17268262525347968865)
XLA Ops:
  0.6 152.5 %attn_block.1 = (bf16[128,2048]{1,0:T(8,128)(2,1)}, bf16[128,2048]{1,0:T(8,128)(2,1)}, f32[3072,128]{1,0:T(8,128)}, f32[128,2048]{1,0:T(8,128)}, f32[2,1,2048]{2,1,0:T(1,128)}) custom-call(bf16[128,2048]{1,0:T(8,128)(2,1)} %bitcast.27, bf16[128,2048]{1,0:T(8,128)(2,1)} %bitcast.28, s32[1,128]{1,0:T(1,128)} %pos_hbm.1, f32[1,2048]{1,0:T(1,128)} %bitcast.29, ...), custom_call_target="tpu_custom_call" | custom-call | tf_op jit(solution)/shard_map/attn_block/pallas_call | solution.py:647
  153.1 3.6 %settle.1 = (bf16[128,2048]{1,0:T(8,128)(2,1)}, bf16[128,2048]{1,0:T(8,128)(2,1)}, f32[2048,128]{1,0:T(8,128)}, f32[512,128]{1,0:T(8,128)}, f32[512,128]{1,0:T(8...) custom-call(bf16[128,2048]{1,0:T(8,128)(2,1)} %get-tuple-element.21.out_i, ...), custom_call_target="tpu_custom_call" | custom-call | tf_op jit(solution)/shard_map/settle/pallas_call | solution.py:667

commit v7 on v6

--- a/solution.py
+++ b/solution.py
@@ -232,9 +232,12 @@
     def keys_values(val, cos_t, sin_t):
         return jnp.concatenate(turned(val[0:hd], cos_t, sin_t) + [val[hd:hw]], axis=0).astype(BF)
 
+    for event in range(2):
+        ring_event(h_ring, jnp.int32(event))
+
     @pl.loop(0, n_chip)
     def _(k):
-        for turn in range(parts):
+        for turn in range(2, parts):
             ring_service(h_ring, parts * k + turn)
 
         @pl.when(k == 5)
@@ -279,6 +282,9 @@
         kv_rot = keys_values(flat[hw:2 * hw], cos_t, sin_t)
         kvt[:, place] = kv_rot
         kv[place, :] = kv_rot.T
+
+        for turn in range(2):
+            ring_service(h_ring, parts * (k + 1) + turn)
 
         @pl.when(b <= chip)
         def _():
@@ -348,9 +354,12 @@
     lane = lax.broadcasted_iota(jnp.int32, (pair, cols_q), 1)
     row = lax.broadcasted_iota(jnp.int32, (pair, cols_q), 0)
 
+    for event in range(2):
+        ring_event(y_ring, jnp.int32(event))
+
     @pl.loop(0, n_chip)
     def _(k):
-        for turn in range(parts - 1):
+        for turn in range(2, parts):
             ring_service(y_ring, parts * k + turn)
         b = ring_origin(k)
         ring_mate(y_ring, k, b)
@@ -376,7 +385,8 @@
                 at = cols_q + pair * t + tok * head
                 bmat[hd:hw, at:at + tok] = da_t[hd * head:hd * head + hd, tok * t:tok * t + tok]
         stats = first_part(b, row <= (lane // pair) * tok + lane % tok, lambda rows: kv[rows, :])
-        ring_service(y_ring, parts * k + parts - 1)
+        for turn in range(2):
+            ring_service(y_ring, parts * (k + 1) + turn)
         second_part(b, stats, lambda part, rows: kvt[part, rows], True)
         a_pair = []
         dq_pair = []

time: 157 us -> 160 us (1.019)
  Pallas kernels: 156 us -> 159 us
    pallas_call x1, Pallas kernels: 153 us -> 156 us  [device_step(): pl.pallas_call(functools.partial(block_kernel, n_dev, hd, kv_w, NEAR, PAR...]
where the time goes in v7:
time: 160 us
  Pallas kernels  159 us (99%)
    pallas_call x1, Pallas kernels, device_step(): pl.pallas_call(functools.partial(block_kernel, n_dev, hd, kv_w, NEAR, PAR...  156 us
    pallas_call x1, Pallas kernels, device_step(): pl.pallas_call(functools.partial(settle_kernel, q_w, kv_w), out_shape=(ja...  3.62 us

profile of v7, /device:TPU:21, one launch (start us, length us, event | category | flops | bytes accessed | tf_op | source)
XLA Modules:
  0.0 160.0 jit_solution(6117651269794397777)
XLA Ops:
  0.6 155.7 %attn_block.1 = (bf16[128,2048]{1,0:T(8,128)(2,1)}, bf16[128,2048]{1,0:T(8,128)(2,1)}, f32[3072,128]{1,0:T(8,128)}, f32[128,2048]{1,0:T(8,128)}, f32[2,1,2048]{2,1,0:T(1,128)}) custom-call(bf16[128,2048]{1,0:T(8,128)(2,1)} %bitcast.27, bf16[128,2048]{1,0:T(8,128)(2,1)} %bitcast.28, s32[1,128]{1,0:T(1,128)} %pos_hbm.1, f32[1,2048]{1,0:T(1,128)} %bitcast.29, ...), custom_call_target="tpu_custom_call" | custom-call | tf_op jit(solution)/shard_map/attn_block/pallas_call | solution.py:657
  156.3 3.6 %settle.1 = (bf16[128,2048]{1,0:T(8,128)(2,1)}, bf16[128,2048]{1,0:T(8,128)(2,1)}, f32[2048,128]{1,0:T(8,128)}, f32[512,128]{1,0:T(8,128)}, f32[512,128]{1,0:T(8...) custom-call(bf16[128,2048]{1,0:T(8,128)(2,1)} %get-tuple-element.21.out_i, ...), custom_call_target="tpu_custom_call" | custom-call | tf_op jit(solution)/shard_map/settle/pallas_call | solution.py:677

commit v8 on v6

--- a/solution.py
+++ b/solution.py
@@ -15,7 +15,7 @@
 F32 = jnp.float32
 NEAR = 1
 PARTS = 4
-FIRST = 2
+FIRST = 1
 HELD = 4
 
 
@@ -32,8 +32,8 @@
     x_hbm, dy_hbm, pos_hbm, gain_hbm, bias_hbm, wq_hbm, wk_hbm, wv_hbm, wo_hbm,
     out_hbm, gx_hbm, gw_hbm, gwo_hbm, gg_hbm,
     hb, dyb, wt, wi, woi, w_far, pos_all, trig,
-    qt, kvt, kv, kvt_far, kv_far, q_far, da_far, bmat, sbuf, dpbuf, mbuf, adq, dkvt, kv_rv, kv_mine, kv_row,
-    dwo, dwt, at_st, dqt_st, at_rv, dt_rv, a_nat, d_nat, x_v, dy_own, gb_v, stat, out_v, gg_st, gg_mx, gg_my, gg_rv, gg_out,
+    qt, kvt, kv, kvt_far, kv_far, da_far, bmat, sbuf, dpbuf, mbuf, adq, dkvt, kv_rv, kv_mine, kv_row,
+    dwo, dwt, at_all, dq_all, at_rv, dt_rv, a_nat, d_nat, x_v, dy_own, gb_v, stat, out_v, gg_st, gg_mx, gg_my, gg_rv, gg_out,
     in_sem, far_sem, wo_sem, w_sem, out_sem, loc_sem,
     hzs, hzr, hds, hdr, yzs, yzr, yds, ydr,
     pos_s, pos_r, a_s, a_r, q_s, q_r, x_s, x_r, kv_s, kv_r, w_s, w_r, wk_s, wk_r, g_s, g_r,
@@ -203,8 +203,6 @@
         local(wv_hbm, wt.at[pl.ds(q_rows + kv_w, kv_w)], w_sem.at[2]),
     ]
     dkvt[...] = jnp.zeros_like(dkvt)
-    dwo[...] = jnp.zeros_like(dwo)
-    dwt[...] = jnp.zeros_like(dwt)
     bmat[...] = jnp.zeros_like(bmat)
 
     freq = jnp.exp(lax.broadcasted_iota(jnp.int32, (quarter, tok), 0).astype(F32) * (-2.0 * math.log(ROPE_BASE) / (hd // 2)))
@@ -348,6 +346,13 @@
     lane = lax.broadcasted_iota(jnp.int32, (pair, cols_q), 1)
     row = lax.broadcasted_iota(jnp.int32, (pair, cols_q), 0)
 
+    def send_rows(slot):
+        cols = part_of(slot, tok)
+        return [
+            remote(dq_all.at[:, cols], dt_rv.at[own_rows], q_s.at[slot], q_r.at[me], slot),
+            remote(at_all.at[:, cols], at_rv.at[own_rows], a_s.at[slot], a_r.at[me], slot),
+        ]
+
     @pl.loop(0, n_chip)
     def _(k):
         for turn in range(parts - 1):
@@ -360,14 +365,16 @@
             for item in weight_loads:
                 item.wait()
 
-        @pl.when((k >= 1) & (k < 1 + n_far))
-        def _():
-            f = k - 1
-            cos_t = trig[chip, 0:quarter, part_of(core, tok)]
-            sin_t = trig[chip, quarter:2 * quarter, part_of(core, tok)]
-            q_t = dot_t(wt[part_of(ring_origin(2 * near + 1 + f), 2 * hw), :], hb[chip, part_of(core, tok), :])
-            for head in range(4):
-                q_far[f, :, tok * head:tok * head + tok] = eighth(jnp.concatenate(turned(q_t[hd * head:hd * head + hd], cos_t, sin_t), axis=0))
+        @pl.when(k == n_chip - 1)
+        def _():
+            for early in range(1 + 2 * near):
+                for t in range(2):
+                    slot = 2 * ring_origin(early) + t
+
+                    @pl.when(slot != me)
+                    def _():
+                        for item in send_rows(slot):
+                            item.start()
 
         da_t = dot_t(woi[...], dyb[b]).astype(BF)
         bmat[0:hd, 0:cols_q] = qt[b]
@@ -378,8 +385,6 @@
         stats = first_part(b, row <= (lane // pair) * tok + lane % tok, lambda rows: kv[rows, :])
         ring_service(y_ring, parts * k + parts - 1)
         second_part(b, stats, lambda part, rows: kvt[part, rows], True)
-        a_pair = []
-        dq_pair = []
         for t in range(2):
             slot = 2 * b + t
             lanes = [slice(pair * t + tok * head, pair * t + tok * head + tok) for head in range(2)]
@@ -387,46 +392,35 @@
             cos_t = trig[b, 0:quarter, tok * t:tok * t + tok]
             sin_t = trig[b, quarter:2 * quarter, tok * t:tok * t + tok]
             dq_t = jnp.concatenate([piece for at in lanes for piece in turned(adq[0:hd, at] * scale, cos_t, -sin_t)], axis=0).astype(BF)
-            a_pair.append(a_t)
-            dq_pair.append(dq_t)
+            at_all[:, part_of(slot, tok)] = a_t
+            dq_all[:, part_of(slot, tok)] = dq_t
 
             @pl.when(slot == me)
             def _():
                 at_rv[own_rows, :] = a_t
                 dt_rv[own_rows, :] = dq_t
 
-            @pl.when((slot != me) & (k < 1 + 2 * near))
-            def _():
-                at_st[slot] = a_t
-                dqt_st[slot] = dq_t
-                remote(dqt_st.at[slot], dt_rv.at[own_rows], q_s.at[slot], q_r.at[me], slot).start()
-                remote(at_st.at[slot], at_rv.at[own_rows], a_s.at[slot], a_r.at[me], slot).start()
-
-        a_pair = jnp.concatenate(a_pair, axis=1)
-        dq_pair = jnp.concatenate(dq_pair, axis=1)
-        for t in range(width // tile):
-            cols = slice(tile * t, tile * t + tile)
-            dwo[:, cols] += dot(a_pair, dyb[b, :, cols])
-            dwt[0:hw, cols] += dot(dq_pair, hb[b, :, cols])
-
     far = [ring_origin(k) for k in range(n_chip - 1, 0, -1)]
     targets = [2 * c + p for c in far for p in range(2)] + [mate]
     near_targets = targets[-1 - 4 * near:]
-    w_sends = [remote(dwt.at[pl.ds(0, hw), part_of(t, tok)], gw_hbm.at[own_rows], w_s.at[t], w_r.at[me], t) for t in targets]
-    for item in w_sends[0:FIRST]:
-        item.start()
-    w_own = local(dwt.at[pl.ds(0, hw), part_of(me, tok)], gw_hbm.at[own_rows], loc_sem.at[0])
-    w_own.start()
-
     swap = remote(dkvt.at[part_of(1 - core, hd)], kv_rv, x_s, x_r, mate)
     swap.start()
-    store_wo = local(dwo, gwo_hbm, out_sem.at[0])
-    store_wo.start()
-
-    finish_ring(y_ring)
-    wo_loads = [local(wo_hbm.at[pl.ds(pair * t, pair)], dyb.at[t], wo_sem.at[t]) for t in range(n_chip)]
-    for item in wo_loads:
-        item.start()
+    w_sends = [remote(dwt.at[pl.ds(0, hw), part_of(t, tok)], gw_hbm.at[own_rows], w_s.at[t], w_r.at[me], t) for t in targets]
+
+    def columns(rows_all, buf, cols):
+        acc = jnp.zeros((rows_all.shape[0], tile), F32)
+        for s in range(n_chip):
+            acc += dot(rows_all[:, pair * s:pair * s + pair], buf[s, :, cols])
+        return acc
+
+    def q_columns(i):
+        cols = part_of(far[i] if i < n_chip - 1 else chip, pair)
+        dwt[0:hw, cols] = columns(dq_all, hb, cols)
+        for item in w_sends[max(2 * i - 2, 0):2 * i]:
+            item.start()
+
+    for i in range(FIRST + 1):
+        q_columns(i)
 
     swap.wait_recv()
     mine = part_of(core, hd)
@@ -442,18 +436,30 @@
         kv_row[:, cols] = g_b
     dt_rv[g_rows, :] = kv_mine[me]
     kv_sends = [remote(kv_mine.at[t], dt_rv.at[g_rows], kv_s.at[t], kv_r.at[me], t) for t in targets]
-    for item in kv_sends + w_sends[FIRST:]:
-        item.start()
+    for item in kv_sends:
+        item.start()
+    for i in range(FIRST + 1, n_chip):
+        q_columns(i)
+    w_sends[-1].start()
+    w_own = local(dwt.at[pl.ds(0, hw), part_of(me, tok)], gw_hbm.at[own_rows], loc_sem.at[0])
+    w_own.start()
     for t in range(width // tile):
         cols = slice(tile * t, tile * t + tile)
-        acc = jnp.zeros((hd, tile), F32)
-        for s in range(n_chip):
-            acc += dot(kv_row[:, pair * s:pair * s + pair], hb[s, :, cols])
-        dwt[hw:hw + hd, cols] = acc
+        dwt[hw:hw + hd, cols] = columns(kv_row, hb, cols)
     wk_own = local(dwt.at[pl.ds(hw, hd), part_of(me, tok)], gw_hbm.at[g_rows], loc_sem.at[1])
     wk_own.start()
     wk_sends = [remote(dwt.at[pl.ds(hw, hd), part_of(t, tok)], gw_hbm.at[g_rows], wk_s.at[t], wk_r.at[me], t) for t in targets]
     for item in wk_sends[0:HELD]:
+        item.start()
+
+    for t in range(width // tile):
+        cols = slice(tile * t, tile * t + tile)
+        dwo[:, cols] = columns(at_all, dyb, cols)
+    store_wo = local(dwo, gwo_hbm, out_sem.at[0])
+    store_wo.start()
+    finish_ring(y_ring)
+    wo_loads = [local(wo_hbm.at[pl.ds(pair * t, pair)], dyb.at[t], wo_sem.at[t]) for t in range(n_chip)]
+    for item in wo_loads:
         item.start()
 
     @pl.loop(0, n_far)
@@ -461,7 +467,9 @@
         c_far = ring_origin(2 * near + 1 + f)
         cos_t = trig[chip, 0:quarter, part_of(core, tok)]
         sin_t = trig[chip, quarter:2 * quarter, part_of(core, tok)]
-        bmat[0:hd, 0:cols_q] = q_far[f]
+        q_t = dot_t(wt[part_of(c_far, 2 * hw), :], hb[chip, part_of(core, tok), :])
+        for head in range(4):
+            bmat[0:hd, tok * head:tok * head + tok] = eighth(jnp.concatenate(turned(q_t[hd * head:hd * head + hd], cos_t, sin_t), axis=0))
         bmat[hd:hw, cols_q:2 * cols_q] = da_far[f]
         stats = first_part(chip, row <= core * tok + lane % tok, lambda rows: kv_far[f, rows, :])
         second_part(chip, stats, lambda part, rows: kvt_far[f, part, rows], False)
@@ -472,7 +480,7 @@
             dt_rv[place, :] = jnp.concatenate(turned(adq[0:hd, at] * scale, cos_t, -sin_t), axis=0).astype(BF)
 
     for t in near_targets:
-        remote(at_st.at[0], at_rv.at[part_of(t, hw)], a_s.at[t], a_r.at[t], t).wait_recv()
+        remote(at_all.at[:, pl.ds(0, tok)], at_rv.at[part_of(t, hw)], a_s.at[t], a_r.at[t], t).wait_recv()
     for item in wo_loads:
         item.wait()
     for t in range(q_rows // tok):
@@ -490,7 +498,7 @@
         return pl.ds(pl.multiple_of(q_rows + (t % 2) * kv_w + (t // 2) * hd, hd), hd)
 
     for t in near_targets:
-        remote(dqt_st.at[0], dt_rv.at[part_of(t, hw)], q_s.at[t], q_r.at[t], t).wait_recv()
+        remote(dq_all.at[:, pl.ds(0, tok)], dt_rv.at[part_of(t, hw)], q_s.at[t], q_r.at[t], t).wait_recv()
     for t in targets:
         remote(kv_mine.at[0], dt_rv.at[kv_place(t)], kv_s.at[t], kv_r.at[t], t).wait_recv()
     swap.wait_send()
@@ -542,8 +550,8 @@
     for item in pos_sends + [g_swap, g_swap_out]:
         item.wait_send()
     for t in near_targets:
-        remote(at_st.at[0], at_rv.at[pl.ds(0, hw)], a_s.at[t], a_r.at[t], t).wait_send()
-        remote(dqt_st.at[0], dt_rv.at[pl.ds(0, hw)], q_s.at[t], q_r.at[t], t).wait_send()
+        remote(at_all.at[:, pl.ds(0, tok)], at_rv.at[pl.ds(0, hw)], a_s.at[t], a_r.at[t], t).wait_send()
+        remote(dq_all.at[:, pl.ds(0, tok)], dt_rv.at[pl.ds(0, hw)], q_s.at[t], q_r.at[t], t).wait_send()
     for item in kv_sends + w_sends + g_sends + wk_sends:
         item.wait_send()
     for t in targets:
@@ -614,7 +622,6 @@
             pltpu.VMEM((n_far, hw, seq), BF),
             pltpu.VMEM((n_far, seq, hw), BF),
             pltpu.VMEM((n_far, hd, 2 * pair), BF),
-            pltpu.VMEM((n_far, hd, 2 * pair), BF),
             pltpu.VMEM((hw, 4 * pair), BF),
             pltpu.VMEM((seq, 2 * pair), F32),
             pltpu.VMEM((seq, 2 * pair), F32),
@@ -626,8 +633,8 @@
             pltpu.VMEM((hd, seq), BF),
             pltpu.VMEM((hw, width), F32),
             pltpu.VMEM((hw + hd, width), F32),
-            pltpu.VMEM((n_dev, hw, tok), BF),
-            pltpu.VMEM((n_dev, hw, tok), BF),
+            pltpu.VMEM((hw, seq), BF),
+            pltpu.VMEM((hw, seq), BF),
             pltpu.VMEM((q_w, tok), BF),
             pltpu.VMEM((n_rows, tok), BF),
             pltpu.VMEM((tok, q_w), BF),

time: 157 us -> 154 us (0.981)
  Pallas kernels: 156 us -> 153 us
    pallas_call x1, Pallas kernels: 153 us -> 149 us  [device_step(): pl.pallas_call(functools.partial(block_kernel, n_dev, hd, kv_w, NEAR, PAR...]
where the time goes in v8:
time: 154 us
  Pallas kernels  153 us (99%)
    pallas_call x1, Pallas kernels, device_step(): pl.pallas_call(functools.partial(block_kernel, n_dev, hd, kv_w, NEAR, PAR...  149 us
    pallas_call x1, Pallas kernels, device_step(): pl.pallas_call(functools.partial(settle_kernel, q_w, kv_w), out_shape=(ja...  3.62 us

profile of v8, /device:TPU:21, one launch (start us, length us, event | category | flops | bytes accessed | tf_op | source)
XLA Modules:
  0.0 153.7 jit_solution(12905381473490314918)
XLA Ops:
  0.6 149.3 %attn_block.1 = (bf16[128,2048]{1,0:T(8,128)(2,1)}, bf16[128,2048]{1,0:T(8,128)(2,1)}, f32[3072,128]{1,0:T(8,128)}, f32[128,2048]{1,0:T(8,128)}, f32[2,1,2048]{2,1,0:T(1,128)}) custom-call(bf16[128,2048]{1,0:T(8,128)(2,1)} %bitcast.27, bf16[128,2048]{1,0:T(8,128)(2,1)} %bitcast.28, s32[1,128]{1,0:T(1,128)} %pos_hbm.1, f32[1,2048]{1,0:T(1,128)} %bitcast.29, ...), custom_call_target="tpu_custom_call" | custom-call | tf_op jit(solution)/shard_map/attn_block/pallas_call | solution.py:654
  149.9 3.6 %settle.1 = (bf16[128,2048]{1,0:T(8,128)(2,1)}, bf16[128,2048]{1,0:T(8,128)(2,1)}, f32[2048,128]{1,0:T(8,128)}, f32[512,128]{1,0:T(8,128)}, f32[512,128]{1,0:T(8...) custom-call(bf16[128,2048]{1,0:T(8,128)(2,1)} %get-tuple-element.21.out_i, ...), custom_call_target="tpu_custom_call" | custom-call | tf_op jit(solution)/shard_map/settle/pallas_call | solution.py:674

commit v9 on v8

--- a/solution.py
+++ b/solution.py
@@ -32,7 +32,7 @@
     x_hbm, dy_hbm, pos_hbm, gain_hbm, bias_hbm, wq_hbm, wk_hbm, wv_hbm, wo_hbm,
     out_hbm, gx_hbm, gw_hbm, gwo_hbm, gg_hbm,
     hb, dyb, wt, wi, woi, w_far, pos_all, trig,
-    qt, kvt, kv, kvt_far, kv_far, da_far, bmat, sbuf, dpbuf, mbuf, adq, dkvt, kv_rv, kv_mine, kv_row,
+    qt, kvt, kv, kvt_far, kv_far, bmat_far, stat_far, bmat, sbuf, dpbuf, mbuf, adq, dkvt, kv_rv, kv_mine, kv_row,
     dwo, dwt, at_all, dq_all, at_rv, dt_rv, a_nat, d_nat, x_v, dy_own, gb_v, stat, out_v, gg_st, gg_mx, gg_my, gg_rv, gg_out,
     in_sem, far_sem, wo_sem, w_sem, out_sem, loc_sem,
     hzs, hzr, hds, hdr, yzs, yzr, yds, ydr,
@@ -102,6 +102,7 @@
         loads.append(local(wv_hbm.at[far_rows], w_far.at[pl.ds(hw * f + hd, hd)], far_sem.at[2 * f + 1]))
         far_wo = part_of(ring_origin(2 * near + 1 + f), 2 * hw)
         far_loads.append(local(wo_hbm.at[far_wo], wt.at[pl.ds(2 * hw * f, 2 * hw)], far_sem.at[2 * n_far + f]))
+        far_loads.append(local(wq_hbm.at[far_wo], wt.at[pl.ds(2 * hw * (n_far + f), 2 * hw)], far_sem.at[3 * n_far + f]))
     for item in loads + far_loads:
         item.start()
 
@@ -204,6 +205,7 @@
     ]
     dkvt[...] = jnp.zeros_like(dkvt)
     bmat[...] = jnp.zeros_like(bmat)
+    bmat_far[...] = jnp.zeros_like(bmat_far)
 
     freq = jnp.exp(lax.broadcasted_iota(jnp.int32, (quarter, tok), 0).astype(F32) * (-2.0 * math.log(ROPE_BASE) / (hd // 2)))
 
@@ -230,6 +232,10 @@
     def keys_values(val, cos_t, sin_t):
         return jnp.concatenate(turned(val[0:hd], cos_t, sin_t) + [val[hd:hw]], axis=0).astype(BF)
 
+    lane = lax.broadcasted_iota(jnp.int32, (pair, cols_q), 1)
+    row = lax.broadcasted_iota(jnp.int32, (pair, cols_q), 0)
+    seen_far = row <= core * tok + lane % tok
+
     @pl.loop(0, n_chip)
     def _(k):
         for turn in range(parts):
@@ -245,26 +251,30 @@
             for item in loads:
                 item.wait()
 
-        @pl.when(k == 2)
-        def _():
-            for item in far_loads:
-                item.wait()
-
-        @pl.when((k >= 2) & (k < 2 + n_far))
-        def _():
-            f = k - 2
-            da_t = dot_t(wt[part_of(f, 2 * hw), :], dy_own[...]).astype(BF)
-            for head in range(4):
-                da_far[f, :, tok * head:tok * head + tok] = da_t[hd * head:hd * head + hd]
-
-        @pl.when(k == 1 + n_far)
-        def _():
-            for item in weight_loads:
-                item.start()
-
         b = ring_origin(k)
         ring_mate(h_ring, k, b)
         make_trig(b)
+
+        @pl.when(k == 0)
+        def _():
+            for item in far_loads:
+                item.wait()
+            cos_t = trig[chip, 0:quarter, part_of(core, tok)]
+            sin_t = trig[chip, quarter:2 * quarter, part_of(core, tok)]
+
+            @pl.loop(0, n_far)
+            def _(f):
+                da_t = dot_t(wt[part_of(f, 2 * hw), :], dy_own[...]).astype(BF)
+                q_t = dot_t(wt[part_of(n_far + f, 2 * hw), :], hb[chip, part_of(core, tok), :])
+                for head in range(4):
+                    part = slice(hd * head, hd * head + hd)
+                    at = tok * head
+                    bmat_far[f, 0:hd, at:at + tok] = eighth(jnp.concatenate(turned(q_t[part], cos_t, sin_t), axis=0))
+                    bmat_far[f, hd:hw, cols_q + at:cols_q + at + tok] = da_t[part]
+
+            for item in weight_loads:
+                item.start()
+
         place = part_of(b, pair)
         cos_t = trig[b, 0:quarter, :]
         sin_t = trig[b, quarter:2 * quarter, :]
@@ -286,15 +296,40 @@
                 kvt_far[f, :, place] = far_rot
                 kv_far[f, place, :] = far_rot.T
 
+            @pl.loop(0, n_far)
+            def _(f):
+                both = dot(kv_far[f, place, :], bmat_far[f])
+                d_p = both[:, cols_q:2 * cols_q]
+
+                @pl.when(k == 0)
+                def _():
+                    s = jnp.where(seen_far, both[:, 0:cols_q], -1e30)
+                    top = jnp.max(s, axis=0, keepdims=True)
+                    p = jnp.exp(s - top)
+                    stat_far[f, 0] = top
+                    stat_far[f, 1] = jnp.sum(p, axis=0, keepdims=True)
+                    stat_far[f, 2] = jnp.sum(p * d_p, axis=0, keepdims=True)
+
+                @pl.when(k > 0)
+                def _():
+                    s = both[:, 0:cols_q]
+                    old = stat_far[f, 0]
+                    new = jnp.maximum(old, jnp.max(s, axis=0, keepdims=True))
+                    p = jnp.exp(s - new)
+                    keep = jnp.exp(old - new)
+                    stat_far[f, 0] = new
+                    stat_far[f, 1] = stat_far[f, 1] * keep + jnp.sum(p, axis=0, keepdims=True)
+                    stat_far[f, 2] = stat_far[f, 2] * keep + jnp.sum(p * d_p, axis=0, keepdims=True)
+
     groups = [slice(tile * g, tile * g + tile) for g in range(cols_q // tile)]
 
-    def first_part(b, seen, kv_of):
-        def both_of(c):
-            rows = part_of(c, pair)
-            both = dot(kv_of(rows), bmat[...])
-            return rows, both[:, 0:cols_q], both[:, cols_q:2 * cols_q]
-
-        rows, s, d_p = both_of(b)
+    def first_part(b, seen):
+        def both_of(rows):
+            both = dot(kv[rows, :], bmat[...])
+            return both[:, 0:cols_q], both[:, cols_q:2 * cols_q]
+
+        rows = part_of(b, pair)
+        s, d_p = both_of(rows)
         s = jnp.where(seen, s, -1e30)
         top = jnp.max(s, axis=0, keepdims=True)
         p = jnp.exp(s - top)
@@ -302,22 +337,26 @@
         dpbuf[rows, :] = d_p
         mbuf[b] = top
 
-        def step(c, state):
+        def step(c, state, chunks=1):
             old, total, weighted = state
-            rows, s, d_p = both_of(c)
+            rows = part_of(c, chunks * pair)
+            s, d_p = both_of(rows)
             new = jnp.maximum(old, jnp.max(s, axis=0, keepdims=True))
             p = jnp.exp(s - new)
             sbuf[rows, :] = p
             dpbuf[rows, :] = d_p
-            mbuf[c] = new
+            for i in range(chunks):
+                mbuf[chunks * c + i] = new
             keep = jnp.exp(old - new)
             return new, total * keep + jnp.sum(p, axis=0, keepdims=True), weighted * keep + jnp.sum(p * d_p, axis=0, keepdims=True)
 
-        top, total, weighted = lax.fori_loop(0, b, step, (top, jnp.sum(p, axis=0, keepdims=True), jnp.sum(p * d_p, axis=0, keepdims=True)))
+        state = (top, jnp.sum(p, axis=0, keepdims=True), jnp.sum(p * d_p, axis=0, keepdims=True))
+        state = lax.fori_loop(0, b // 2, functools.partial(step, chunks=2), state)
+        top, total, weighted = lax.fori_loop(2 * (b // 2), b, step, state)
         inv = 1.0 / total
         return top, inv, weighted * inv
 
-    def second_part(b, stats, kvt_of, with_keys):
+    def second_part(b, stats):
         top, inv, row_dot = stats
         adq[...] = jnp.zeros_like(adq)
 
@@ -329,22 +368,18 @@
                 p = sbuf[rows, at] * factor[:, at]
                 p_b = p.astype(BF)
                 ds_b = (p * (dpbuf[rows, at] - row_dot[:, at])).astype(BF)
-                adq[0:hd, at] += dot(kvt_of(slice(0, hd), rows), ds_b)
-                adq[hd:hw, at] += dot(kvt_of(slice(hd, hw), rows), p_b)
-                if with_keys:
-                    more_k = dot_t(bmat[0:hd, at], ds_b)
-                    more_v = dot_t(bmat[hd:hw, cols_q + at.start:cols_q + at.stop], p_b)
-                    d_k = more_k if d_k is None else d_k + more_k
-                    d_v = more_v if d_v is None else d_v + more_v
-            if with_keys:
-                dkvt[0:hd, rows] += d_k
-                dkvt[hd:hw, rows] += d_v
+                adq[0:hd, at] += dot(kvt[0:hd, rows], ds_b)
+                adq[hd:hw, at] += dot(kvt[hd:hw, rows], p_b)
+                more_k = dot_t(bmat[0:hd, at], ds_b)
+                more_v = dot_t(bmat[hd:hw, cols_q + at.start:cols_q + at.stop], p_b)
+                d_k = more_k if d_k is None else d_k + more_k
+                d_v = more_v if d_v is None else d_v + more_v
+            dkvt[0:hd, rows] += d_k
+            dkvt[hd:hw, rows] += d_v
             return carry
 
         lax.fori_loop(0, b + 1, step, 0)
 
-    lane = lax.broadcasted_iota(jnp.int32, (pair, cols_q), 1)
-    row = lax.broadcasted_iota(jnp.int32, (pair, cols_q), 0)
 
     def send_rows(slot):
         cols = part_of(slot, tok)
@@ -382,9 +417,9 @@
             for head in range(2):
                 at = cols_q + pair * t + tok * head
                 bmat[hd:hw, at:at + tok] = da_t[hd * head:hd * head + hd, tok * t:tok * t + tok]
-        stats = first_part(b, row <= (lane // pair) * tok + lane % tok, lambda rows: kv[rows, :])
+        stats = first_part(b, row <= (lane // pair) * tok + lane % tok)
         ring_service(y_ring, parts * k + parts - 1)
-        second_part(b, stats, lambda part, rows: kvt[part, rows], True)
+        second_part(b, stats)
         for t in range(2):
             slot = 2 * b + t
             lanes = [slice(pair * t + tok * head, pair * t + tok * head + tok) for head in range(2)]
@@ -467,12 +502,36 @@
         c_far = ring_origin(2 * near + 1 + f)
         cos_t = trig[chip, 0:quarter, part_of(core, tok)]
         sin_t = trig[chip, quarter:2 * quarter, part_of(core, tok)]
-        q_t = dot_t(wt[part_of(c_far, 2 * hw), :], hb[chip, part_of(core, tok), :])
-        for head in range(4):
-            bmat[0:hd, tok * head:tok * head + tok] = eighth(jnp.concatenate(turned(q_t[hd * head:hd * head + hd], cos_t, sin_t), axis=0))
-        bmat[hd:hw, cols_q:2 * cols_q] = da_far[f]
-        stats = first_part(chip, row <= core * tok + lane % tok, lambda rows: kv_far[f, rows, :])
-        second_part(chip, stats, lambda part, rows: kvt_far[f, part, rows], False)
+        top = stat_far[f, 0]
+        inv = 1.0 / stat_far[f, 1]
+        row_dot = stat_far[f, 2] * inv
+
+        def add_chunk(c, diagonal, chunks=1):
+            rows = part_of(c, chunks * pair)
+            for at in groups:
+                keys = kv_far[f, rows, :]
+                s = dot(keys, bmat_far[f, :, at])
+                d_p = dot(keys, bmat_far[f, :, cols_q + at.start:cols_q + at.stop])
+                if diagonal:
+                    s = jnp.where(seen_far[:, at], s, -1e30)
+                p = jnp.exp(s - top[:, at]) * inv[:, at]
+                p_b = p.astype(BF)
+                ds_b = (p * (d_p - row_dot[:, at])).astype(BF)
+                d_q = dot(kvt_far[f, 0:hd, rows], ds_b)
+                d_a = dot(kvt_far[f, hd:hw, rows], p_b)
+                adq[0:hd, at] = d_q if diagonal else adq[0:hd, at] + d_q
+                adq[hd:hw, at] = d_a if diagonal else adq[hd:hw, at] + d_a
+
+        add_chunk(chip, True)
+
+        @pl.loop(0, chip // 2)
+        def _(c):
+            add_chunk(c, False, 2)
+
+        @pl.when(chip % 2 == 1)
+        def _():
+            add_chunk(chip - 1, False)
+
         for head in range(4):
             at = slice(tok * head, tok * head + tok)
             place = pl.ds(pl.multiple_of(c_far * 2 * hw + hd * head, hd), hd)
@@ -621,7 +680,8 @@
             pltpu.VMEM((seq, hw), BF),
             pltpu.VMEM((n_far, hw, seq), BF),
             pltpu.VMEM((n_far, seq, hw), BF),
-            pltpu.VMEM((n_far, hd, 2 * pair), BF),
+            pltpu.VMEM((n_far, hw, 4 * pair), BF),
+            pltpu.VMEM((n_far, 3, 1, 2 * pair), F32),
             pltpu.VMEM((hw, 4 * pair), BF),
             pltpu.VMEM((seq, 2 * pair), F32),
             pltpu.VMEM((seq, 2 * pair), F32),
@@ -649,7 +709,7 @@
             pltpu.VMEM((1, width), F32),
             pltpu.VMEM((n_chip, 1, width), F32),
             pltpu.VMEM((2, 1, width), F32),
-            dma((10,)), dma((3 * n_far,)), dma((n_chip,)), dma((3,)), dma((4,)), dma((2,)),
+            dma((10,)), dma((4 * n_far,)), dma((n_chip,)), dma((3,)), dma((4,)), dma((2,)),
         ] + [dma((9 * PARTS,)), dma((7 * PARTS,)), dma((8 * PARTS,)), dma((8 * PARTS,))] * 2 + [dma((n_dev,))] * 6 + [dma] * 2 + [dma((n_dev,))] * 8
         out, gx, gw, gwo, gg = pl.pallas_call(
             functools.partial(block_kernel, n_dev, hd, kv_w, NEAR, PARTS),

time: 154 us -> 155 us (level)
  no operation moved by 1% of the time
where the time goes in v9:
time: 155 us
  Pallas kernels  154 us (99%)
    pallas_call x1, Pallas kernels, device_step(): pl.pallas_call(functools.partial(block_kernel, n_dev, hd, kv_w, NEAR, PAR...  151 us
    pallas_call x1, Pallas kernels, device_step(): pl.pallas_call(functools.partial(settle_kernel, q_w, kv_w), out_shape=(ja...  3.62 us

profile of v9, /device:TPU:21, one launch (start us, length us, event | category | flops | bytes accessed | tf_op | source)
XLA Modules:
  0.0 155.2 jit_solution(6641989968237531991)
XLA Ops:
  0.6 150.8 %attn_block.1 = (bf16[128,2048]{1,0:T(8,128)(2,1)}, bf16[128,2048]{1,0:T(8,128)(2,1)}, f32[3072,128]{1,0:T(8,128)}, f32[128,2048]{1,0:T(8,128)}, f32[2,1,2048]{2,1,0:T(1,128)}) custom-call(bf16[128,2048]{1,0:T(8,128)(2,1)} %bitcast.27, bf16[128,2048]{1,0:T(8,128)(2,1)} %bitcast.28, s32[1,128]{1,0:T(1,128)} %pos_hbm.1, f32[1,2048]{1,0:T(1,128)} %bitcast.29, ...), custom_call_target="tpu_custom_call" | custom-call | tf_op jit(solution)/shard_map/attn_block/pallas_call | solution.py:714
  151.4 3.6 %settle.1 = (bf16[128,2048]{1,0:T(8,128)(2,1)}, bf16[128,2048]{1,0:T(8,128)(2,1)}, f32[2048,128]{1,0:T(8,128)}, f32[512,128]{1,0:T(8,128)}, f32[512,128]{1,0:T(8...) custom-call(bf16[128,2048]{1,0:T(8,128)(2,1)} %get-tuple-element.21.out_i, ...), custom_call_target="tpu_custom_call" | custom-call | tf_op jit(solution)/shard_map/settle/pallas_call | solution.py:734

commit v10 on v9

--- a/solution.py
+++ b/solution.py
@@ -388,10 +388,16 @@
             remote(at_all.at[:, cols], at_rv.at[own_rows], a_s.at[slot], a_r.at[me], slot),
         ]
 
+    for event in range(2):
+        ring_event(y_ring, jnp.int32(event))
+
     @pl.loop(0, n_chip)
     def _(k):
-        for turn in range(parts - 1):
-            ring_service(y_ring, parts * k + turn)
+        @pl.when(k % 2 == 1)
+        def _():
+            for turn in range(2, parts):
+                ring_service(y_ring, parts * k + turn)
+
         b = ring_origin(k)
         ring_mate(y_ring, k, b)
 
@@ -418,7 +424,8 @@
                 at = cols_q + pair * t + tok * head
                 bmat[hd:hw, at:at + tok] = da_t[hd * head:hd * head + hd, tok * t:tok * t + tok]
         stats = first_part(b, row <= (lane // pair) * tok + lane % tok)
-        ring_service(y_ring, parts * k + parts - 1)
+        for turn in range(2):
+            ring_service(y_ring, parts * k + 2 + 2 * (k % 2) + turn)
         second_part(b, stats)
         for t in range(2):
             slot = 2 * b + t
@@ -434,6 +441,11 @@
             def _():
                 at_rv[own_rows, :] = a_t
                 dt_rv[own_rows, :] = dq_t
+
+        @pl.when(k % 2 == 0)
+        def _():
+            for turn in range(2):
+                ring_service(y_ring, parts * (k + 1) + turn)
 
     far = [ring_origin(k) for k in range(n_chip - 1, 0, -1)]
     targets = [2 * c + p for c in far for p in range(2)] + [mate]

time: 155 us -> 154 us (level)
  no operation moved by 1% of the time
where the time goes in v10:
time: 154 us
  Pallas kernels  153 us (99%)
    pallas_call x1, Pallas kernels, device_step(): pl.pallas_call(functools.partial(block_kernel, n_dev, hd, kv_w, NEAR, PAR...  150 us
    pallas_call x1, Pallas kernels, device_step(): pl.pallas_call(functools.partial(settle_kernel, q_w, kv_w), out_shape=(ja...  3.62 us

profile of v10, /device:TPU:21, one launch (start us, length us, event | category | flops | bytes accessed | tf_op | source)
XLA Modules:
  0.0 154.3 jit_solution(5343713678132541022)
XLA Ops:
  0.6 149.9 %attn_block.1 = (bf16[128,2048]{1,0:T(8,128)(2,1)}, bf16[128,2048]{1,0:T(8,128)(2,1)}, f32[3072,128]{1,0:T(8,128)}, f32[128,2048]{1,0:T(8,128)}, f32[2,1,2048]{2,1,0:T(1,128)}) custom-call(bf16[128,2048]{1,0:T(8,128)(2,1)} %bitcast.27, bf16[128,2048]{1,0:T(8,128)(2,1)} %bitcast.28, s32[1,128]{1,0:T(1,128)} %pos_hbm.1, f32[1,2048]{1,0:T(1,128)} %bitcast.29, ...), custom_call_target="tpu_custom_call" | custom-call | tf_op jit(solution)/shard_map/attn_block/pallas_call | solution.py:726
  150.5 3.6 %settle.1 = (bf16[128,2048]{1,0:T(8,128)(2,1)}, bf16[128,2048]{1,0:T(8,128)(2,1)}, f32[2048,128]{1,0:T(8,128)}, f32[512,128]{1,0:T(8,128)}, f32[512,128]{1,0:T(8...) custom-call(bf16[128,2048]{1,0:T(8,128)(2,1)} %get-tuple-element.21.out_i, ...), custom_call_target="tpu_custom_call" | custom-call | tf_op jit(solution)/shard_map/settle/pallas_call | solution.py:746

commit v11 on v10

--- a/solution.py
+++ b/solution.py
@@ -65,6 +65,9 @@
     def part_of(i, size):
         return pl.ds(pl.multiple_of(i * size, size), size)
 
+    def once(cond):
+        return pl.loop(0, jnp.where(cond, 1, 0))
+
     def ring_steps(k):
         step = (k + 1) // 2
         return step, k % 2
@@ -206,6 +209,10 @@
     dkvt[...] = jnp.zeros_like(dkvt)
     bmat[...] = jnp.zeros_like(bmat)
     bmat_far[...] = jnp.zeros_like(bmat_far)
+    for f in range(n_far):
+        stat_far[f, 0] = jnp.full((1, cols_q), -3e38, F32)
+        stat_far[f, 1] = jnp.zeros((1, cols_q), F32)
+        stat_far[f, 2] = jnp.zeros((1, cols_q), F32)
 
     freq = jnp.exp(lax.broadcasted_iota(jnp.int32, (quarter, tok), 0).astype(F32) * (-2.0 * math.log(ROPE_BASE) / (hd // 2)))
 
@@ -241,13 +248,13 @@
         for turn in range(parts):
             ring_service(h_ring, parts * k + turn)
 
-        @pl.when(k == 5)
-        def _():
+        @once(k == 5)
+        def _(_):
             for item in own_sends(*y_ring):
                 item.start()
 
-        @pl.when(k == 0)
-        def _():
+        @once(k == 0)
+        def _(_):
             for item in loads:
                 item.wait()
 
@@ -255,8 +262,8 @@
         ring_mate(h_ring, k, b)
         make_trig(b)
 
-        @pl.when(k == 0)
-        def _():
+        @once(k == 0)
+        def _(_):
             for item in far_loads:
                 item.wait()
             cos_t = trig[chip, 0:quarter, part_of(core, tok)]
@@ -299,27 +306,14 @@
             @pl.loop(0, n_far)
             def _(f):
                 both = dot(kv_far[f, place, :], bmat_far[f])
-                d_p = both[:, cols_q:2 * cols_q]
-
-                @pl.when(k == 0)
-                def _():
-                    s = jnp.where(seen_far, both[:, 0:cols_q], -1e30)
-                    top = jnp.max(s, axis=0, keepdims=True)
-                    p = jnp.exp(s - top)
-                    stat_far[f, 0] = top
-                    stat_far[f, 1] = jnp.sum(p, axis=0, keepdims=True)
-                    stat_far[f, 2] = jnp.sum(p * d_p, axis=0, keepdims=True)
-
-                @pl.when(k > 0)
-                def _():
-                    s = both[:, 0:cols_q]
-                    old = stat_far[f, 0]
-                    new = jnp.maximum(old, jnp.max(s, axis=0, keepdims=True))
-                    p = jnp.exp(s - new)
-                    keep = jnp.exp(old - new)
-                    stat_far[f, 0] = new
-                    stat_far[f, 1] = stat_far[f, 1] * keep + jnp.sum(p, axis=0, keepdims=True)
-                    stat_far[f, 2] = stat_far[f, 2] * keep + jnp.sum(p * d_p, axis=0, keepdims=True)
+                s = jnp.where(seen_far | (k > 0), both[:, 0:cols_q], -1e30)
+                old = stat_far[f, 0]
+                new = jnp.maximum(old, jnp.max(s, axis=0, keepdims=True))
+                p = jnp.exp(s - new)
+                keep = jnp.exp(old - new)
+                stat_far[f, 0] = new
+                stat_far[f, 1] = stat_far[f, 1] * keep + jnp.sum(p, axis=0, keepdims=True)
+                stat_far[f, 2] = stat_far[f, 2] * keep + jnp.sum(p * both[:, cols_q:2 * cols_q], axis=0, keepdims=True)
 
     groups = [slice(tile * g, tile * g + tile) for g in range(cols_q // tile)]
 
@@ -406,16 +400,14 @@
             for item in weight_loads:
                 item.wait()
 
-        @pl.when(k == n_chip - 1)
-        def _():
-            for early in range(1 + 2 * near):
-                for t in range(2):
-                    slot = 2 * ring_origin(early) + t
-
-                    @pl.when(slot != me)
-                    def _():
-                        for item in send_rows(slot):
-                            item.start()
+        @pl.loop(0, jnp.where(k == n_chip - 1, 2 + 4 * near, 0))
+        def _(early):
+            slot = 2 * ring_origin(early // 2) + early % 2
+
+            @pl.when(slot != me)
+            def _():
+                for item in send_rows(slot):
+                    item.start()
 
         da_t = dot_t(woi[...], dyb[b]).astype(BF)
         bmat[0:hd, 0:cols_q] = qt[b]

time: 154 us -> 154 us (level)
  no operation moved by 1% of the time
where the time goes in v11:
time: 154 us
  Pallas kernels  153 us (99%)
    pallas_call x1, Pallas kernels, device_step(): pl.pallas_call(functools.partial(block_kernel, n_dev, hd, kv_w, NEAR, PAR...  150 us
    pallas_call x1, Pallas kernels, device_step(): pl.pallas_call(functools.partial(settle_kernel, q_w, kv_w), out_shape=(ja...  3.62 us

profile of v11, /device:TPU:21, one launch (start us, length us, event | category | flops | bytes accessed | tf_op | source)
XLA Modules:
  0.0 154.1 jit_solution(14104803489455867472)
XLA Ops:
  0.6 149.7 %attn_block.1 = (bf16[128,2048]{1,0:T(8,128)(2,1)}, bf16[128,2048]{1,0:T(8,128)(2,1)}, f32[3072,128]{1,0:T(8,128)}, f32[128,2048]{1,0:T(8,128)}, f32[2,1,2048]{2,1,0:T(1,128)}) custom-call(bf16[128,2048]{1,0:T(8,128)(2,1)} %bitcast.27, bf16[128,2048]{1,0:T(8,128)(2,1)} %bitcast.28, s32[1,128]{1,0:T(1,128)} %pos_hbm.1, f32[1,2048]{1,0:T(1,128)} %bitcast.29, ...), custom_call_target="tpu_custom_call" | custom-call | tf_op jit(solution)/shard_map/attn_block/pallas_call | solution.py:718
  150.3 3.6 %settle.1 = (bf16[128,2048]{1,0:T(8,128)(2,1)}, bf16[128,2048]{1,0:T(8,128)(2,1)}, f32[2048,128]{1,0:T(8,128)}, f32[512,128]{1,0:T(8,128)}, f32[512,128]{1,0:T(8...) custom-call(bf16[128,2048]{1,0:T(8,128)(2,1)} %get-tuple-element.21.out_i, ...), custom_call_target="tpu_custom_call" | custom-call | tf_op jit(solution)/shard_map/settle/pallas_call | solution.py:738

commit v12 on v11

--- a/solution.py
+++ b/solution.py
@@ -32,11 +32,11 @@
     x_hbm, dy_hbm, pos_hbm, gain_hbm, bias_hbm, wq_hbm, wk_hbm, wv_hbm, wo_hbm,
     out_hbm, gx_hbm, gw_hbm, gwo_hbm, gg_hbm,
     hb, dyb, wt, wi, woi, w_far, pos_all, trig,
-    qt, kvt, kv, kvt_far, kv_far, bmat_far, stat_far, bmat, sbuf, dpbuf, mbuf, adq, dkvt, kv_rv, kv_mine, kv_row,
+    qt, kvt, kv, kvt_far, kv_far, bmat_far, stat_far, bmat, da_rv, sbuf, dpbuf, mbuf, adq, dkvt, kv_rv, kv_mine, kv_row,
     dwo, dwt, at_all, dq_all, at_rv, dt_rv, a_nat, d_nat, x_v, dy_own, gb_v, stat, out_v, gg_st, gg_mx, gg_my, gg_rv, gg_out,
     in_sem, far_sem, wo_sem, w_sem, out_sem, loc_sem,
     hzs, hzr, hds, hdr, yzs, yzr, yds, ydr,
-    pos_s, pos_r, a_s, a_r, q_s, q_r, x_s, x_r, kv_s, kv_r, w_s, w_r, wk_s, wk_r, g_s, g_r,
+    d_s, d_r, pos_s, pos_r, a_s, a_r, q_s, q_r, x_s, x_r, kv_s, kv_r, w_s, w_r, wk_s, wk_r, g_s, g_r,
 ):
     tok, width = x_v.shape
     n_chip = n_dev // 2
@@ -243,6 +243,12 @@
     row = lax.broadcasted_iota(jnp.int32, (pair, cols_q), 0)
     seen_far = row <= core * tok + lane % tok
 
+    opposite = ring_origin(n_chip - 1)
+
+    def opposite_send(head):
+        block = bmat_far.at[n_far - 1, pl.ds(hd, hd), pl.ds(cols_q + tok * head, tok)]
+        return remote(block, da_rv.at[2 * core + head % 2], d_s.at[head], d_r.at[2 * core + head % 2], 2 * opposite + head // 2)
+
     @pl.loop(0, n_chip)
     def _(k):
         for turn in range(parts):
@@ -281,6 +287,11 @@
 
             for item in weight_loads:
                 item.start()
+
+        @once(k == 1)
+        def _(_):
+            for head in range(4):
+                opposite_send(head).start()
 
         place = part_of(b, pair)
         cos_t = trig[b, 0:quarter, :]
@@ -382,25 +393,35 @@
             remote(at_all.at[:, cols], at_rv.at[own_rows], a_s.at[slot], a_r.at[me], slot),
         ]
 
-    for event in range(2):
-        ring_event(y_ring, jnp.int32(event))
+    last = 6 * parts
+
+    def serve(event):
+        @pl.when((event >= 0) & (event < last))
+        def _():
+            ring_event(y_ring, event)
 
     @pl.loop(0, n_chip)
-    def _(k):
-        @pl.when(k % 2 == 1)
+    def _(j):
+        k = j - 1
+
+        @pl.when(k == 0)
+        def _():
+            for turn in range(2):
+                ring_event(y_ring, k + turn)
+
+        @pl.when((k % 2 == 1) & (k > 0))
         def _():
             for turn in range(2, parts):
-                ring_service(y_ring, parts * k + turn)
-
-        b = ring_origin(k)
-        ring_mate(y_ring, k, b)
-
-        @pl.when(k == 1)
-        def _():
+                serve(parts * k + turn)
+
+        b = jnp.where(j == 0, opposite, ring_origin(jnp.maximum(k, 0)))
+
+        @once(k == 1)
+        def _(_):
             for item in weight_loads:
                 item.wait()
 
-        @pl.loop(0, jnp.where(k == n_chip - 1, 2 + 4 * near, 0))
+        @pl.loop(0, jnp.where(j == n_chip - 1, 2 + 4 * near, 0))
         def _(early):
             slot = 2 * ring_origin(early // 2) + early % 2
 
@@ -409,15 +430,26 @@
                 for item in send_rows(slot):
                     item.start()
 
-        da_t = dot_t(woi[...], dyb[b]).astype(BF)
         bmat[0:hd, 0:cols_q] = qt[b]
-        for t in range(2):
-            for head in range(2):
-                at = cols_q + pair * t + tok * head
-                bmat[hd:hw, at:at + tok] = da_t[hd * head:hd * head + hd, tok * t:tok * t + tok]
+
+        @once(j == 0)
+        def _(_):
+            for i in range(4):
+                remote(da_rv.at[i], da_rv.at[i], d_s.at[0], d_r.at[i], mate).wait_recv()
+                bmat[hd:hw, cols_q + tok * i:cols_q + tok * i + tok] = da_rv[i]
+
+        @once(j > 0)
+        def _(_):
+            ring_mate(y_ring, k, b)
+            da_t = dot_t(woi[...], dyb[b]).astype(BF)
+            for t in range(2):
+                for head in range(2):
+                    at = cols_q + pair * t + tok * head
+                    bmat[hd:hw, at:at + tok] = da_t[hd * head:hd * head + hd, tok * t:tok * t + tok]
+
         stats = first_part(b, row <= (lane // pair) * tok + lane % tok)
         for turn in range(2):
-            ring_service(y_ring, parts * k + 2 + 2 * (k % 2) + turn)
+            serve(jnp.where(k < 0, -1, parts * k + 2 + 2 * (k % 2) + turn))
         second_part(b, stats)
         for t in range(2):
             slot = 2 * b + t
@@ -434,10 +466,10 @@
                 at_rv[own_rows, :] = a_t
                 dt_rv[own_rows, :] = dq_t
 
-        @pl.when(k % 2 == 0)
+        @pl.when((k % 2 == 0) & (k >= 0))
         def _():
             for turn in range(2):
-                ring_service(y_ring, parts * (k + 1) + turn)
+                serve(parts * (k + 1) + turn)
 
     far = [ring_origin(k) for k in range(n_chip - 1, 0, -1)]
     targets = [2 * c + p for c in far for p in range(2)] + [mate]
@@ -491,6 +523,11 @@
     for item in wk_sends[0:HELD]:
         item.start()
 
+    @pl.loop(last, 7 * parts)
+    def _(event):
+        ring_event(y_ring, event)
+
+    ring_mate(y_ring, n_chip - 1, opposite)
     for t in range(width // tile):
         cols = slice(tile * t, tile * t + tile)
         dwo[:, cols] = columns(at_all, dyb, cols)
@@ -610,7 +647,7 @@
     store_gg.start()
 
     finish_ring(h_ring)
-    for item in pos_sends + [g_swap, g_swap_out]:
+    for item in pos_sends + [g_swap, g_swap_out] + [opposite_send(head) for head in range(4)]:
         item.wait_send()
     for t in near_targets:
         remote(at_all.at[:, pl.ds(0, tok)], at_rv.at[pl.ds(0, hw)], a_s.at[t], a_r.at[t], t).wait_send()
@@ -687,6 +724,7 @@
             pltpu.VMEM((n_far, hw, 4 * pair), BF),
             pltpu.VMEM((n_far, 3, 1, 2 * pair), F32),
             pltpu.VMEM((hw, 4 * pair), BF),
+            pltpu.VMEM((4, hd, tok), BF),
             pltpu.VMEM((seq, 2 * pair), F32),
             pltpu.VMEM((seq, 2 * pair), F32),
             pltpu.VMEM((n_chip, 1, 2 * pair), F32),
@@ -714,7 +752,7 @@
             pltpu.VMEM((n_chip, 1, width), F32),
             pltpu.VMEM((2, 1, width), F32),
             dma((10,)), dma((4 * n_far,)), dma((n_chip,)), dma((3,)), dma((4,)), dma((2,)),
-        ] + [dma((9 * PARTS,)), dma((7 * PARTS,)), dma((8 * PARTS,)), dma((8 * PARTS,))] * 2 + [dma((n_dev,))] * 6 + [dma] * 2 + [dma((n_dev,))] * 8
+        ] + [dma((9 * PARTS,)), dma((7 * PARTS,)), dma((8 * PARTS,)), dma((8 * PARTS,))] * 2 + [dma((4,))] * 2 + [dma((n_dev,))] * 6 + [dma] * 2 + [dma((n_dev,))] * 8
         out, gx, gw, gwo, gg = pl.pallas_call(
             functools.partial(block_kernel, n_dev, hd, kv_w, NEAR, PARTS),
             out_shape=(

time: 154 us -> 151 us (0.981)
  Pallas kernels: 153 us -> 150 us
    pallas_call x1, Pallas kernels: 150 us -> 147 us  [device_step(): pl.pallas_call(functools.partial(block_kernel, n_dev, hd, kv_w, NEAR, PAR...]
where the time goes in v12:
time: 151 us
  Pallas kernels  150 us (99%)
    pallas_call x1, Pallas kernels, device_step(): pl.pallas_call(functools.partial(block_kernel, n_dev, hd, kv_w, NEAR, PAR...  147 us
    pallas_call x1, Pallas kernels, device_step(): pl.pallas_call(functools.partial(settle_kernel, q_w, kv_w), out_shape=(ja...  3.62 us

profile of v12, /device:TPU:21, one launch (start us, length us, event | category | flops | bytes accessed | tf_op | source)
XLA Modules:
  0.0 151.0 jit_solution(9251666878144370316)
XLA Ops:
  0.6 146.6 %attn_block.1 = (bf16[128,2048]{1,0:T(8,128)(2,1)}, bf16[128,2048]{1,0:T(8,128)(2,1)}, f32[3072,128]{1,0:T(8,128)}, f32[128,2048]{1,0:T(8,128)}, f32[2,1,2048]{2,1,0:T(1,128)}) custom-call(bf16[128,2048]{1,0:T(8,128)(2,1)} %bitcast.27, bf16[128,2048]{1,0:T(8,128)(2,1)} %bitcast.28, s32[1,128]{1,0:T(1,128)} %pos_hbm.1, f32[1,2048]{1,0:T(1,128)} %bitcast.29, ...), custom_call_target="tpu_custom_call" | custom-call | tf_op jit(solution)/shard_map/attn_block/pallas_call | solution.py:756
  147.2 3.6 %settle.1 = (bf16[128,2048]{1,0:T(8,128)(2,1)}, bf16[128,2048]{1,0:T(8,128)(2,1)}, f32[2048,128]{1,0:T(8,128)}, f32[512,128]{1,0:T(8,128)}, f32[512,128]{1,0:T(8...) custom-call(bf16[128,2048]{1,0:T(8,128)(2,1)} %get-tuple-element.21.out_i, ...), custom_call_target="tpu_custom_call" | custom-call | tf_op jit(solution)/shard_map/settle/pallas_call | solution.py:776

commit v13 on v12

--- a/solution.py
+++ b/solution.py
@@ -21,6 +21,18 @@
 
 def dot(lhs, rhs):
     return jnp.dot(lhs, rhs, preferred_element_type=F32)
+
+
+def col_sum(val):
+    return jnp.sum(val, axis=0, keepdims=True)
+
+
+def col_max(val):
+    return jnp.max(val, axis=0, keepdims=True)
+
+
+def row_mean(val):
+    return jnp.mean(val, axis=-1, keepdims=True)
 
 
 def dot_t(lhs, rhs):
@@ -118,9 +130,9 @@
     def _(i):
         rows = part_of(i, block)
         x_f = x_v[rows, :].astype(F32)
-        mean = jnp.mean(x_f, axis=-1, keepdims=True)
+        mean = row_mean(x_f)
         centered = x_f - mean
-        inv_std = lax.rsqrt(jnp.mean(centered * centered, axis=-1, keepdims=True) + EPS)
+        inv_std = lax.rsqrt(row_mean(centered * centered) + EPS)
         hb[chip, part_of(core * (tok // block) + i, block), :] = (centered * inv_std * gain_one + gb_v[1]).astype(BF)
         stat[0, rows, :] = jnp.broadcast_to(mean, (block, 128))
         stat[1, rows, :] = jnp.broadcast_to(inv_std, (block, 128))
@@ -319,12 +331,12 @@
                 both = dot(kv_far[f, place, :], bmat_far[f])
                 s = jnp.where(seen_far | (k > 0), both[:, 0:cols_q], -1e30)
                 old = stat_far[f, 0]
-                new = jnp.maximum(old, jnp.max(s, axis=0, keepdims=True))
+                new = jnp.maximum(old, col_max(s))
                 p = jnp.exp(s - new)
                 keep = jnp.exp(old - new)
                 stat_far[f, 0] = new
-                stat_far[f, 1] = stat_far[f, 1] * keep + jnp.sum(p, axis=0, keepdims=True)
-                stat_far[f, 2] = stat_far[f, 2] * keep + jnp.sum(p * both[:, cols_q:2 * cols_q], axis=0, keepdims=True)
+                stat_far[f, 1] = stat_far[f, 1] * keep + col_sum(p)
+                stat_far[f, 2] = stat_far[f, 2] * keep + col_sum(p * both[:, cols_q:2 * cols_q])
 
     groups = [slice(tile * g, tile * g + tile) for g in range(cols_q // tile)]
 
@@ -336,7 +348,7 @@
         rows = part_of(b, pair)
         s, d_p = both_of(rows)
         s = jnp.where(seen, s, -1e30)
-        top = jnp.max(s, axis=0, keepdims=True)
+        top = col_max(s)
         p = jnp.exp(s - top)
         sbuf[rows, :] = p
         dpbuf[rows, :] = d_p
@@ -346,16 +358,16 @@
             old, total, weighted = state
             rows = part_of(c, chunks * pair)
             s, d_p = both_of(rows)
-            new = jnp.maximum(old, jnp.max(s, axis=0, keepdims=True))
+            new = jnp.maximum(old, col_max(s))
             p = jnp.exp(s - new)
             sbuf[rows, :] = p
             dpbuf[rows, :] = d_p
             for i in range(chunks):
                 mbuf[chunks * c + i] = new
             keep = jnp.exp(old - new)
-            return new, total * keep + jnp.sum(p, axis=0, keepdims=True), weighted * keep + jnp.sum(p * d_p, axis=0, keepdims=True)
-
-        state = (top, jnp.sum(p, axis=0, keepdims=True), jnp.sum(p * d_p, axis=0, keepdims=True))
+            return new, total * keep + col_sum(p), weighted * keep + col_sum(p * d_p)
+
+        state = (top, col_sum(p), col_sum(p * d_p))
         state = lax.fori_loop(0, b // 2, functools.partial(step, chunks=2), state)
         top, total, weighted = lax.fori_loop(2 * (b // 2), b, step, state)
         inv = 1.0 / total
@@ -396,7 +408,7 @@
     last = 6 * parts
 
     def serve(event):
-        @pl.when((event >= 0) & (event < last))
+        @pl.when(event < last)
         def _():
             ring_event(y_ring, event)
 
@@ -404,12 +416,7 @@
     def _(j):
         k = j - 1
 
-        @pl.when(k == 0)
-        def _():
-            for turn in range(2):
-                ring_event(y_ring, k + turn)
-
-        @pl.when((k % 2 == 1) & (k > 0))
+        @pl.when((k % 2 == 1) & (k > 1))
         def _():
             for turn in range(2, parts):
                 serve(parts * k + turn)
@@ -449,7 +456,7 @@
 
         stats = first_part(b, row <= (lane // pair) * tok + lane % tok)
         for turn in range(2):
-            serve(jnp.where(k < 0, -1, parts * k + 2 + 2 * (k % 2) + turn))
+            serve(jnp.where(k < 1, parts * j, parts * k + 2 + 2 * (k % 2)) + turn)
         second_part(b, stats)
         for t in range(2):
             slot = 2 * b + t
@@ -466,10 +473,10 @@
                 at_rv[own_rows, :] = a_t
                 dt_rv[own_rows, :] = dq_t
 
-        @pl.when((k % 2 == 0) & (k >= 0))
+        @pl.when((k % 2 == 0) | (j == 0))
         def _():
             for turn in range(2):
-                serve(parts * (k + 1) + turn)
+                serve(parts * j + jnp.where(k < 1, 2, 0) + turn)
 
     far = [ring_origin(k) for k in range(n_chip - 1, 0, -1)]
     targets = [2 * c + p for c in far for p in range(2)] + [mate]
@@ -614,8 +621,8 @@
         for s in range(n_rows // tile):
             acc += dot(d_nat[:, tile * s:tile * s + tile], wt[tile * s:tile * s + tile, cols])
         dh[:, cols] = acc
-        gg_st[0, :, cols] = jnp.sum(acc * ((x_v[:, cols].astype(F32) - mean) * inv_std), axis=0, keepdims=True)
-        gg_st[1, :, cols] = jnp.sum(acc, axis=0, keepdims=True)
+        gg_st[0, :, cols] = col_sum(acc * ((x_v[:, cols].astype(F32) - mean) * inv_std))
+        gg_st[1, :, cols] = col_sum(acc)
     g_swap = remote(gg_st.at[1 - core], gg_mx, g_s.at[n_chip], g_r.at[n_chip], mate)
     g_swap.start()
     g_swap.wait_recv()
@@ -627,8 +634,8 @@
 
     grad_hat = dh[...] * gain_one
     x_hat = (x_v[...].astype(F32) - mean) * inv_std
-    mean_one = jnp.mean(grad_hat, axis=-1, keepdims=True)
-    mean_two = jnp.mean(grad_hat * x_hat, axis=-1, keepdims=True)
+    mean_one = row_mean(grad_hat)
+    mean_two = row_mean(grad_hat * x_hat)
     store_out.wait()
     out_v[...] = (dy_own[...].astype(F32) + inv_std * (grad_hat - mean_one - x_hat * mean_two)).astype(BF)
     store_gx = local(out_v, gx_hbm, out_sem.at[2])

time: 151 us -> 152 us (level)
  no operation moved by 1% of the time
where the time goes in v13:
time: 152 us; the launch traced here: 151 us
  Pallas kernels  151 us (99%)
    pallas_call x1, Pallas kernels, device_step(): pl.pallas_call(functools.partial(block_kernel, n_dev, hd, kv_w, NEAR, PAR...  147 us
    pallas_call x1, Pallas kernels, device_step(): pl.pallas_call(functools.partial(settle_kernel, q_w, kv_w), out_shape=(ja...  3.62 us

profile of v13, /device:TPU:21, one launch (start us, length us, event | category | flops | bytes accessed | tf_op | source)
XLA Modules:
  0.0 151.5 jit_solution(771729317796095952)
XLA Ops:
  0.6 147.0 %attn_block.1 = (bf16[128,2048]{1,0:T(8,128)(2,1)}, bf16[128,2048]{1,0:T(8,128)(2,1)}, f32[3072,128]{1,0:T(8,128)}, f32[128,2048]{1,0:T(8,128)}, f32[2,1,2048]{2,1,0:T(1,128)}) custom-call(bf16[128,2048]{1,0:T(8,128)(2,1)} %bitcast.27, bf16[128,2048]{1,0:T(8,128)(2,1)} %bitcast.28, s32[1,128]{1,0:T(1,128)} %pos_hbm.1, f32[1,2048]{1,0:T(1,128)} %bitcast.29, ...), custom_call_target="tpu_custom_call" | custom-call | tf_op jit(solution)/shard_map/attn_block/pallas_call | solution.py:763
  147.7 3.6 %settle.1 = (bf16[128,2048]{1,0:T(8,128)(2,1)}, bf16[128,2048]{1,0:T(8,128)(2,1)}, f32[2048,128]{1,0:T(8,128)}, f32[512,128]{1,0:T(8,128)}, f32[512,128]{1,0:T(8...) custom-call(bf16[128,2048]{1,0:T(8,128)(2,1)} %get-tuple-element.21.out_i, ...), custom_call_target="tpu_custom_call" | custom-call | tf_op jit(solution)/shard_map/settle/pallas_call | solution.py:783

commit v14 on v13

--- a/solution.py
+++ b/solution.py
@@ -13,7 +13,7 @@
 MESH = pl.DeviceIdType.MESH
 BF = jnp.bfloat16
 F32 = jnp.float32
-NEAR = 1
+NEAR = 0
 PARTS = 4
 FIRST = 1
 HELD = 4
@@ -43,7 +43,7 @@
     n_dev, hd, kv_w, near, parts,
     x_hbm, dy_hbm, pos_hbm, gain_hbm, bias_hbm, wq_hbm, wk_hbm, wv_hbm, wo_hbm,
     out_hbm, gx_hbm, gw_hbm, gwo_hbm, gg_hbm,
-    hb, dyb, wt, wi, woi, w_far, pos_all, trig,
+    hb, dyb, wt, wi, woi, pos_all, trig,
     qt, kvt, kv, kvt_far, kv_far, bmat_far, stat_far, bmat, da_rv, sbuf, dpbuf, mbuf, adq, dkvt, kv_rv, kv_mine, kv_row,
     dwo, dwt, at_all, dq_all, at_rv, dt_rv, a_nat, d_nat, x_v, dy_own, gb_v, stat, out_v, gg_st, gg_mx, gg_my, gg_rv, gg_out,
     in_sem, far_sem, wo_sem, w_sem, out_sem, loc_sem,
@@ -111,13 +111,15 @@
         local(dy_hbm, dy_own, in_sem.at[9]),
     ]
     far_loads = []
+    far_first = n_far * 2 * hw
     for f in range(n_far):
-        far_rows = part_of(ring_origin(2 * near + 1 + f), hd)
-        loads.append(local(wk_hbm.at[far_rows], w_far.at[pl.ds(hw * f, hd)], far_sem.at[2 * f]))
-        loads.append(local(wv_hbm.at[far_rows], w_far.at[pl.ds(hw * f + hd, hd)], far_sem.at[2 * f + 1]))
-        far_wo = part_of(ring_origin(2 * near + 1 + f), 2 * hw)
-        far_loads.append(local(wo_hbm.at[far_wo], wt.at[pl.ds(2 * hw * f, 2 * hw)], far_sem.at[2 * n_far + f]))
-        far_loads.append(local(wq_hbm.at[far_wo], wt.at[pl.ds(2 * hw * (n_far + f), 2 * hw)], far_sem.at[3 * n_far + f]))
+        c_far = ring_origin(2 * near + 1 + f)
+        far_rows = part_of(c_far, hd)
+        loads.append(local(wk_hbm.at[far_rows], wt.at[pl.ds(far_first + hw * f, hd)], far_sem.at[f]))
+        loads.append(local(wv_hbm.at[far_rows], wt.at[pl.ds(far_first + hw * f + hd, hd)], far_sem.at[n_far + f]))
+        far_w = part_of(c_far, pair)
+        far_loads.append(local(wo_hbm.at[far_w], wt.at[pl.ds(pair * f, pair)], far_sem.at[2 * n_far + f]))
+        far_loads.append(local(wq_hbm.at[far_w], dyb.at[c_far], far_sem.at[3 * n_far + f]))
     for item in loads + far_loads:
         item.start()
 
@@ -263,8 +265,13 @@
 
     @pl.loop(0, n_chip)
     def _(k):
-        for turn in range(parts):
+        for turn in range(2):
             ring_service(h_ring, parts * k + turn)
+
+        @pl.when(k % 2 == 1)
+        def _():
+            ring_service(h_ring, parts * k + 2)
+
 
         @once(k == 5)
         def _(_):
@@ -290,15 +297,12 @@
             @pl.loop(0, n_far)
             def _(f):
                 da_t = dot_t(wt[part_of(f, 2 * hw), :], dy_own[...]).astype(BF)
-                q_t = dot_t(wt[part_of(n_far + f, 2 * hw), :], hb[chip, part_of(core, tok), :])
+                q_t = dot_t(dyb[ring_origin(2 * near + 1 + f)], hb[chip, part_of(core, tok), :])
                 for head in range(4):
                     part = slice(hd * head, hd * head + hd)
                     at = tok * head
                     bmat_far[f, 0:hd, at:at + tok] = eighth(jnp.concatenate(turned(q_t[part], cos_t, sin_t), axis=0))
                     bmat_far[f, hd:hw, cols_q + at:cols_q + at + tok] = da_t[part]
-
-            for item in weight_loads:
-                item.start()
 
         @once(k == 1)
         def _(_):
@@ -318,9 +322,15 @@
         kvt[:, place] = kv_rot
         kv[place, :] = kv_rot.T
 
+        @pl.when(k % 2 == 0)
+        def _():
+            ring_service(h_ring, parts * k + 2)
+
+        ring_service(h_ring, parts * k + parts - 1)
+
         @pl.when(b <= chip)
         def _():
-            flat_far = dot_t(w_far[...], hb[b])
+            flat_far = dot_t(wt[far_first:far_first + n_far * hw, :], hb[b])
             for f in range(n_far):
                 far_rot = keys_values(flat_far[hw * f:hw * f + hw], cos_t, sin_t)
                 kvt_far[f, :, place] = far_rot
@@ -416,17 +426,22 @@
     def _(j):
         k = j - 1
 
-        @pl.when((k % 2 == 1) & (k > 1))
+        @pl.when(k == 0)
+        def _():
+            for turn in range(2):
+                ring_event(y_ring, k + turn)
+
+        @pl.when((k % 2 == 1) & (k > 0))
         def _():
             for turn in range(2, parts):
                 serve(parts * k + turn)
 
         b = jnp.where(j == 0, opposite, ring_origin(jnp.maximum(k, 0)))
 
-        @once(k == 1)
+        @once(j == 0)
         def _(_):
             for item in weight_loads:
-                item.wait()
+                item.start()
 
         @pl.loop(0, jnp.where(j == n_chip - 1, 2 + 4 * near, 0))
         def _(early):
@@ -456,7 +471,7 @@
 
         stats = first_part(b, row <= (lane // pair) * tok + lane % tok)
         for turn in range(2):
-            serve(jnp.where(k < 1, parts * j, parts * k + 2 + 2 * (k % 2)) + turn)
+            serve(jnp.where(k < 0, last, parts * k + 2 + 2 * (k % 2)) + turn)
         second_part(b, stats)
         for t in range(2):
             slot = 2 * b + t
@@ -473,10 +488,10 @@
                 at_rv[own_rows, :] = a_t
                 dt_rv[own_rows, :] = dq_t
 
-        @pl.when((k % 2 == 0) | (j == 0))
+        @pl.when((k % 2 == 0) & (k >= 0))
         def _():
             for turn in range(2):
-                serve(parts * j + jnp.where(k < 1, 2, 0) + turn)
+                serve(parts * j + turn)
 
     far = [ring_origin(k) for k in range(n_chip - 1, 0, -1)]
     targets = [2 * c + p for c in far for p in range(2)] + [mate]
@@ -601,6 +616,9 @@
     store_out = local(out_v, out_hbm, out_sem.at[1])
     store_out.start()
 
+    for item in weight_loads:
+        item.wait()
+
     def kv_place(t):
         return pl.ds(pl.multiple_of(q_rows + (t % 2) * kv_w + (t // 2) * hd, hd), hd)
 
@@ -720,7 +738,6 @@
             pltpu.VMEM((n_rows, width), BF),
             pltpu.VMEM((2 * hw, width), BF),
             pltpu.VMEM((hw, width), BF),
-            pltpu.VMEM((n_far * hw, width), BF),
             pltpu.VMEM((n_dev, 1, tok), jnp.int32),
             pltpu.VMEM((n_chip, hd // 2, pair), F32),
             pltpu.VMEM((n_chip, hd, 2 * pair), BF),

time: 152 us -> 163 us (1.072)
  Pallas kernels: 151 us -> 162 us
    pallas_call x1, Pallas kernels: 147 us -> 158 us  [device_step(): pl.pallas_call(functools.partial(block_kernel, n_dev, hd, kv_w, NEAR, PAR...]
where the time goes in v14:
time: 163 us
  Pallas kernels  162 us (99%)
    pallas_call x1, Pallas kernels, device_step(): pl.pallas_call(functools.partial(block_kernel, n_dev, hd, kv_w, NEAR, PAR...  158 us
    pallas_call x1, Pallas kernels, device_step(): pl.pallas_call(functools.partial(settle_kernel, q_w, kv_w), out_shape=(ja...  3.62 us

profile of v14, /device:TPU:21, one launch (start us, length us, event | category | flops | bytes accessed | tf_op | source)
XLA Modules:
  0.0 162.7 jit_solution(8484466206710995692)
XLA Ops:
  0.6 158.3 %attn_block.1 = (bf16[128,2048]{1,0:T(8,128)(2,1)}, bf16[128,2048]{1,0:T(8,128)(2,1)}, f32[3072,128]{1,0:T(8,128)}, f32[128,2048]{1,0:T(8,128)}, f32[2,1,2048]{2,1,0:T(1,128)}) custom-call(bf16[128,2048]{1,0:T(8,128)(2,1)} %bitcast.27, bf16[128,2048]{1,0:T(8,128)(2,1)} %bitcast.28, s32[1,128]{1,0:T(1,128)} %pos_hbm.1, f32[1,2048]{1,0:T(1,128)} %bitcast.29, ...), custom_call_target="tpu_custom_call" | custom-call | tf_op jit(solution)/shard_map/attn_block/pallas_call | solution.py:780
  158.9 3.6 %settle.1 = (bf16[128,2048]{1,0:T(8,128)(2,1)}, bf16[128,2048]{1,0:T(8,128)(2,1)}, f32[2048,128]{1,0:T(8,128)}, f32[512,128]{1,0:T(8,128)}, f32[512,128]{1,0:T(8...) custom-call(bf16[128,2048]{1,0:T(8,128)(2,1)} %get-tuple-element.21.out_i, ...), custom_call_target="tpu_custom_call" | custom-call | tf_op jit(solution)/shard_map/settle/pallas_call | solution.py:800

commit v15 on v13

--- a/solution.py
+++ b/solution.py
@@ -263,8 +263,13 @@
 
     @pl.loop(0, n_chip)
     def _(k):
-        for turn in range(parts):
+        for turn in range(2):
             ring_service(h_ring, parts * k + turn)
+
+        @pl.when(k % 2 == 1)
+        def _():
+            ring_service(h_ring, parts * k + 2)
+
 
         @once(k == 5)
         def _(_):
@@ -317,6 +322,12 @@
         kv_rot = keys_values(flat[hw:2 * hw], cos_t, sin_t)
         kvt[:, place] = kv_rot
         kv[place, :] = kv_rot.T
+
+        @pl.when(k % 2 == 0)
+        def _():
+            ring_service(h_ring, parts * k + 2)
+
+        ring_service(h_ring, parts * k + parts - 1)
 
         @pl.when(b <= chip)
         def _():
@@ -416,7 +427,12 @@
     def _(j):
         k = j - 1
 
-        @pl.when((k % 2 == 1) & (k > 1))
+        @pl.when(k == 0)
+        def _():
+            for turn in range(2):
+                ring_event(y_ring, k + turn)
+
+        @pl.when((k % 2 == 1) & (k > 0))
         def _():
             for turn in range(2, parts):
                 serve(parts * k + turn)
@@ -456,7 +472,7 @@
 
         stats = first_part(b, row <= (lane // pair) * tok + lane % tok)
         for turn in range(2):
-            serve(jnp.where(k < 1, parts * j, parts * k + 2 + 2 * (k % 2)) + turn)
+            serve(jnp.where(k < 0, last, parts * k + 2 + 2 * (k % 2)) + turn)
         second_part(b, stats)
         for t in range(2):
             slot = 2 * b + t
@@ -473,10 +489,10 @@
                 at_rv[own_rows, :] = a_t
                 dt_rv[own_rows, :] = dq_t
 
-        @pl.when((k % 2 == 0) | (j == 0))
+        @pl.when((k % 2 == 0) & (k >= 0))
         def _():
             for turn in range(2):
-                serve(parts * j + jnp.where(k < 1, 2, 0) + turn)
+                serve(parts * j + turn)
 
     far = [ring_origin(k) for k in range(n_chip - 1, 0, -1)]
     targets = [2 * c + p for c in far for p in range(2)] + [mate]

time: 152 us -> 160 us (1.053)
  Pallas kernels: 151 us -> 160 us
    pallas_call x1, Pallas kernels: 147 us -> 156 us  [device_step(): pl.pallas_call(functools.partial(block_kernel, n_dev, hd, kv_w, NEAR, PAR...]
where the time goes in v15:
time: 160 us
  Pallas kernels  160 us (100%)
    pallas_call x1, Pallas kernels, device_step(): pl.pallas_call(functools.partial(block_kernel, n_dev, hd, kv_w, NEAR, PAR...  156 us
    pallas_call x1, Pallas kernels, device_step(): pl.pallas_call(functools.partial(settle_kernel, q_w, kv_w), out_shape=(ja...  3.62 us

profile of v15, /device:TPU:21, one launch (start us, length us, event | category | flops | bytes accessed | tf_op | source)
XLA Modules:
  0.0 160.3 jit_solution(13954761385263496080)
XLA Ops:
  0.6 155.9 %attn_block.1 = (bf16[128,2048]{1,0:T(8,128)(2,1)}, bf16[128,2048]{1,0:T(8,128)(2,1)}, f32[3072,128]{1,0:T(8,128)}, f32[128,2048]{1,0:T(8,128)}, f32[2,1,2048]{2,1,0:T(1,128)}) custom-call(bf16[128,2048]{1,0:T(8,128)(2,1)} %bitcast.27, bf16[128,2048]{1,0:T(8,128)(2,1)} %bitcast.28, s32[1,128]{1,0:T(1,128)} %pos_hbm.1, f32[1,2048]{1,0:T(1,128)} %bitcast.29, ...), custom_call_target="tpu_custom_call" | custom-call | tf_op jit(solution)/shard_map/attn_block/pallas_call | solution.py:779
  156.5 3.6 %settle.1 = (bf16[128,2048]{1,0:T(8,128)(2,1)}, bf16[128,2048]{1,0:T(8,128)(2,1)}, f32[2048,128]{1,0:T(8,128)}, f32[512,128]{1,0:T(8,128)}, f32[512,128]{1,0:T(8...) custom-call(bf16[128,2048]{1,0:T(8,128)(2,1)} %get-tuple-element.21.out_i, ...), custom_call_target="tpu_custom_call" | custom-call | tf_op jit(solution)/shard_map/settle/pallas_call | solution.py:799

commit v16 on v14

--- a/solution.py
+++ b/solution.py
@@ -273,11 +273,6 @@
             ring_service(h_ring, parts * k + 2)
 
 
-        @once(k == 5)
-        def _(_):
-            for item in own_sends(*y_ring):
-                item.start()
-
         @once(k == 0)
         def _(_):
             for item in loads:
@@ -327,6 +322,11 @@
             ring_service(h_ring, parts * k + 2)
 
         ring_service(h_ring, parts * k + parts - 1)
+
+        @once(k == 5)
+        def _(_):
+            for item in own_sends(*y_ring):
+                item.start()
 
         @pl.when(b <= chip)
         def _():

time: 163 us -> 153 us (0.939)
  Pallas kernels: 162 us -> 152 us
    pallas_call x1, Pallas kernels: 158 us -> 149 us  [device_step(): pl.pallas_call(functools.partial(block_kernel, n_dev, hd, kv_w, NEAR, PAR...]
where the time goes in v16:
time: 153 us
  Pallas kernels  152 us (99%)
    pallas_call x1, Pallas kernels, device_step(): pl.pallas_call(functools.partial(block_kernel, n_dev, hd, kv_w, NEAR, PAR...  149 us
    pallas_call x1, Pallas kernels, device_step(): pl.pallas_call(functools.partial(settle_kernel, q_w, kv_w), out_shape=(ja...  3.62 us

profile of v16, /device:TPU:21, one launch (start us, length us, event | category | flops | bytes accessed | tf_op | source)
XLA Modules:
  0.0 153.2 jit_solution(8950381179486985811)
XLA Ops:
  0.6 148.7 %attn_block.1 = (bf16[128,2048]{1,0:T(8,128)(2,1)}, bf16[128,2048]{1,0:T(8,128)(2,1)}, f32[3072,128]{1,0:T(8,128)}, f32[128,2048]{1,0:T(8,128)}, f32[2,1,2048]{2,1,0:T(1,128)}) custom-call(bf16[128,2048]{1,0:T(8,128)(2,1)} %bitcast.27, bf16[128,2048]{1,0:T(8,128)(2,1)} %bitcast.28, s32[1,128]{1,0:T(1,128)} %pos_hbm.1, f32[1,2048]{1,0:T(1,128)} %bitcast.29, ...), custom_call_target="tpu_custom_call" | custom-call | tf_op jit(solution)/shard_map/attn_block/pallas_call | solution.py:780
  149.4 3.6 %settle.1 = (bf16[128,2048]{1,0:T(8,128)(2,1)}, bf16[128,2048]{1,0:T(8,128)(2,1)}, f32[2048,128]{1,0:T(8,128)}, f32[512,128]{1,0:T(8,128)}, f32[512,128]{1,0:T(8...) custom-call(bf16[128,2048]{1,0:T(8,128)(2,1)} %get-tuple-element.21.out_i, ...), custom_call_target="tpu_custom_call" | custom-call | tf_op jit(solution)/shard_map/settle/pallas_call | solution.py:800

commit v17 on v15

--- a/solution.py
+++ b/solution.py
@@ -271,11 +271,6 @@
             ring_service(h_ring, parts * k + 2)
 
 
-        @once(k == 5)
-        def _(_):
-            for item in own_sends(*y_ring):
-                item.start()
-
         @once(k == 0)
         def _(_):
             for item in loads:
@@ -328,6 +323,11 @@
             ring_service(h_ring, parts * k + 2)
 
         ring_service(h_ring, parts * k + parts - 1)
+
+        @once(k == 5)
+        def _(_):
+            for item in own_sends(*y_ring):
+                item.start()
 
         @pl.when(b <= chip)
         def _():

time: 160 us -> 152 us (0.950)
  Pallas kernels: 160 us -> 151 us
    pallas_call x1, Pallas kernels: 156 us -> 147 us  [device_step(): pl.pallas_call(functools.partial(block_kernel, n_dev, hd, kv_w, NEAR, PAR...]
where the time goes in v17:
time: 152 us
  Pallas kernels  151 us (99%)
    pallas_call x1, Pallas kernels, device_step(): pl.pallas_call(functools.partial(block_kernel, n_dev, hd, kv_w, NEAR, PAR...  147 us
    pallas_call x1, Pallas kernels, device_step(): pl.pallas_call(functools.partial(settle_kernel, q_w, kv_w), out_shape=(ja...  3.62 us

profile of v17, /device:TPU:21, one launch (start us, length us, event | category | flops | bytes accessed | tf_op | source)
XLA Modules:
  0.0 151.6 jit_solution(7444859582250683339)
XLA Ops:
  0.6 147.2 %attn_block.1 = (bf16[128,2048]{1,0:T(8,128)(2,1)}, bf16[128,2048]{1,0:T(8,128)(2,1)}, f32[3072,128]{1,0:T(8,128)}, f32[128,2048]{1,0:T(8,128)}, f32[2,1,2048]{2,1,0:T(1,128)}) custom-call(bf16[128,2048]{1,0:T(8,128)(2,1)} %bitcast.27, bf16[128,2048]{1,0:T(8,128)(2,1)} %bitcast.28, s32[1,128]{1,0:T(1,128)} %pos_hbm.1, f32[1,2048]{1,0:T(1,128)} %bitcast.29, ...), custom_call_target="tpu_custom_call" | custom-call | tf_op jit(solution)/shard_map/attn_block/pallas_call | solution.py:779
  147.8 3.6 %settle.1 = (bf16[128,2048]{1,0:T(8,128)(2,1)}, bf16[128,2048]{1,0:T(8,128)(2,1)}, f32[2048,128]{1,0:T(8,128)}, f32[512,128]{1,0:T(8,128)}, f32[512,128]{1,0:T(8...) custom-call(bf16[128,2048]{1,0:T(8,128)(2,1)} %get-tuple-element.21.out_i, ...), custom_call_target="tpu_custom_call" | custom-call | tf_op jit(solution)/shard_map/settle/pallas_call | solution.py:799

commit v18 on v15

--- a/solution.py
+++ b/solution.py
@@ -263,17 +263,12 @@
 
     @pl.loop(0, n_chip)
     def _(k):
-        for turn in range(2):
+        for turn in range(parts):
             ring_service(h_ring, parts * k + turn)
-
-        @pl.when(k % 2 == 1)
-        def _():
-            ring_service(h_ring, parts * k + 2)
-
 
         @once(k == 5)
         def _(_):
-            for item in own_sends(*y_ring):
+            for item in [opposite_send(head) for head in range(4)] + own_sends(*y_ring):
                 item.start()
 
         @once(k == 0)
@@ -304,11 +299,6 @@
 
             for item in weight_loads:
                 item.start()
-
-        @once(k == 1)
-        def _(_):
-            for head in range(4):
-                opposite_send(head).start()
 
         place = part_of(b, pair)
         cos_t = trig[b, 0:quarter, :]
@@ -322,12 +312,6 @@
         kv_rot = keys_values(flat[hw:2 * hw], cos_t, sin_t)
         kvt[:, place] = kv_rot
         kv[place, :] = kv_rot.T
-
-        @pl.when(k % 2 == 0)
-        def _():
-            ring_service(h_ring, parts * k + 2)
-
-        ring_service(h_ring, parts * k + parts - 1)
 
         @pl.when(b <= chip)
         def _():

time: 160 us -> 151 us (0.944)
  Pallas kernels: 160 us -> 150 us
    pallas_call x1, Pallas kernels: 156 us -> 146 us  [device_step(): pl.pallas_call(functools.partial(block_kernel, n_dev, hd, kv_w, NEAR, PAR...]
where the time goes in v18:
time: 151 us
  Pallas kernels  150 us (99%)
    pallas_call x1, Pallas kernels, device_step(): pl.pallas_call(functools.partial(block_kernel, n_dev, hd, kv_w, NEAR, PAR...  146 us
    pallas_call x1, Pallas kernels, device_step(): pl.pallas_call(functools.partial(settle_kernel, q_w, kv_w), out_shape=(ja...  3.62 us

profile of v18, /device:TPU:21, one launch (start us, length us, event | category | flops | bytes accessed | tf_op | source)
XLA Modules:
  0.0 150.9 jit_solution(6971050389082318801)
XLA Ops:
  0.6 146.5 %attn_block.1 = (bf16[128,2048]{1,0:T(8,128)(2,1)}, bf16[128,2048]{1,0:T(8,128)(2,1)}, f32[3072,128]{1,0:T(8,128)}, f32[128,2048]{1,0:T(8,128)}, f32[2,1,2048]{2,1,0:T(1,128)}) custom-call(bf16[128,2048]{1,0:T(8,128)(2,1)} %bitcast.27, bf16[128,2048]{1,0:T(8,128)(2,1)} %bitcast.28, s32[1,128]{1,0:T(1,128)} %pos_hbm.1, f32[1,2048]{1,0:T(1,128)} %bitcast.29, ...), custom_call_target="tpu_custom_call" | custom-call | tf_op jit(solution)/shard_map/attn_block/pallas_call | solution.py:763
  147.1 3.6 %settle.1 = (bf16[128,2048]{1,0:T(8,128)(2,1)}, bf16[128,2048]{1,0:T(8,128)(2,1)}, f32[2048,128]{1,0:T(8,128)}, f32[512,128]{1,0:T(8,128)}, f32[512,128]{1,0:T(8...) custom-call(bf16[128,2048]{1,0:T(8,128)(2,1)} %get-tuple-element.21.out_i, ...), custom_call_target="tpu_custom_call" | custom-call | tf_op jit(solution)/shard_map/settle/pallas_call | solution.py:783

commit v19 on v18

--- a/solution.py
+++ b/solution.py
@@ -15,7 +15,7 @@
 F32 = jnp.float32
 NEAR = 1
 PARTS = 4
-FIRST = 1
+FIRST = 2
 HELD = 4
 
 
@@ -669,14 +669,20 @@
 
 
 def settle_kernel(q_rows, kv_w, out_i, gx_i, gw_i, gwo_i, gg_i, out_o, gx_o, gq_o, gk_o, gv_o, gwo_o, gain_o, bias_o, b_act, b_q, b_kv, b_o, b_gg, sem_in, sem_out, sem_gg):
-    half_q = q_rows // 2
-    half_o = gwo_i.shape[0] // 2
-    moves = [(out_i, b_act.at[0], out_o), (gx_i, b_act.at[1], gx_o)]
-    for t in range(2):
-        moves.append((gw_i.at[pl.ds(half_q * t, half_q)], b_q.at[t], gq_o.at[pl.ds(half_q * t, half_q)]))
-        moves.append((gwo_i.at[pl.ds(half_o * t, half_o)], b_o.at[t], gwo_o.at[pl.ds(half_o * t, half_o)]))
-    moves.append((gw_i.at[pl.ds(q_rows, kv_w)], b_kv.at[0], gk_o))
-    moves.append((gw_i.at[pl.ds(q_rows + kv_w, kv_w)], b_kv.at[1], gv_o))
+    moves = []
+
+    def split(src, mid, dst, pieces):
+        rows = dst.shape[0] // pieces
+        for i in range(pieces):
+            part = pl.ds(rows * i, rows)
+            moves.append((src.at[part], mid.at[part], dst.at[part]))
+
+    split(out_i, b_act.at[0], out_o, 2)
+    split(gx_i, b_act.at[1], gx_o, 2)
+    split(gwo_i, b_o, gwo_o, 4)
+    split(gw_i.at[pl.ds(0, q_rows)], b_q, gq_o, 4)
+    split(gw_i.at[pl.ds(q_rows, kv_w)], b_kv.at[0], gk_o, 1)
+    split(gw_i.at[pl.ds(q_rows + kv_w, kv_w)], b_kv.at[1], gv_o, 1)
     loads = [pltpu.make_async_copy(src, mid, sem_in.at[i]) for i, (src, mid, _) in enumerate(moves)]
     stores = [pltpu.make_async_copy(mid, dst, sem_out.at[i]) for i, (_, mid, dst) in enumerate(moves)]
     load_gg = pltpu.make_async_copy(gg_i, b_gg, sem_gg)
@@ -796,11 +802,11 @@
             out_specs=(hbm,) * 6 + (vmem,) * 2,
             scratch_shapes=[
                 pltpu.VMEM((2, tok, width), BF),
-                pltpu.VMEM((2, q_w // 2, tok), F32),
+                pltpu.VMEM((q_w, tok), F32),
                 pltpu.VMEM((2, kv_w, tok), F32),
-                pltpu.VMEM((2, hw // 2, width), F32),
+                pltpu.VMEM((hw, width), F32),
                 pltpu.VMEM((2, 1, width), F32),
-                dma((8,)), dma((8,)), dma,
+                dma((14,)), dma((14,)), dma,
             ],
             name='settle',
         )(out, gx, gw, gwo, gg)

time: 151 us -> 152 us (level)
  no operation moved by 1% of the time
where the time goes in v19:
time: 152 us
  Pallas kernels  151 us (99%)
    pallas_call x1, Pallas kernels, device_step(): pl.pallas_call(functools.partial(block_kernel, n_dev, hd, kv_w, NEAR, PAR...  147 us
    pallas_call x1, Pallas kernels, device_step(): pl.pallas_call(functools.partial(settle_kernel, q_w, kv_w), out_shape=(ja...  3.9 us

profile of v19, /device:TPU:21, one launch (start us, length us, event | category | flops | bytes accessed | tf_op | source)
XLA Modules:
  0.0 152.0 jit_solution(15061256603344128218)
XLA Ops:
  0.6 147.3 %attn_block.1 = (bf16[128,2048]{1,0:T(8,128)(2,1)}, bf16[128,2048]{1,0:T(8,128)(2,1)}, f32[3072,128]{1,0:T(8,128)}, f32[128,2048]{1,0:T(8,128)}, f32[2,1,2048]{2,1,0:T(1,128)}) custom-call(bf16[128,2048]{1,0:T(8,128)(2,1)} %bitcast.27, bf16[128,2048]{1,0:T(8,128)(2,1)} %bitcast.28, s32[1,128]{1,0:T(1,128)} %pos_hbm.1, f32[1,2048]{1,0:T(1,128)} %bitcast.29, ...), custom_call_target="tpu_custom_call" | custom-call | tf_op jit(solution)/shard_map/attn_block/pallas_call | solution.py:769
  147.9 3.9 %settle.1 = (bf16[128,2048]{1,0:T(8,128)(2,1)}, bf16[128,2048]{1,0:T(8,128)(2,1)}, f32[2048,128]{1,0:T(8,128)}, f32[512,128]{1,0:T(8,128)}, f32[512,128]{1,0:T(8...) custom-call(bf16[128,2048]{1,0:T(8,128)(2,1)} %get-tuple-element.21.out_i, ...), custom_call_target="tpu_custom_call" | custom-call | tf_op jit(solution)/shard_map/settle/pallas_call | solution.py:789

commit v20 on v18

--- a/solution.py
+++ b/solution.py
@@ -15,7 +15,7 @@
 F32 = jnp.float32
 NEAR = 1
 PARTS = 4
-FIRST = 1
+FIRST = 0
 HELD = 4
 
 
@@ -668,25 +668,25 @@
         item.wait()
 
 
-def settle_kernel(q_rows, kv_w, out_i, gx_i, gw_i, gwo_i, gg_i, out_o, gx_o, gq_o, gk_o, gv_o, gwo_o, gain_o, bias_o, b_act, b_q, b_kv, b_o, b_gg, sem_in, sem_out, sem_gg):
-    half_q = q_rows // 2
-    half_o = gwo_i.shape[0] // 2
-    moves = [(out_i, b_act.at[0], out_o), (gx_i, b_act.at[1], gx_o)]
-    for t in range(2):
-        moves.append((gw_i.at[pl.ds(half_q * t, half_q)], b_q.at[t], gq_o.at[pl.ds(half_q * t, half_q)]))
-        moves.append((gwo_i.at[pl.ds(half_o * t, half_o)], b_o.at[t], gwo_o.at[pl.ds(half_o * t, half_o)]))
-    moves.append((gw_i.at[pl.ds(q_rows, kv_w)], b_kv.at[0], gk_o))
-    moves.append((gw_i.at[pl.ds(q_rows + kv_w, kv_w)], b_kv.at[1], gv_o))
-    loads = [pltpu.make_async_copy(src, mid, sem_in.at[i]) for i, (src, mid, _) in enumerate(moves)]
-    stores = [pltpu.make_async_copy(mid, dst, sem_out.at[i]) for i, (_, mid, dst) in enumerate(moves)]
-    load_gg = pltpu.make_async_copy(gg_i, b_gg, sem_gg)
-    load_gg.start()
+def settle_kernel(q_rows, kv_w, out_i, gx_i, gw_i, gwo_i, gg_i, out_o, gx_o, gq_o, gk_o, gv_o, gwo_o, gain_o, bias_o, b_out, b_gx, b_w, b_o, b_gg, sem_in, sem_out):
+    pairs = [(gg_i, b_gg), (gw_i, b_w), (gwo_i, b_o), (out_i, b_out), (gx_i, b_gx)]
+    loads = [pltpu.make_async_copy(src, dst, sem_in.at[i]) for i, (src, dst) in enumerate(pairs)]
     for item in loads:
         item.start()
-    for load, store in zip(loads, stores):
-        load.wait()
-        store.start()
-    load_gg.wait()
+    k_row, v_row = q_rows, q_rows + kv_w
+    moves = [
+        (1, b_w.at[pl.ds(0, q_rows)], gq_o), (1, b_w.at[pl.ds(k_row, kv_w)], gk_o), (1, b_w.at[pl.ds(v_row, kv_w)], gv_o),
+        (2, b_o, gwo_o), (3, b_out, out_o), (4, b_gx, gx_o),
+    ]
+    stores = []
+    waited = set()
+    for i, (which, src, dst) in enumerate(moves):
+        if which not in waited:
+            loads[which].wait()
+            waited.add(which)
+        stores.append(pltpu.make_async_copy(src, dst, sem_out.at[i]))
+        stores[i].start()
+    loads[0].wait()
     gain_o[...] = b_gg[0, 0]
     bias_o[...] = b_gg[1, 0]
     for item in stores:
@@ -795,12 +795,12 @@
             in_specs=[hbm] * 5,
             out_specs=(hbm,) * 6 + (vmem,) * 2,
             scratch_shapes=[
-                pltpu.VMEM((2, tok, width), BF),
-                pltpu.VMEM((2, q_w // 2, tok), F32),
-                pltpu.VMEM((2, kv_w, tok), F32),
-                pltpu.VMEM((2, hw // 2, width), F32),
+                pltpu.VMEM((tok, width), BF),
+                pltpu.VMEM((tok, width), BF),
+                pltpu.VMEM((n_rows, tok), F32),
+                pltpu.VMEM((hw, width), F32),
                 pltpu.VMEM((2, 1, width), F32),
-                dma((8,)), dma((8,)), dma,
+                dma((5,)), dma((6,)),
             ],
             name='settle',
         )(out, gx, gw, gwo, gg)

time: 151 us -> 153 us (1.013)
  Pallas kernels: 150 us -> 152 us
where the time goes in v20:
time: 153 us
  Pallas kernels  152 us (99%)
    pallas_call x1, Pallas kernels, device_step(): pl.pallas_call(functools.partial(block_kernel, n_dev, hd, kv_w, NEAR, PAR...  148 us
    pallas_call x1, Pallas kernels, device_step(): pl.pallas_call(functools.partial(settle_kernel, q_w, kv_w), out_shape=(ja...  3.95 us

profile of v20, /device:TPU:21, one launch (start us, length us, event | category | flops | bytes accessed | tf_op | source)
XLA Modules:
  0.0 152.7 jit_solution(13643173966134837260)
XLA Ops:
  0.6 148.0 %attn_block.1 = (bf16[128,2048]{1,0:T(8,128)(2,1)}, bf16[128,2048]{1,0:T(8,128)(2,1)}, f32[3072,128]{1,0:T(8,128)}, f32[128,2048]{1,0:T(8,128)}, f32[2,1,2048]{2,1,0:T(1,128)}) custom-call(bf16[128,2048]{1,0:T(8,128)(2,1)} %bitcast.27, bf16[128,2048]{1,0:T(8,128)(2,1)} %bitcast.28, s32[1,128]{1,0:T(1,128)} %pos_hbm.1, f32[1,2048]{1,0:T(1,128)} %bitcast.29, ...), custom_call_target="tpu_custom_call" | custom-call | tf_op jit(solution)/shard_map/attn_block/pallas_call | solution.py:763
  148.6 4.0 %settle.1 = (bf16[128,2048]{1,0:T(8,128)(2,1)}, bf16[128,2048]{1,0:T(8,128)(2,1)}, f32[2048,128]{1,0:T(8,128)}, f32[512,128]{1,0:T(8,128)}, f32[512,128]{1,0:T(8...) custom-call(bf16[128,2048]{1,0:T(8,128)(2,1)} %get-tuple-element.21.out_i, ...), custom_call_target="tpu_custom_call" | custom-call | tf_op jit(solution)/shard_map/settle/pallas_call | solution.py:783

commit v21 on v18

--- a/solution.py
+++ b/solution.py
@@ -16,7 +16,7 @@
 NEAR = 1
 PARTS = 4
 FIRST = 1
-HELD = 4
+HELD = 8
 
 
 def dot(lhs, rhs):

time: 151 us -> 151 us (level)
  no operation moved by 1% of the time
where the time goes in v21:
time: 151 us
  Pallas kernels  150 us (99%)
    pallas_call x1, Pallas kernels, device_step(): pl.pallas_call(functools.partial(block_kernel, n_dev, hd, kv_w, NEAR, PAR...  146 us
    pallas_call x1, Pallas kernels, device_step(): pl.pallas_call(functools.partial(settle_kernel, q_w, kv_w), out_shape=(ja...  3.62 us

profile of v21, /device:TPU:21, one launch (start us, length us, event | category | flops | bytes accessed | tf_op | source)
XLA Modules:
  0.0 150.8 jit_solution(13430678760586248002)
XLA Ops:
  0.6 146.4 %attn_block.1 = (bf16[128,2048]{1,0:T(8,128)(2,1)}, bf16[128,2048]{1,0:T(8,128)(2,1)}, f32[3072,128]{1,0:T(8,128)}, f32[128,2048]{1,0:T(8,128)}, f32[2,1,2048]{2,1,0:T(1,128)}) custom-call(bf16[128,2048]{1,0:T(8,128)(2,1)} %bitcast.27, bf16[128,2048]{1,0:T(8,128)(2,1)} %bitcast.28, s32[1,128]{1,0:T(1,128)} %pos_hbm.1, f32[1,2048]{1,0:T(1,128)} %bitcast.29, ...), custom_call_target="tpu_custom_call" | custom-call | tf_op jit(solution)/shard_map/attn_block/pallas_call | solution.py:763
  147.0 3.6 %settle.1 = (bf16[128,2048]{1,0:T(8,128)(2,1)}, bf16[128,2048]{1,0:T(8,128)(2,1)}, f32[2048,128]{1,0:T(8,128)}, f32[512,128]{1,0:T(8,128)}, f32[512,128]{1,0:T(8...) custom-call(bf16[128,2048]{1,0:T(8,128)(2,1)} %get-tuple-element.21.out_i, ...), custom_call_target="tpu_custom_call" | custom-call | tf_op jit(solution)/shard_map/settle/pallas_call | solution.py:783
